TPU v7x, 8 devices: a whole 2x2x1 slice. The times are simulated.
8 devices in a mesh: dp: 1 (over z), ff: 2 (over y), hd: 4 (over x, core).
Axes of the slice: x: 2, y: 2, z: 1, core: 2. Of those that a mesh axis runs over, the one named last changes fastest.
Arguments:
- x_in: bfloat16 [128, 4096], P('dp', 'hd')
- w_up: bfloat16 [4096, 20480], P('hd', 'ff')
- b_up: float32 [20480], P('ff')
- w_down: bfloat16 [10240, 4096], P('ff', 'hd')
- b_down: float32 [4096], P('hd')
- ln_gain: float32 [4096], P('hd')
- ln_bias: float32 [4096], P('hd')
- dy_in: bfloat16 [128, 4096], P('dp', 'hd')
Outputs:
- output 1: bfloat16 [128, 4096], P('dp', 'hd')
- output 2: bfloat16 [128, 4096], P('dp', 'hd')
- output 3: float32 [4096, 20480], P(('dp', 'hd'), 'ff')
- output 4: float32 [10240, 4096], P(('dp', 'ff'), 'hd')
- output 5: float32 [20480], P(('dp', 'ff'))
- output 6: float32 [4096], P(('dp', 'hd'))
- output 7: float32 [4096], P(('dp', 'hd'))
- output 8: float32 [4096], P(('dp', 'hd'))
All inputs are finite; a program needn't handle non-finite values.
Results may differ from a plain program's by a relative error of at most 0.0181239.
Values are sent between devices in bfloat16 or wider.
A program may use at most 1 GiB of HBM per device.

v0:
```python
import math
import jax
import jax.numpy as jnp
from jax import lax
from jax.sharding import PartitionSpec as P

PAIR = 128
ALPHA = math.sqrt(140.0)
LN_EPS = 1e-5


def gelu_tanh(z_val):
    return jax.nn.gelu(z_val, approximate=True)


def solution(mesh):
    hd_size = mesh.shape['hd']
    data_spec = P('dp', 'hd')
    hid_spec = P('hd')
    in_specs = (data_spec, P('hd', 'ff'), P('ff'), P('ff', 'hd'), hid_spec, hid_spec, hid_spec, data_spec)
    out_specs = (data_spec, data_spec, P(('dp', 'hd'), 'ff'), P(('dp', 'ff'), 'hd'), P(('dp', 'ff')), P(('dp', 'hd')), P(('dp', 'hd')), P(('dp', 'hd')))

    def device_step(x_loc, w_up, b_up, w_down, b_down, ln_gain, ln_bias, dy_loc):
        tokens, hid_loc = x_loc.shape
        hidden = hid_loc * hd_size
        n_blocks = w_up.shape[1] // (2 * PAIR)
        ffn_loc = n_blocks * PAIR
        w_up4 = w_up.reshape(hid_loc, n_blocks, 2, PAIR)
        u_part = jnp.einsum('th,hbkc->tbkc', x_loc, w_up4, preferred_element_type=jnp.float32)
        u_summed = lax.psum(u_part.astype(jnp.bfloat16), 'hd')
        u_act = (u_summed.astype(jnp.float32) + b_up.reshape(n_blocks, 2, PAIR)).astype(jnp.bfloat16)
        val_half = u_act[:, :, 0, :].astype(jnp.float32)
        gate_half = u_act[:, :, 1, :].astype(jnp.float32)
        gelu_out, gelu_vjp = jax.vjp(gelu_tanh, gate_half)
        m_act = (val_half * gelu_out).astype(jnp.bfloat16).reshape(tokens, ffn_loc)
        f_part = jnp.dot(m_act, w_down, preferred_element_type=jnp.float32)
        f_out = lax.psum(f_part.astype(jnp.bfloat16), 'ff').astype(jnp.float32)
        residual = ALPHA * x_loc.astype(jnp.float32) + f_out + b_down
        moments = lax.psum(jnp.stack([jnp.sum(residual, axis=1), jnp.sum(residual * residual, axis=1)]), 'hd')
        row_mean = (moments[0] / hidden)[:, None]
        inv_std = lax.rsqrt(moments[1][:, None] / hidden - row_mean * row_mean + LN_EPS)
        normed = (residual - row_mean) * inv_std
        y_loc = (ln_gain * normed + ln_bias).astype(jnp.bfloat16)
        dy_f = dy_loc.astype(jnp.float32)
        g_dy = dy_f * ln_gain
        grad_moments = lax.psum(jnp.stack([jnp.sum(g_dy, axis=1), jnp.sum(g_dy * normed, axis=1)]), 'hd')
        d_resid = inv_std * (g_dy - (grad_moments[0] / hidden)[:, None] - normed * (grad_moments[1] / hidden)[:, None])
        dr_b = d_resid.astype(jnp.bfloat16)
        dm_part = jnp.einsum('th,fh->tf', dr_b, w_down, preferred_element_type=jnp.float32)
        d_mact = lax.psum(dm_part.astype(jnp.bfloat16), 'hd').astype(jnp.float32).reshape(tokens, n_blocks, PAIR)
        dw_down = jnp.einsum('tf,th->fh', m_act, dr_b, preferred_element_type=jnp.float32)
        d_val = d_mact * gelu_out
        d_gate = gelu_vjp(d_mact * val_half)[0]
        du_f = jnp.stack([d_val, d_gate], axis=2)
        du_b = du_f.astype(jnp.bfloat16)
        dw_up = jnp.einsum('th,tbkc->hbkc', x_loc, du_b, preferred_element_type=jnp.float32).reshape(hid_loc, 2 * ffn_loc)
        dx_part = jnp.einsum('tbkc,hbkc->th', du_b, w_up4, preferred_element_type=jnp.float32)
        dx_sum = lax.psum(dx_part.astype(jnp.bfloat16), 'ff').astype(jnp.float32)
        dx_loc = (ALPHA * d_resid + dx_sum).astype(jnp.bfloat16)
        db_up = jnp.sum(du_f, axis=0).reshape(2 * ffn_loc)
        return (y_loc, dx_loc, dw_up, dw_down, db_up, jnp.sum(d_resid, axis=0), jnp.sum(dy_f * normed, axis=0), jnp.sum(dy_f, axis=0))

    return jax.shard_map(device_step, mesh=mesh, in_specs=in_specs, out_specs=out_specs, check_vma=False)
```

profile of v0, /device:TPU:0, one launch (start us, length us, event | category | flops | bytes accessed | tf_op | source)
XLA Modules:
  0.0 296.1 jit_solution(15416595854776409155)
XLA Ops:
  7.2 0.0 copy-start.2
  7.2 0.0 all-reduce.5.cloned.1.call-start
  7.2 30.6 %reshape.85 = bf16[1024,40,2,128]{3,2,1,0:T(2,128)(2,1)} reshape(bf16[1024,10240]{1,0:T(8,128)(2,1)} %param.9) | data formatting | bytes 41943040 | tf_op jit(solution)/shard_map/reshape | solution.py:28
  37.8 0.0 copy-done.2
  37.8 12.3 %fusion.22 = bf16[128,40,2,128]{3,0,2,1:T(8,128)(2,1)} fusion(bf16[1024,40,2,128]{3,2,1,0:T(2,128)(2,1)} %reshape.85, bf16[128,1024]{1,0:T(8,128)(2,1)S(1)} %copy-done.2), kind=kOutput, calls=%fused_computation.33 | convolution fusion | flops 2685665280 | bytes 23855104 | tf_op jit(solution)/shard_map/th,hbkc->tbkc/dot_general | solution.py:29
  50.1 0.0 all-reduce.5.cloned.1.call-update
  50.1 0.0 all-reduce.7.cloned.1.call-start
  50.2 57.1 %all-reduce.5.cloned.1.call-done = bf16[128,40,2,128]{3,0,2,1:T(8,128)(2,1)} async-done(((bf16[128,40,2,128]{3,0,2,1:T(8,128)(2,1)}), bf16[128,40,2,128]{3,0,2,1:T(8,128)(2,1)}) %all-reduce.5.cloned.1.call-update) | async-done | bytes 2621456 | tf_op jit(solution)/shard_map/psum | solution.py:30
  107.3 0.0 copy-done.4
  107.3 2.6 add_convert_fusion
  109.8 0.0 copy-start.1
  109.9 2.3 slice_convert_fusion
  112.2 0.0 copy-done.1
  112.2 3.3 %copy.22 = f32[128,40,1,128]{0,3,1,2:T(8,128)} copy(f32[128,40,1,128]{3,0,2,1:T(8,128)} %get-tuple-element.35) | data formatting | bytes 5242880 | tf_op jit(solution)/shard_map/convert_element_type | solution.py:33
  115.5 2.1 copy.21
  117.5 3.5 %fusion.21 = bf16[128,5120]{0,1:T(8,128)(2,1)S(1)} fusion(f32[128,40,1,128]{0,3,1,2:T(8,128)} %copy.22, f32[128,40,1,128]{0,3,1,2:T(8,128)} %copy.21), kind=kLoop, calls=%fused_computation.32 | loop fusion | flops 6553600 | bytes 6553600 | tf_op jit(solution)/shard_map/convert_element_type | solution.py:35
  121.0 0.0 copy-start.5
  121.0 0.0 copy-start.3
  121.0 0.0 copy-start.6
  121.0 0.0 copy-start.7
  121.1 6.3 %convolution_convert_fusion.1 = bf16[128,1024]{1,0:T(8,128)(2,1)} fusion(bf16[128,5120]{0,1:T(8,128)(2,1)S(1)} %fusion.21, bf16[5120,1024]{1,0:T(8,128)(2,1)} %param.11), kind=kOutput, calls=%fused_computation.37 | convolution fusion | flops 1342308352 | bytes 12058624 | tf_op jit(solution)/shard_map/dot_general | solution.py:36
  127.3 0.0 all-reduce.7.cloned.1.call-update
  127.3 0.0 all-reduce.9.cloned.1.call-start
  127.4 17.7 %all-reduce.7.cloned.1.call-done = bf16[128,1024]{1,0:T(8,128)(2,1)} async-done(((bf16[128,1024]{1,0:T(8,128)(2,1)}), bf16[128,1024]{1,0:T(8,128)(2,1)}) %all-reduce.7.cloned.1.call-update) | async-done | bytes 262160 | tf_op jit(solution)/shard_map/psum | solution.py:37
  145.1 0.0 copy-done.5
  145.1 1.2 fusion.41
  146.3 6.2 %psum.44 = f32[2,128]{1,0:T(2,128)S(1)} all-reduce(f32[2,128]{1,0:T(2,128)S(1)} %pad_maximum_fusion.1), channel_id=1, replica_groups=mesh['dp'=1,'ff'=2,'hd'=4] {'hd'}, use_global_device_ids=true, to_apply=%region_4.0 | all-reduce | flops 256 | bytes 2048 | tf_op jit(solution)/shard_map/psum | solution.py:39
  152.5 0.0 copy-done.3
  152.5 0.0 copy-done.6
  152.5 1.9 fusion.37
  154.4 6.2 %psum.45 = f32[2,128]{1,0:T(2,128)S(1)} all-reduce(f32[2,128]{1,0:T(2,128)S(1)} %pad_maximum_fusion.2), channel_id=1, replica_groups=mesh['dp'=1,'ff'=2,'hd'=4] {'hd'}, use_global_device_ids=true, to_apply=%region_7.0 | all-reduce | flops 256 | bytes 2048 | tf_op jit(solution)/shard_map/psum | solution.py:46
  160.7 0.0 copy-done.7
  160.7 2.5 fusion.51
  163.2 7.5 %convolution_convert_fusion = bf16[128,5120]{1,0:T(8,128)(2,1)S(1)} fusion(bf16[5120,1024]{1,0:T(8,128)(2,1)} %param.11, f32[128,1024]{1,0:T(8,128)S(1)} %get-tuple-element.31), kind=kOutput, calls=%fused_computation.4 | convolution fusion | flops 1342963712 | bytes 12320768 | tf_op jit(solution)/shard_map/th,fh->tf/dot_general | solution.py:49
  170.7 1.4 copy.23
  172.2 2.4 copy.24
  174.6 0.0 all-reduce.9.cloned.1.call-update
  174.6 0.0 all-reduce.11.cloned.1.call-start
  174.7 9.1 %fusion.44 = f32[5120,1024]{1,0:T(8,128)} fusion(bf16[128,5120]{0,1:T(8,128)(2,1)S(1)} %fusion.21, f32[128,1024]{1,0:T(8,128)S(1)} %get-tuple-element.31), kind=kOutput, calls=%fused_computation.58 | convolution fusion | flops 1342308352 | bytes 22806528 | tf_op jit(solution)/shard_map/tf,th->fh/dot_general | solution.py:51
  183.7 24.1 %all-reduce.9.cloned.1.call-done = bf16[128,40,1,128]{3,0,2,1:T(8,128)(2,1)} async-done(((bf16[128,40,1,128]{3,0,2,1:T(8,128)(2,1)}), bf16[128,40,1,128]{3,0,2,1:T(8,128)(2,1)}) %all-reduce.9.cloned.1.call-update) | async-done | bytes 1310736 | tf_op jit(solution)/shard_map/psum | solution.py:50
  207.8 3.7 %convert_multiply_fusion.3 = (f32[128,40,1,128]{3,0,2,1:T(8,128)S(1)}, f32[128,40,1,128]{3,0,2,1:T(8,128)S(1)}) fusion(bf16[128,40,1,128]{3,0,2,1:T(8,128)(2,1)} %all-reduce.9.cloned.1.call-done, bf16[128,40,2,128]{3,0,2,1:T(8,128)(2,1)} %copy-done.1), kind=kLoop, calls=%fused_computation.16 | loop fusion | flops 16384000 | bytes 9175040 | tf_op jit(solution)/shard_map/mul | solution.py:52
  211.6 1.5 copy-done
  213.1 12.0 %fusion.28 = bf16[128,1024]{1,0:T(8,128)(2,1)} fusion(bf16[1024,40,2,128]{3,2,1,0:T(2,128)(2,1)} %reshape.85, f32[128,40,1,128]{3,0,2,1:T(8,128)S(1)} %get-tuple-element.33, f32[128,40,1,128]{3,0,2,1:T(8,128)S(1)} %get-tuple-element.32), kind=kOutput, calls=%fused_computation.36 | convolution fusion | flops 2685796352 | bytes 26476544 | tf_op jit(solution)/shard_map/tbkc,hbkc->th/dot_general | solution.py:57
  225.1 0.0 all-reduce.11.cloned.1.call-update
  225.1 18.1 %fusion.38 = f32[40,2,128,1024]{3,2,1,0:T(8,128)} fusion(f32[128,40,1,128]{3,0,2,1:T(8,128)} %copy-done, f32[128,40,1,128]{3,0,2,1:T(8,128)S(1)} %get-tuple-element.32, bf16[128,1024]{1,0:T(8,128)(2,1)S(1)} %copy-done.2), kind=kOutput, calls=%fused_computation.54 | convolution fusion | flops 2685665280 | bytes 47448064 | tf_op jit(solution)/shard_map/th,tbkc->hbkc/dot_general | solution.py:56
  243.2 41.6 %copy.27 = f32[1024,10240]{1,0:T(8,128)} copy(f32[1024,10240]{0,1:T(8,128)} %bitcast.45) | data formatting | bytes 83886080
  284.9 3.0 %fusion.4 = f32[40,2,128]{2,1,0:T(2,128)} fusion(f32[128,40,1,128]{3,0,2,1:T(8,128)} %copy-done, f32[128,40,1,128]{3,0,2,1:T(8,128)S(1)} %get-tuple-element.32), kind=kLoop, calls=%fused_computation.7 | loop fusion | flops 2611200 | bytes 5283840 | tf_op jit(solution)/shard_map/reduce_sum | solution.py:60
  287.9 1.7 add_convert_fusion.1
  (8 shorter events, 0.0 us)
Async XLA Ops:
  7.2 30.6 %copy-start.2 = (bf16[128,1024]{1,0:T(8,128)(2,1)S(1)}, bf16[128,1024]{1,0:T(8,128)(2,1)}, u32[]{:S(2)}) copy-start(bf16[128,1024]{1,0:T(8,128)(2,1)} %param.8) | copy-start | bytes 786436
  7.2 100.1 %all-reduce.5.cloned.1.call-start = ((), (), s32[]{:S(2)}) async-start(), calls=%async_computation | async-start | bytes 5242880 | tf_op jit(solution)/shard_map/psum | solution.py:30
  50.1 57.2 %copy-start.4 = (f32[10240]{0:T(1024)S(1)}, f32[10240]{0:T(1024)}, u32[]{:S(2)}) copy-start(f32[10240]{0:T(1024)} %param.10) | copy-start | bytes 122884
  50.1 95.0 %all-reduce.7.cloned.1.call-start = ((), (), s32[]{:S(2)}) async-start(), calls=%async_computation.1 | async-start | bytes 524288 | tf_op jit(solution)/shard_map/psum | solution.py:37
  109.8 2.4 copy-start.1
  121.0 24.1 %copy-start.5 = (f32[1024]{0:T(1024)S(1)}, f32[1024]{0:T(1024)}, u32[]{:S(2)}) copy-start(f32[1024]{0:T(1024)} %param.12) | copy-start | bytes 12292
  121.0 31.5 %copy-start.3 = (bf16[128,1024]{1,0:T(8,128)(2,1)S(1)}, bf16[128,1024]{1,0:T(8,128)(2,1)}, u32[]{:S(2)}) copy-start(bf16[128,1024]{1,0:T(8,128)(2,1)} %param.15) | copy-start | bytes 786436
  121.0 31.5 %copy-start.6 = (f32[1024]{0:T(1024)S(1)}, f32[1024]{0:T(1024)}, u32[]{:S(2)}) copy-start(f32[1024]{0:T(1024)} %param.13) | copy-start | bytes 12292
  121.0 39.6 %copy-start.7 = (f32[1024]{0:T(1024)S(1)}, f32[1024]{0:T(1024)}, u32[]{:S(2)}) copy-start(f32[1024]{0:T(1024)} %param.14) | copy-start | bytes 12292
  127.3 80.5 %all-reduce.9.cloned.1.call-start = ((), (), s32[]{:S(2)}) async-start(), calls=%async_computation.2 | async-start | bytes 2621440 | tf_op jit(solution)/shard_map/psum | solution.py:50
  174.6 113.3 %all-reduce.11.cloned.1.call-start = ((), (), s32[]{:S(2)}) async-start(), calls=%async_computation.3 | async-start | bytes 524288 | tf_op jit(solution)/shard_map/psum | solution.py:58
  211.6 1.5 copy-start
Sparse Core Ops, SparseCore 0:
  50.2 56.9 all-reduce.4
  127.5 17.5 all-reduce.6
  174.7 33.0 all-reduce.8
  225.2 17.4 all-reduce.10
where the time goes:
time: 298 us; the launch traced here: 296 us
  waiting for transfers between devices  99 us (33%)
  local copies, waits for them, and re-layouts  82.9 us (28%)
  matrix products  65.2 us (22%)
  other arithmetic  22.5 us (8%)
  between operations  13.9 us (5%)
  blocking collectives  12.4 us (4%)
    psum x1, waiting for transfers between devices, device_step(): u_summed = lax.psum(u_part.astype(jnp.bfloat16), 'hd')  57.1 us
    unnamed x17, local copies, waits for them, and re-layouts  43.2 us
    reshape x1, local copies, waits for them, and re-layouts, device_step(): w_up4 = w_up.reshape(hid_loc, n_blocks, 2, PAIR)  30.6 us
    psum x1, waiting for transfers between devices, device_step(): lax.psum(dm_part.astype(jnp.bfloat16), 'hd').astype(jnp.float32)  24.1 us
    dot_general x1, matrix products, device_step(): jnp.einsum('th,tbkc->hbkc', x_loc, du_b, preferred_element_type=jnp.float32)  18.1 us
    psum x1, waiting for transfers between devices, device_step(): f_out = lax.psum(f_part.astype(jnp.bfloat16), 'ff').astype(jnp.float32)  17.7 us
    dot_general x1, matrix products, device_step(): jnp.einsum('th,hbkc->tbkc', x_loc, w_up4, preferred_element_type=jnp.floa...  12.3 us
    dot_general x1, matrix products, device_step(): jnp.einsum('tbkc,hbkc->th', du_b, w_up4, preferred_element_type=jnp.float32)  12 us
  transfers between devices with their start and end apart: 4, of which 3 were waited for; matrix products, arithmetic and copies ran while one was open for 24% of the time, Pallas kernels for 0%

commit v1 on v0

v1 whole, which is shorter than its diff:
```python
import functools
import math
import jax
import jax.numpy as jnp
from jax import lax
from jax.experimental import pallas as pl
from jax.experimental.pallas import tpu as pltpu
from jax.sharding import PartitionSpec as P

PAIR = 128
ALPHA = math.sqrt(140.0)
LN_EPS = 1e-5
C0 = math.sqrt(2.0 / math.pi)
C1 = 0.044715
MESH = pl.DeviceIdType.MESH
F32 = jnp.float32
BF = jnp.bfloat16
T = 128
H = 1024
NC = 5
Q = 256
S = 2
VLIM = 62 * 1024 * 1024

VMEM = pl.BlockSpec(memory_space=pltpu.VMEM)
ANY = pl.BlockSpec(memory_space=pl.ANY)


def sds(shape, dtype):
    return jax.ShapeDtypeStruct(shape, dtype)


def dot(a, b):
    return jnp.dot(a, b, preferred_element_type=F32)


def dot_t(a, b):
    return lax.dot_general(a, b, (((1,), (1,)), ((), ())), preferred_element_type=F32)


def split_u(u):
    v = jnp.concatenate([u[:, 0:128], u[:, 256:384]], axis=1)
    g = jnp.concatenate([u[:, 128:256], u[:, 384:512]], axis=1)
    return v, g


def gelu(g):
    t = jnp.tanh(C0 * (g + C1 * (g * g * g)))
    return g * (0.5 * (1.0 + t))


def gelu_both(g):
    g2 = g * g
    t = jnp.tanh(C0 * (g + C1 * (g2 * g)))
    cdf = 0.5 * (1.0 + t)
    slope = cdf + (0.5 * g) * (1.0 - t * t) * (C0 * (1.0 + (3.0 * C1) * g2))
    return g * cdf, slope


def grad_u(u, dm):
    v, g = split_u(u.astype(F32))
    val, slope = gelu_both(g)
    dv = dm * val
    dg = dm * v * slope
    return jnp.concatenate([dv[:, 0:128], dg[:, 0:128], dv[:, 128:256], dg[:, 128:256]], axis=1)


def places():
    h = lax.axis_index("hd")
    y = lax.axis_index("ff")
    c = lax.rem(h, 2)
    sib = h + 1 - 2 * c
    xn = lax.rem(h + 2, 4)
    xs = lax.rem(sib + 2, 4)
    return h, y, c, sib, xn, xs


def remote(src, dst, sems, k, dev):
    return pltpu.make_async_remote_copy(src_ref=src, dst_ref=dst, send_sem=sems[0].at[k], recv_sem=sems[1].at[k],
                                        device_id=dev, device_id_type=MESH)


def w1_cols(w1_ref, j, q):
    return w1_ref.at[:, pl.ds(pl.multiple_of(j * 4 * 512 + q * 512, 512), 512)]


N_SEM = {"ud": 2 * NC, "ux": NC, "mx": NC, "md": NC, "mf": NC, "gx": NC, "gd": NC, "gf": NC, "fy": 2, "st": 3,
         "dd": 2 * NC, "dx": NC, "df": 2 * NC}
SEM_NAMES = list(N_SEM)


def forward_kernel(x_ref, w1_ref, b1_ref, w2_ref, b2_ref, gam_ref, dy_ref,
                   m_ref, u_ref, d_ref, dr_ref, nrm_ref, dmf_ref, dms_ref,
                   w1b, w2b, ub, rb, xsb, xrb, facc, fs, fr, stb, dmb, dmr, dsum, dxr,
                   ls1, ls2, *sem_list):
    sems = {n: (sem_list[2 * i], sem_list[2 * i + 1]) for i, n in enumerate(SEM_NAMES)}
    h, y, c, sib, xn, xs = places()
    dev_sib, dev_x, dev_xs, dev_y = (0, y, sib), (0, y, xn), (0, y, xs), (0, 1 - y, h)
    order = [xs, xn, sib, h]
    for j in range(NC):
        for k in range(4):
            pltpu.make_async_copy(w1_cols(w1_ref, j, order[k]), w1b.at[j, k], ls1.at[j, k]).start()
    for j in range(NC):
        pltpu.make_async_copy(w2_ref.at[j * 1024:(j + 1) * 1024, :], w2b.at[j], ls2.at[j]).start()
    bar = pltpu.get_barrier_semaphore()
    for dev in (dev_sib, dev_x, dev_xs, dev_y):
        pl.semaphore_signal(bar, inc=1, device_id=dev, device_id_type=MESH)
    pl.semaphore_wait(bar, 4)

    live = []

    def send(src, dst, name, k, dev):
        cp = remote(src, dst, sems[name], k, dev)
        cp.start()
        live.append(cp)
        return cp

    def u_part(j):
        for k in range(4):
            pltpu.make_async_copy(w1_cols(w1_ref, j, order[k]), w1b.at[j, k], ls1.at[j, k]).wait()
            ub[j, k] = dot(x_ref[...], w1b[j, k]).astype(BF)
            if k == 0:
                c_ud[j, 1] = send(ub.at[j, 0], rb.at[j, 1], "ud", 2 * j + 1, dev_sib)
            if k == 2:
                c_ud[j, 0] = send(ub.at[j, 2], rb.at[j, 0], "ud", 2 * j, dev_sib)

    def s1(j):
        c_ud[j, 1].wait_recv()
        xsb[j] = (ub[j, 1].astype(F32) + rb[j, 1].astype(F32)).astype(BF)
        c_ux[j] = send(xsb.at[j], xrb.at[j], "ux", j, dev_x)

    def s2(j):
        c_ud[j, 0].wait_recv()
        c_ux[j].wait_recv()
        u = ub[j, 3].astype(F32) + rb[j, 0].astype(F32) + xrb[j].astype(F32) + b1_ref[j * 4 + h]
        u = u.astype(BF)
        u_ref[j, h] = u
        v, g = split_u(u.astype(F32))
        m_ref[j, h] = (v * gelu(g)).astype(BF)
        c_mx[j] = send(m_ref.at[j, h], m_ref.at[j, h], "mx", j, dev_x)
        c_md[j] = send(m_ref.at[j, h], m_ref.at[j, h], "md", j, dev_sib)

    def s3(j):
        c_mx[j].wait_recv()
        c_mf[j] = send(m_ref.at[j, xn], m_ref.at[j, xn], "mf", j, dev_sib)

    def s4(j):
        c_md[j].wait_recv()
        c_mf[j].wait_recv()
        pltpu.make_async_copy(w2_ref.at[j * 1024:(j + 1) * 1024, :], w2b.at[j], ls2.at[j]).wait()
        m = jnp.concatenate([m_ref[j, q] for q in range(4)], axis=1)
        for n in range(2):
            cols = slice(n * 512, (n + 1) * 512)
            part = dot(m, w2b[j, :, cols])
            if j > 0:
                part = facc[:, cols] + part
            if j < NC - 1:
                facc[:, cols] = part
            else:
                fs[n] = part.astype(BF)
                c_fy.append(send(fs.at[n], fr.at[n], "fy", n, dev_y))

    def gather_u(j):
        c_gx[j] = send(u_ref.at[j, h], u_ref.at[j, h], "gx", j, dev_x)
        c_gd[j] = send(u_ref.at[j, h], u_ref.at[j, h], "gd", j, dev_sib)

    def forward_u(j):
        c_gx[j].wait_recv()
        c_gf[j] = send(u_ref.at[j, xn], u_ref.at[j, xn], "gf", j, dev_sib)

    c_ud, c_ux, c_mx, c_md, c_mf, c_fy, c_gx, c_gd, c_gf = {}, {}, {}, {}, {}, [], {}, {}, {}
    u_part(0)
    u_part(1)
    s1(0)
    u_part(2)
    s1(1)
    u_part(3)
    s1(2)
    s2(0)
    u_part(4)
    s1(3)
    s1(4)
    s2(1)
    s2(2)
    s2(3)
    s3(0)
    s4(0)
    s2(4)
    for j in range(NC):
        gather_u(j)
    for j in range(1, NC):
        s3(j)
        if j > 1:
            s4(j - 1)
    s4(NC - 1)

    for n in range(2):
        cols = slice(n * 512, (n + 1) * 512)
        c_fy[n].wait_recv()
        f = fs[n].astype(F32) + fr[n].astype(F32)
        nrm_ref[:, cols] = ALPHA * x_ref[:, cols].astype(F32) + f + b2_ref[:, cols]
    r = nrm_ref[...]
    gdy = dy_ref[...].astype(F32) * gam_ref[...]
    m_loc = jnp.sum(r, axis=1, keepdims=True) * (1.0 / H)
    cen = r - m_loc
    m2 = jnp.sum(cen * cen, axis=1, keepdims=True)
    sg = jnp.sum(gdy, axis=1, keepdims=True)
    cg = jnp.sum(gdy * cen, axis=1, keepdims=True)
    lane = lax.broadcasted_iota(jnp.int32, (T, 128), 1)
    pack = jnp.where(lane == 0, m_loc, jnp.where(lane == 1, m2, jnp.where(lane == 2, sg, cg)))
    stb[h] = pack.T[0:8]
    c_st = [send(stb.at[h], stb.at[h], "st", i, dev) for i, dev in enumerate((dev_sib, dev_x, dev_xs))]
    for cp in c_st:
        cp.wait_recv()
    st = [stb[i] for i in range(4)]
    mu = ((st[0][0:1] + st[1][0:1]) + (st[2][0:1] + st[3][0:1])) * 0.25
    m2t = jnp.zeros_like(mu)
    sgt = jnp.zeros_like(mu)
    cgt = jnp.zeros_like(mu)
    for i in range(4):
        delta = st[i][0:1] - mu
        m2t += st[i][1:2] + (H * delta) * delta
        sgt += st[i][2:3]
        cgt += st[i][3:4] + delta * st[i][2:3]
    rho = lax.rsqrt(m2t * (1.0 / (4 * H)) + LN_EPS)
    rows = jnp.concatenate([mu, rho, sgt * (1.0 / (4 * H)), cgt * rho * (1.0 / (4 * H)), jnp.zeros((124, T), F32)], axis=0)
    colst = rows.T
    mu_c, rho_c, mg_c, mgr_c = (colst[:, i:i + 1] for i in range(4))
    nrm = (r - mu_c) * rho_c
    dr = rho_c * (gdy - mg_c - nrm * mgr_c)
    nrm_ref[...] = nrm
    dr_ref[...] = dr
    d_ref[...] = dr.astype(BF)
    d_t = dr.T.astype(BF)

    c_dd, c_dx, c_df = {}, {}, {}
    mine, theirs = (c, c + 2), (1 - c, 3 - c)

    def dm_part(j):
        for i, q in enumerate(theirs + mine):
            rows_q = pl.ds(pl.multiple_of(q * Q, Q), Q)
            dmb[j, i] = dot(w2b[j, rows_q, :], d_t).T.astype(BF)
            if i < 2:
                c_dd[j, i] = send(dmb.at[j, i], dmr.at[j, i], "dd", 2 * j + i, dev_sib)

    def dm_sum(j):
        for i in range(2):
            c_dd[j, i].wait_recv()
            val = (dmb[j, 2 + i].astype(F32) + dmr[j, i].astype(F32)).astype(BF)
            if j < S:
                dsum[j, i] = val
            else:
                dms_ref[j - S, i] = val
        if j < S:
            c_dx[j] = send(dsum.at[j], dxr.at[j], "dx", j, dev_x)

    def dm_full(j):
        c_dx[j].wait_recv()
        for i in range(2):
            q = mine[i]
            dmf_ref[j, q] = (dsum[j, i].astype(F32) + dxr[j, i].astype(F32)).astype(BF)
            c_df[j, i] = send(dmf_ref.at[j, q], dmf_ref.at[j, q], "df", 2 * j + i, dev_sib)

    dm_part(0)
    dm_part(1)
    dm_sum(0)
    for j in range(2, NC):
        dm_part(j)
        dm_sum(j - 1)
        forward_u(j - 2)
    dm_sum(NC - 1)
    forward_u(NC - 2)
    forward_u(NC - 1)
    for j in range(S):
        dm_full(j)
    for cp in list(c_gd.values()) + list(c_gf.values()) + list(c_df.values()):
        cp.wait_recv()
    for cp in live:
        cp.wait_send()


def forward_call(x, w1, b1, w2, b2, gam, dy):
    scratch = [pltpu.VMEM((NC, 4, H, 512), BF), pltpu.VMEM((NC, 1024, H), BF),
               pltpu.VMEM((NC, 4, T, 512), BF), pltpu.VMEM((NC, 2, T, 512), BF),
               pltpu.VMEM((NC, T, 512), BF), pltpu.VMEM((NC, T, 512), BF),
               pltpu.VMEM((T, H), F32), pltpu.VMEM((2, T, 512), BF), pltpu.VMEM((2, T, 512), BF),
               pltpu.VMEM((4, 8, T), F32),
               pltpu.VMEM((NC, 4, T, Q), BF), pltpu.VMEM((NC, 2, T, Q), BF),
               pltpu.VMEM((S, 2, T, Q), BF), pltpu.VMEM((S, 2, T, Q), BF),
               pltpu.SemaphoreType.DMA((NC, 4)), pltpu.SemaphoreType.DMA((NC,))]
    for n in SEM_NAMES:
        scratch += [pltpu.SemaphoreType.DMA((N_SEM[n],)), pltpu.SemaphoreType.DMA((N_SEM[n],))]
    outs = [sds((NC, 4, T, Q), BF), sds((NC, 4, T, 512), BF), sds((T, H), BF), sds((T, H), F32), sds((T, H), F32),
            sds((S, 4, T, Q), BF), sds((NC - S, 2, T, Q), BF)]
    return pl.pallas_call(
        forward_kernel, out_shape=outs, name="fwd",
        in_specs=[VMEM, ANY, VMEM, ANY, VMEM, VMEM, VMEM], out_specs=[VMEM] * len(outs), scratch_shapes=scratch,
        compiler_params=pltpu.CompilerParams(collective_id=0, has_side_effects=True, vmem_limit_bytes=VLIM),
        cost_estimate=pl.CostEstimate(flops=5 * 10 ** 9, bytes_accessed=32 << 20, transcendentals=0),
    )(x, w1, b1, w2, b2, gam, dy)


NB2 = 6
NB1 = 4


def first_grads_kernel(m_ref, u_ref, d_ref, dr_ref, nrm_ref, dmf_ref, x_ref, gam_ref, beta_ref, dy_ref, w1_ref,
                       dw1_ref, dw2_ref, y_ref, db2_ref, dgam_ref, dbeta_ref, db1_ref, dxt_ref,
                       w1b, ob2, ob1, xt, ls1, so2, so1):
    def w1_load(j, q):
        return pltpu.make_async_copy(w1_ref.at[:, (j * 4 + q) * 512:(j * 4 + q + 1) * 512], w1b.at[j, q], ls1.at[j, q])

    for j in range(S):
        for q in range(4):
            w1_load(j, q).start()

    def put2(t):
        return pltpu.make_async_copy(ob2.at[t % NB2], dw2_ref.at[t * Q:(t + 1) * Q, :], so2.at[t % NB2])

    for t in range(NC * 4):
        if t >= NB2:
            put2(t - NB2).wait()
        ob2[t % NB2] = dot(m_ref[t // 4, t % 4].T, d_ref[...])
        put2(t).start()

    dy = dy_ref[...].astype(F32)
    y_ref[...] = (gam_ref[...] * nrm_ref[...] + beta_ref[...]).astype(BF)
    db2_ref[...] = jnp.sum(dr_ref[...], axis=0, keepdims=True)
    dgam_ref[...] = jnp.sum(dy * nrm_ref[...], axis=0, keepdims=True)
    dbeta_ref[...] = jnp.sum(dy, axis=0, keepdims=True)
    xt[...] = x_ref[...].T

    def put1(t):
        return pltpu.make_async_copy(ob1.at[t % NB1], dw1_ref.at[:, t * 512:(t + 1) * 512], so1.at[t % NB1])

    for t in range(S * 4):
        j, q = t // 4, t % 4
        du_f = grad_u(u_ref[j, q], dmf_ref[j, q].astype(F32))
        db1_ref[j, q] = jnp.sum(du_f, axis=0, keepdims=True)
        du = du_f.astype(BF)
        if t >= NB1:
            put1(t - NB1).wait()
        ob1[t % NB1] = dot(xt[...], du)
        put1(t).start()
        w1_load(j, q).wait()
        part = dot(w1b[j, q], du_f.T.astype(BF))
        dxt_ref[...] = part if t == 0 else dxt_ref[...] + part
    for t in range(NC * 4 - NB2, NC * 4):
        put2(t).wait()
    for t in range(max(0, S * 4 - NB1), S * 4):
        put1(t).wait()


def first_grads_call(m, u, d, dr, nrm, dmf, x, gam, beta, dy, w1):
    outs = [sds((H, NC * 2048), F32), sds((NC * 1024, H), F32), sds((T, H), BF), sds((1, H), F32), sds((1, H), F32),
            sds((1, H), F32), sds((S, 4, 1, 512), F32), sds((H, T), F32)]
    return pl.pallas_call(
        first_grads_kernel, out_shape=outs, name="ga",
        in_specs=[VMEM] * 10 + [ANY], out_specs=[ANY, ANY] + [VMEM] * 6,
        scratch_shapes=[pltpu.VMEM((S, 4, H, 512), BF), pltpu.VMEM((NB2, Q, H), F32), pltpu.VMEM((NB1, H, 512), F32),
                        pltpu.VMEM((H, T), BF), pltpu.SemaphoreType.DMA((S, 4)), pltpu.SemaphoreType.DMA((NB2,)),
                        pltpu.SemaphoreType.DMA((NB1,))],
        compiler_params=pltpu.CompilerParams(vmem_limit_bytes=48 * 1024 * 1024),
        cost_estimate=pl.CostEstimate(flops=3 * 10 ** 9, bytes_accessed=44 << 20, transcendentals=0),
    )(m, u, d, dr, nrm, dmf, x, gam, beta, dy, w1)


B = NC - S


def second_kernel(dms_ref, dmx_ref, u_ref, dxt_ref, w1_ref, du_ref, db1_ref, dxp_ref,
                  w1b, dmf, acc, ls1, ss, rs):
    h, y, c, sib, xn, xs = places()
    mine, theirs = (c, c + 2), (1 - c, 3 - c)
    dev_sib = (0, y, sib)

    def w1_load(j, k, q):
        return pltpu.make_async_copy(w1_cols(w1_ref, S + j, q), w1b.at[j, k], ls1.at[j, k])

    steps = [(j, i, mine[i]) for j in range(B) for i in range(2)] + [(j, 2 + i, theirs[i]) for j in range(B) for i in range(2)]
    for j, k, q in steps:
        w1_load(j, k, q).start()
    bar = pltpu.get_barrier_semaphore()
    pl.semaphore_signal(bar, inc=1, device_id=dev_sib, device_id_type=MESH)
    pl.semaphore_wait(bar, 1)
    cps = {}
    for j in range(B):
        for i in range(2):
            q = mine[i]
            dmf[j, q] = (dms_ref[j, i].astype(F32) + dmx_ref[j, i].astype(F32)).astype(BF)
            cps[j, i] = remote(dmf.at[j, q], dmf.at[j, q], (ss, rs), 2 * j + i, dev_sib)
            cps[j, i].start()
    for n, (j, k, q) in enumerate(steps):
        if k >= 2:
            cps[j, k - 2].wait_recv()
        du_f = grad_u(u_ref[S + j, q], dmf[j, q].astype(F32))
        db1_ref[j, q] = jnp.sum(du_f, axis=0, keepdims=True)
        du_ref[j, q] = du_f.astype(BF)
        w1_load(j, k, q).wait()
        part = dot(w1b[j, k], du_f.T.astype(BF))
        acc[...] = (dxt_ref[...] if n == 0 else acc[...]) + part
    dxp_ref[...] = acc[...].T.astype(BF)
    for cp in cps.values():
        cp.wait_send()


def second_call(dms, dmx, u, dxt, w1):
    outs = [sds((B, 4, T, 512), BF), sds((B, 4, 1, 512), F32), sds((T, H), BF)]
    return pl.pallas_call(
        second_kernel, out_shape=outs, name="mid",
        in_specs=[VMEM] * 4 + [ANY], out_specs=[VMEM] * 3,
        scratch_shapes=[pltpu.VMEM((B, 4, H, 512), BF), pltpu.VMEM((B, 4, T, Q), BF), pltpu.VMEM((H, T), F32),
                        pltpu.SemaphoreType.DMA((B, 4)), pltpu.SemaphoreType.DMA((2 * B,)), pltpu.SemaphoreType.DMA((2 * B,))],
        compiler_params=pltpu.CompilerParams(collective_id=1, has_side_effects=True, vmem_limit_bytes=32 * 1024 * 1024),
        cost_estimate=pl.CostEstimate(flops=2 * 10 ** 9, bytes_accessed=14 << 20, transcendentals=0),
    )(dms, dmx, u, dxt, w1)


def last_grads_kernel(x_ref, du_ref, dba_ref, dbb_ref, dw1_in, dw1_ref, db1_ref, ob1, xt, so1):
    xt[...] = x_ref[...].T

    def put1(t):
        return pltpu.make_async_copy(ob1.at[t % NB1], dw1_ref.at[:, (S * 4 + t) * 512:(S * 4 + t + 1) * 512], so1.at[t % NB1])

    for t in range(B * 4):
        if t >= NB1:
            put1(t - NB1).wait()
        ob1[t % NB1] = dot(xt[...], du_ref[t // 4, t % 4])
        put1(t).start()
    for j in range(NC):
        for q in range(4):
            src = dba_ref[j, q] if j < S else dbb_ref[j - S, q]
            db1_ref[:, (j * 4 + q) * 512:(j * 4 + q + 1) * 512] = src
    for t in range(B * 4 - NB1, B * 4):
        put1(t).wait()


def last_grads_call(x, du, dba, dbb, dw1):
    outs = [sds((H, NC * 2048), F32), sds((1, NC * 2048), F32)]
    return pl.pallas_call(
        last_grads_kernel, out_shape=outs, name="gb",
        in_specs=[VMEM] * 4 + [ANY], out_specs=[ANY, VMEM],
        scratch_shapes=[pltpu.VMEM((NB1, H, 512), F32), pltpu.VMEM((H, T), BF), pltpu.SemaphoreType.DMA((NB1,))],
        input_output_aliases={4: 0},
        compiler_params=pltpu.CompilerParams(vmem_limit_bytes=24 * 1024 * 1024),
        cost_estimate=pl.CostEstimate(flops=10 ** 9, bytes_accessed=26 << 20, transcendentals=0),
    )(x, du, dba, dbb, dw1)


def solution(mesh):
    data_spec = P('dp', 'hd')
    hid_spec = P('hd')
    in_specs = (data_spec, P('hd', 'ff'), P('ff'), P('ff', 'hd'), hid_spec, hid_spec, hid_spec, data_spec)
    out_specs = (data_spec, data_spec, P(('dp', 'hd'), 'ff'), P(('dp', 'ff'), 'hd'), P(('dp', 'ff')), P(('dp', 'hd')), P(('dp', 'hd')), P(('dp', 'hd')))

    def device_step(x, w1, b1, w2, b2, gam, beta, dy):
        b2, gam, beta = (a.reshape(1, H) for a in (b2, gam, beta))
        m, u, d, dr, nrm, dmf, dms = forward_call(x, w1, b1.reshape(NC * 4, 1, 512), w2, b2, gam, dy)
        dmx = lax.ppermute(dms, 'hd', [(0, 2), (2, 0), (1, 3), (3, 1)])
        dw1, dw2, y, db2, dgam, dbeta, dba, dxt = first_grads_call(m, u, d, dr, nrm, dmf, x, gam, beta, dy, w1)
        du, dbb, dxp = second_call(dms, dmx, u, dxt, w1)
        dxr = lax.ppermute(dxp, 'ff', [(0, 1), (1, 0)])
        dw1, db1 = last_grads_call(x, du, dba, dbb, dw1)
        dx = (ALPHA * dr + (dxp.astype(F32) + dxr.astype(F32))).astype(BF)
        return y, dx, dw1, dw2, db1.reshape(-1), db2.reshape(-1), dgam.reshape(-1), dbeta.reshape(-1)

    return jax.shard_map(device_step, mesh=mesh, in_specs=in_specs, out_specs=out_specs, check_vma=False)
```

time: 298 us -> 110 us (0.37)
  Pallas kernels: 0 us -> 100 us
  waiting for transfers between devices: 99 us -> 0.01 us
  local copies, waits for them, and re-layouts: 82.9 us -> 5.41 us
  matrix products: 65.2 us -> 0 us
  other arithmetic: 22.5 us -> 0.82 us
  between operations: 13.9 us -> 0.76 us
  blocking collectives: 12.4 us -> 0 us
    pallas_call x0 -> x4, Pallas kernels: none -> 100 us  [the longest x1 59.6 us: forward_call(): pl.pallas_call(forward_kernel, out_shape=outs, name='fwd', in_specs=[VMEM...]
    psum x4 -> x0, waiting for transfers between devices: 98.9 us -> none  [the longest x1 57.1 us: device_step(): u_summed = lax.psum(u_part.astype(jnp.bfloat16), 'hd')]
    dot_general x6 -> x0, matrix products: 65.2 us -> none  [the longest x1 18.1 us: device_step(): jnp.einsum('th,tbkc->hbkc', x_loc, du_b, preferred_element_type=jnp.float32)]
    unnamed x17 -> x22, local copies, waits for them, and re-layouts: 43.2 us -> 5.41 us
    reshape x2 -> x0, local copies, waits for them, and re-layouts: 33 us -> none  [the longest x1 30.6 us: device_step(): w_up4 = w_up.reshape(hid_loc, n_blocks, 2, PAIR)]
    psum x2 -> x0, blocking collectives: 12.4 us -> none  [the longest x1 6.22 us: device_step(): lax.psum(jnp.stack([jnp.sum(g_dy, axis=1), jnp.sum(g_dy * normed, axis=1)...]
    convert_element_type x4 -> x1, other arithmetic: 10.1 us -> 0.82 us  [device_step(): dx = (ALPHA * dr + (dxp.astype(F32) + dxr.astype(F32))).astype(BF)]
    reduce_sum x4 -> x0, other arithmetic: 8.62 us -> none  [the longest x1 3.01 us: device_step(): db_up = jnp.sum(du_f, axis=0).reshape(2 * ffn_loc)]
  transfers between devices with their start and end apart: 4 -> 2, of which waited for: 3 -> 0; matrix products, arithmetic and copies ran while one was open for 24% -> 0% of each run, Pallas kernels for 0% -> 27%
where the time goes in v1:
time: 110 us; the launch traced here: 109 us
  Pallas kernels  100 us (91%)
  local copies, waits for them, and re-layouts  5.41 us (5%)
  starting transfers between devices  2.51 us (2%)
    pallas_call x1, Pallas kernels, forward_call(): pl.pallas_call(forward_kernel, out_shape=outs, name='fwd', in_specs=[VMEM...  59.6 us
    pallas_call x1, Pallas kernels, first_grads_call(): pl.pallas_call(first_grads_kernel, out_shape=outs, name='ga', in_specs=[V...  19.8 us
    pallas_call x1, Pallas kernels, second_call(): pl.pallas_call(second_kernel, out_shape=outs, name='mid', in_specs=[VMEM]...  11 us
    pallas_call x1, Pallas kernels, last_grads_call(): pl.pallas_call(last_grads_kernel, out_shape=outs, name='gb', in_specs=[VM...  9.5 us
    unnamed x22, local copies, waits for them, and re-layouts  5.41 us
  transfers between devices with their start and end apart: 2, of which 0 were waited for; matrix products, arithmetic and copies ran while one was open for 0% of the time, Pallas kernels for 27%

profile of v1, /device:TPU:0, one launch (start us, length us, event | category | flops | bytes accessed | tf_op | source)
XLA Modules:
  0.0 109.5 jit_solution(6598769848337932767)
XLA Ops:
  0.6 0.0 copy-start.1
  0.6 0.0 copy-start.9
  0.7 0.0 copy-start.4
  0.7 0.0 copy-start.10
  0.7 59.6 %fwd.1 = (bf16[5,4,128,256]{3,2,1,0:T(8,128)(2,1)}, bf16[5,4,128,512]{3,2,1,0:T(8,128)(2,1)}, bf16[128,1024]{1,0:T(8,128)(2,1)}, f32[128,1024]{1,0:T(8,128)}, f3...) custom-call(bf16[128,1024]{1,0:T(8,128)(2,1)} %x_ref.5, ...), custom_call_target="tpu_custom_call" | custom-call | flops 5000000000 | bytes 33554432 | tf_op jit(solution)/shard_map/fwd/pallas_call | solution.py:295
  60.3 0.0 copy-start
  60.3 1.0 collective-permute-start
  61.3 0.0 copy-done.1
  61.3 0.0 copy-done.9
  61.3 0.0 copy-done.4
  61.3 0.0 copy-done.10
  61.3 0.0 copy-start.2
  61.3 1.0 copy-done.2
  62.4 0.0 copy-start.3
  62.4 1.3 %copy-done.3 = bf16[5,4,128,256]{3,2,1,0:T(8,128)(2,1)S(1)} copy-done((bf16[5,4,128,256]{3,2,1,0:T(8,128)(2,1)S(1)}, bf16[5,4,128,256]{3,2,1,0:T(8,128)(2,1)}, u32[]{:S(2)}) %copy-start.3) | copy-done | bytes 1310744
  63.7 0.0 copy-start.5
  63.7 1.0 copy-done.5
  64.7 0.0 copy-start.6
  64.7 1.0 copy-done.6
  65.8 0.0 copy-start.8
  65.8 0.9 copy-done.8
  66.7 0.0 copy-start.7
  66.7 19.8 %ga.1 = (f32[1024,10240]{1,0:T(8,128)}, f32[5120,1024]{1,0:T(8,128)}, bf16[128,1024]{1,0:T(8,128)(2,1)}, f32[1,1024]{1,0:T(1,128)}, f32[1,1024]{1,0:T(1,128)}, /...) custom-call(bf16[5,4,128,256]{3,2,1,0:T(8,128)(2,1)S(1)} %copy-done.3, ...), custom_call_target="tpu_custom_call" | custom-call | flops 3000000000 | bytes 46137344 | tf_op jit(solution)/shard_map/ga/pallas_call | solution.py:357
  86.6 0.0 collective-permute-done.dmx_ref
  86.6 0.0 copy-done
  86.6 0.0 copy-done.7
  86.6 11.0 %mid.1 = (bf16[3,4,128,512]{3,2,1,0:T(8,128)(2,1)S(1)}, f32[3,4,1,512]{3,2,1,0:T(1,128)S(1)}, bf16[128,1024]{1,0:T(8,128)(2,1)S(1)}) custom-call(bf16[3,2,128,256]{3,2,1,0:T(8,128)(2,1)S(1)} %copy-done.7, bf16[3,2,128,256]{3,2,1,0:T(8,128)(2,1)S(1)} %collective-permute-done.dmx_ref, bf16[5,4,128,512]{3,2,1,0:T(8,128)(2,1)S(1)} %copy-done, ...), custom_call_target="tpu_custom_call" | custom-call | flops 2000000000 | bytes 14680064 | tf_op jit(solution)/shard_map/mid/pallas_call | solution.py:409
  97.6 1.5 %collective-permute-start.1 = (bf16[128,1024]{1,0:T(8,128)(2,1)S(1)}, bf16[128,1024]{1,0:T(8,128)(2,1)S(1)}, u32[]{:S(2)}, u32[]{:S(2)}) collective-permute-start(bf16[128,1024]{1,0:T(8,128)(2,1)S(1)} %get-tuple-element.37), channel_id=1, source_target_pairs={{0,4},{4,0},{1,5},{5,1},{2,6},{6,2},{3,7},{7,3}} | collective-permute-start | bytes 786440 | tf_op jit(solution)/shard_map/ppermute | solution.py:462
  99.1 9.5 %gb.1 = (f32[1024,10240]{1,0:T(8,128)}, f32[1,10240]{1,0:T(1,128)}) custom-call(bf16[128,1024]{1,0:T(8,128)(2,1)S(1)} %copy-done.1, bf16[3,4,128,512]{3,2,1,0:T(8,128)(2,1)S(1)} %get-tuple-element.38.du_ref, f32[2,4,1,512]{3,2,1,0:T(1,128)S(1)} %get-tuple-element.39.dba_ref, ...), custom_call_target="tpu_custom_call", output_to_operand_aliasing={{0}: (4, {})} | custom-call | flops 1000000000 | bytes 27262976 | tf_op jit(solution)/shard_map/gb/pallas_call | solution.py:440
  108.6 0.0 collective-permute-done.1
  108.6 0.8 add_convert_fusion
Async XLA Ops:
  0.6 60.7 %copy-start.1 = (bf16[128,1024]{1,0:T(8,128)(2,1)S(1)}, bf16[128,1024]{1,0:T(8,128)(2,1)}, u32[]{:S(2)}) copy-start(bf16[128,1024]{1,0:T(8,128)(2,1)} %x_ref.5) | copy-start | bytes 786436
  0.6 60.7 %copy-start.9 = (f32[1024]{0:T(1024)S(1)}, f32[1024]{0:T(1024)}, u32[]{:S(2)}) copy-start(f32[1024]{0:T(1024)} %param.13) | copy-start | bytes 12292
  0.7 60.7 %copy-start.4 = (bf16[128,1024]{1,0:T(8,128)(2,1)S(1)}, bf16[128,1024]{1,0:T(8,128)(2,1)}, u32[]{:S(2)}) copy-start(bf16[128,1024]{1,0:T(8,128)(2,1)} %dy_ref.3) | copy-start | bytes 786436
  0.7 60.6 %copy-start.10 = (f32[1024]{0:T(1024)S(1)}, f32[1024]{0:T(1024)}, u32[]{:S(2)}) copy-start(f32[1024]{0:T(1024)} %param.14) | copy-start | bytes 12292
  60.3 26.3 %copy-start = (bf16[5,4,128,512]{3,2,1,0:T(8,128)(2,1)S(1)}, bf16[5,4,128,512]{3,2,1,0:T(8,128)(2,1)}, u32[]{:S(2)}) copy-start(bf16[5,4,128,512]{3,2,1,0:T(8,128)(2,1)} %get-tuple-element.29.u_ref) | copy-start | bytes 7864324
  60.3 26.3 %collective-permute-start = (bf16[3,2,128,256]{3,2,1,0:T(8,128)(2,1)}, bf16[3,2,128,256]{3,2,1,0:T(8,128)(2,1)S(1)}, u32[]{:S(2)}, u32[]{:S(2)}) collective-permute-start(bf16[3,2,128,256]{3,2,1,0:T(8,128)(2,1)} %get-tuple-element.35.dms_ref), channel_id=1, source_target_pairs={{0,2},{2,0},{1,3},{3,1},{4,6},{6,4},{5,7},{7,5}} | collective-permute-start | bytes 1179656 | tf_op jit(solution)/shard_map/ppermute | solution.py:459
  61.3 1.0 copy-start.2
  62.4 1.3 %copy-start.3 = (bf16[5,4,128,256]{3,2,1,0:T(8,128)(2,1)S(1)}, bf16[5,4,128,256]{3,2,1,0:T(8,128)(2,1)}, u32[]{:S(2)}) copy-start(bf16[5,4,128,256]{3,2,1,0:T(8,128)(2,1)} %get-tuple-element.28.m_ref) | copy-start | bytes 3932164
  63.7 1.0 copy-start.5
  64.7 1.0 copy-start.6
  65.8 0.9 copy-start.8
  66.7 19.9 %copy-start.7 = (bf16[3,2,128,256]{3,2,1,0:T(8,128)(2,1)S(1)}, bf16[3,2,128,256]{3,2,1,0:T(8,128)(2,1)}, u32[]{:S(2)}) copy-start(bf16[3,2,128,256]{3,2,1,0:T(8,128)(2,1)} %get-tuple-element.35.dms_ref) | copy-start | bytes 1179652
  97.6 11.0 %collective-permute-start.1 = (bf16[128,1024]{1,0:T(8,128)(2,1)S(1)}, bf16[128,1024]{1,0:T(8,128)(2,1)S(1)}, u32[]{:S(2)}, u32[]{:S(2)}) collective-permute-start(bf16[128,1024]{1,0:T(8,128)(2,1)S(1)} %get-tuple-element.37), channel_id=1, source_target_pairs={{0,4},{4,0},{1,5},{5,1},{2,6},{6,2},{3,7},{7,3}} | collective-permute-start | bytes 786440 | tf_op jit(solution)/shard_map/ppermute | solution.py:462

commit v2 on v1

v2 whole, which is shorter than its diff:
```python
import functools
import math
import jax
import jax.numpy as jnp
from jax import lax
from jax.experimental import pallas as pl
from jax.experimental.pallas import tpu as pltpu
from jax.sharding import PartitionSpec as P

PAIR = 128
ALPHA = math.sqrt(140.0)
LN_EPS = 1e-5
C0 = math.sqrt(2.0 / math.pi)
C1 = 0.044715
MESH = pl.DeviceIdType.MESH
F32 = jnp.float32
BF = jnp.bfloat16
T = 128
H = 1024
NU = 10
CH = ((0, 1), (1, 3), (3, 5), (5, 7), (7, 9), (9, 10))
NC = len(CH)
VLIM = 62 * 1024 * 1024

VMEM = pl.BlockSpec(memory_space=pltpu.VMEM)
ANY = pl.BlockSpec(memory_space=pl.ANY)


def sds(shape, dtype):
    return jax.ShapeDtypeStruct(shape, dtype)


def dot(a, b):
    return jnp.dot(a, b, preferred_element_type=F32)


def gelu(g):
    t = jnp.tanh(C0 * (g + C1 * (g * g * g)))
    return g * (0.5 * (1.0 + t))


def gelu_both(g):
    g2 = g * g
    t = jnp.tanh(C0 * (g + C1 * (g2 * g)))
    cdf = 0.5 * (1.0 + t)
    slope = cdf + (0.5 * g) * (1.0 - t * t) * (C0 * (1.0 + (3.0 * C1) * g2))
    return g * cdf, slope


def grad_u(u, dm):
    u = u.astype(F32)
    v, g = u[:, :PAIR], u[:, PAIR:]
    val, slope = gelu_both(g)
    return jnp.concatenate([dm * val, dm * v * slope], axis=1)


def places():
    h = lax.axis_index("hd")
    y = lax.axis_index("ff")
    c = lax.rem(h, 2)
    sib = h + 1 - 2 * c
    xn = lax.rem(h + 2, 4)
    xs = lax.rem(sib + 2, 4)
    return h, y, c, sib, xn, xs


def remote(src, dst, sems, k, dev):
    return pltpu.make_async_remote_copy(src_ref=src, dst_ref=dst, send_sem=sems[0].at[k], recv_sem=sems[1].at[k],
                                        device_id=dev, device_id_type=MESH)


def unit(j, q):
    u0, u1 = CH[j]
    return 4 * u0 + q * (u1 - u0)


def aligned(start, size, tile):
    return pl.ds(pl.multiple_of(start * tile, tile), size * tile)


N_SEM = {"ud": 2 * NC, "ux": NC, "mx": NC, "md": NC, "mf": NC, "gx": NC, "gd": NC, "gf": NC, "fy": 2, "st": 3,
         "dd": 2 * NC, "dx": NC, "df": 2 * NC}
SEM_NAMES = list(N_SEM)


def comm_kernel(x_ref, w1_ref, b1_ref, w2_ref, b2_ref, gam_ref, dy_ref,
                m_out, du_out, d_out, dr_out, nrm_out, db1_ref, dxp_ref,
                w1b, w2b, ub, rb, xsb, xrb, facc, fs, fr, stb, dmb, dmr, dsum, dxr, m_ref, u_ref, dmf, du_ref,
                d_ref, dr_ref, nrm_ref, acc,
                ls1, ls2, os, *sem_list):
    sems = {n: (sem_list[2 * i], sem_list[2 * i + 1]) for i, n in enumerate(SEM_NAMES)}
    h, y, c, sib, xn, xs = places()
    dev_sib, dev_x, dev_xs, dev_y = (0, y, sib), (0, y, xn), (0, y, xs), (0, 1 - y, h)
    order = [xs, xn, sib, h]
    outs = []

    def w1_load(j, k):
        u0, u1 = CH[j]
        n = u1 - u0
        return pltpu.make_async_copy(w1_ref.at[:, aligned(unit(j, order[k]), n, 256)], w1b.at[k, :, u0 * 256:u1 * 256],
                                     ls1.at[j, k])

    def w2_load(j):
        rows = slice(4 * 128 * CH[j][0], 4 * 128 * CH[j][1])
        return pltpu.make_async_copy(w2_ref.at[rows, :], w2b.at[rows, :], ls2.at[j])

    def put(src, dst):
        cp = pltpu.make_async_copy(src, dst, os.at[len(outs)])
        cp.start()
        outs.append(cp)

    for j in range(NC + 1):
        for k in (0, 1):
            if j < NC:
                w1_load(j, k).start()
        for k in (2, 3):
            if j > 0:
                w1_load(j - 1, k).start()
    bar = pltpu.get_barrier_semaphore()
    for dev in (dev_sib, dev_x, dev_xs, dev_y):
        pl.semaphore_signal(bar, inc=1, device_id=dev, device_id_type=MESH)
    pl.semaphore_wait(bar, 4)

    live = []

    def send(src, dst, name, k, dev):
        cp = remote(src, dst, sems[name], k, dev)
        cp.start()
        live.append(cp)
        return cp

    def u_part(j, ks):
        u0, u1 = CH[j]
        us = slice(u0, u1)
        for k in ks:
            w1_load(j, k).wait()
            r = dot(x_ref[...], w1b[k, :, u0 * 256:u1 * 256]).astype(BF)
            for i in range(u1 - u0):
                ub[k, u0 + i] = r[:, i * 256:(i + 1) * 256]
            if k == 0:
                c_ud[j, 1] = send(ub.at[0, us], rb.at[1, us], "ud", 2 * j + 1, dev_sib)
            if k == 2:
                c_ud[j, 0] = send(ub.at[2, us], rb.at[0, us], "ud", 2 * j, dev_sib)

    def ux(j):
        u_part(j, (0, 1))

    def uo(j):
        u_part(j, (2, 3))

    def s1(j):
        us = slice(*CH[j])
        c_ud[j, 1].wait_recv()
        xsb[us] = (ub[1, us].astype(F32) + rb[1, us].astype(F32)).astype(BF)
        c_ux[j] = send(xsb.at[us], xrb.at[us], "ux", j, dev_x)

    def s2(j):
        u0, u1 = CH[j]
        us = slice(u0, u1)
        c_ud[j, 0].wait_recv()
        c_ux[j].wait_recv()
        for i in range(u1 - u0):
            a = u0 + i
            u = ub[3, a].astype(F32) + rb[0, a].astype(F32) + xrb[a].astype(F32) + b1_ref[unit(j, h) + i]
            u = u.astype(BF)
            u_ref[h, a] = u
            u = u.astype(F32)
            m_ref[h, a] = (u[:, :PAIR] * gelu(u[:, PAIR:])).astype(BF)
        c_mx[j] = send(m_ref.at[h, us], m_ref.at[h, us], "mx", j, dev_x)
        c_md[j] = send(m_ref.at[h, us], m_ref.at[h, us], "md", j, dev_sib)

    def s3(j):
        us = slice(*CH[j])
        c_mx[j].wait_recv()
        c_mf[j] = send(m_ref.at[xn, us], m_ref.at[xn, us], "mf", j, dev_sib)

    def s4(j):
        u0, u1 = CH[j]
        c_md[j].wait_recv()
        c_mf[j].wait_recv()
        w2_load(j).wait()
        m = jnp.concatenate([m_ref[q, a] for q in range(4) for a in range(u0, u1)], axis=1)
        for n in range(2):
            cols = slice(n * 512, (n + 1) * 512)
            part = dot(m, w2b[4 * 128 * u0:4 * 128 * u1, cols])
            if j > 0:
                part = facc[:, cols] + part
            if j < NC - 1:
                facc[:, cols] = part
            else:
                fs[n] = part.astype(BF)
                c_fy.append(send(fs.at[n], fr.at[n], "fy", n, dev_y))

    def gather_u(j):
        us = slice(*CH[j])
        c_gx[j] = send(u_ref.at[h, us], u_ref.at[h, us], "gx", j, dev_x)
        c_gd[j] = send(u_ref.at[h, us], u_ref.at[h, us], "gd", j, dev_sib)

    def forward_u(j):
        us = slice(*CH[j])
        c_gx[j].wait_recv()
        c_gf[j] = send(u_ref.at[xn, us], u_ref.at[xn, us], "gf", j, dev_sib)

    c_ud, c_ux, c_mx, c_md, c_mf, c_fy, c_gx, c_gd, c_gf = {}, {}, {}, {}, {}, [], {}, {}, {}
    ux(0)
    ux(1)
    s1(0)
    uo(0)
    ux(2)
    s1(1)
    uo(1)
    ux(3)
    s1(2)
    for j in range(NC):
        w2_load(j).start()
    uo(2)
    ux(4)
    s1(3)
    s2(0)
    ux(5)
    s1(4)
    uo(3)
    s1(5)
    uo(4)
    s2(1)
    uo(5)
    s2(2)
    s2(3)
    s2(4)
    s3(0)
    s4(0)
    s2(5)
    for j in range(NC):
        gather_u(j)
    for j in range(1, NC):
        s3(j)
        if j > 1:
            s4(j - 1)
    s4(NC - 1)
    put(m_ref, m_out)

    for n in range(2):
        cols = slice(n * 512, (n + 1) * 512)
        c_fy[n].wait_recv()
        f = fs[n].astype(F32) + fr[n].astype(F32)
        nrm_ref[:, cols] = ALPHA * x_ref[:, cols].astype(F32) + f + b2_ref[:, cols]
    r = nrm_ref[...]
    gdy = dy_ref[...].astype(F32) * gam_ref[...]
    m_loc = jnp.sum(r, axis=1, keepdims=True) * (1.0 / H)
    cen = r - m_loc
    m2 = jnp.sum(cen * cen, axis=1, keepdims=True)
    sg = jnp.sum(gdy, axis=1, keepdims=True)
    cg = jnp.sum(gdy * cen, axis=1, keepdims=True)
    lane = lax.broadcasted_iota(jnp.int32, (T, 128), 1)
    pack = jnp.where(lane == 0, m_loc, jnp.where(lane == 1, m2, jnp.where(lane == 2, sg, cg)))
    stb[h] = pack.T[0:8]
    c_st = [send(stb.at[h], stb.at[h], "st", i, dev) for i, dev in enumerate((dev_sib, dev_x, dev_xs))]
    for cp in c_st:
        cp.wait_recv()
    st = [stb[i] for i in range(4)]
    mu = ((st[0][0:1] + st[1][0:1]) + (st[2][0:1] + st[3][0:1])) * 0.25
    m2t = jnp.zeros_like(mu)
    sgt = jnp.zeros_like(mu)
    cgt = jnp.zeros_like(mu)
    for i in range(4):
        delta = st[i][0:1] - mu
        m2t += st[i][1:2] + (H * delta) * delta
        sgt += st[i][2:3]
        cgt += st[i][3:4] + delta * st[i][2:3]
    rho = lax.rsqrt(m2t * (1.0 / (4 * H)) + LN_EPS)
    rows = jnp.concatenate([mu, rho, sgt * (1.0 / (4 * H)), cgt * rho * (1.0 / (4 * H)), jnp.zeros((124, T), F32)], axis=0)
    colst = rows.T
    mu_c, rho_c, mg_c, mgr_c = (colst[:, i:i + 1] for i in range(4))
    nrm = (r - mu_c) * rho_c
    dr = rho_c * (gdy - mg_c - nrm * mgr_c)
    nrm_ref[...] = nrm
    dr_ref[...] = dr
    d_ref[...] = dr.astype(BF)
    d_t = dr.T.astype(BF)
    put(nrm_ref, nrm_out)
    put(dr_ref, dr_out)
    put(d_ref, d_out)

    c_dd, c_dx, c_df = {}, {}, {}
    mine, mine_k, theirs, theirs_k = (h, xn), (3, 1), (sib, xs), (2, 0)

    def dm_part(j):
        u0, u1 = CH[j]
        n = u1 - u0
        for i, q in enumerate(theirs + mine):
            r = dot(w2b[aligned(unit(j, q), n, 128), :], d_t).T.astype(BF)
            for a in range(n):
                dmb[i, u0 + a] = r[:, a * 128:(a + 1) * 128]
            if i < 2:
                c_dd[j, i] = send(dmb.at[i, u0:u1], dmr.at[i, u0:u1], "dd", 2 * j + i, dev_sib)

    def dm_sum(j):
        us = slice(*CH[j])
        for i in range(2):
            c_dd[j, i].wait_recv()
            dsum[i, us] = (dmb[2 + i, us].astype(F32) + dmr[i, us].astype(F32)).astype(BF)
        c_dx[j] = send(dsum.at[:, us], dxr.at[:, us], "dx", j, dev_x)

    def dm_full(j):
        us = slice(*CH[j])
        c_dx[j].wait_recv()
        for i in range(2):
            q = mine[i]
            dmf[q, us] = (dsum[i, us].astype(F32) + dxr[1 - i, us].astype(F32)).astype(BF)
            c_df[j, i] = send(dmf.at[q, us], dmf.at[q, us], "df", 2 * j + i, dev_sib)

    def grads(j, qs, ks, first):
        u0, u1 = CH[j]
        for q, k in zip(qs, ks):
            parts = []
            for a in range(u0, u1):
                du_f = grad_u(u_ref[q, a], dmf[q, a].astype(F32))
                db1_ref[unit(j, q) + a - u0] = jnp.sum(du_f, axis=0, keepdims=True)
                du_ref[q, a] = du_f.astype(BF)
                parts.append(du_f)
            du_t = jnp.concatenate(parts, axis=1).T.astype(BF)
            part = dot(w1b[k, :, u0 * 256:u1 * 256], du_t)
            acc[...] = part if first else acc[...] + part
            first = False

    def grads_mine(j):
        dm_full(j)
        grads(j, mine, mine_k, j == 0)

    def grads_theirs(j):
        us = slice(*CH[j])
        for i in range(2):
            c_df[j, i].wait_recv()
        grads(j, theirs, theirs_k, False)
        put(du_ref.at[:, us], du_out.at[:, us])

    dm_part(0)
    dm_part(1)
    dm_sum(0)
    for j in range(2, NC):
        dm_part(j)
        dm_sum(j - 1)
        forward_u(j - 2)
    dm_sum(NC - 1)
    forward_u(NC - 2)
    forward_u(NC - 1)
    for cp in list(c_gd.values()) + list(c_gf.values()):
        cp.wait_recv()
    for j in range(NC):
        grads_mine(j)
        if j > 0:
            grads_theirs(j - 1)
    grads_theirs(NC - 1)
    dxp_ref[...] = acc[...].T.astype(BF)
    for cp in live:
        cp.wait_send()
    for cp in outs:
        cp.wait()


def comm_call(x, w1, b1, w2, b2, gam, dy):
    scratch = [pltpu.VMEM((4, H, NU * 256), BF), pltpu.VMEM((4 * NU * 128, H), BF),
               pltpu.VMEM((4, NU, T, 256), BF), pltpu.VMEM((2, NU, T, 256), BF),
               pltpu.VMEM((NU, T, 256), BF), pltpu.VMEM((NU, T, 256), BF),
               pltpu.VMEM((T, H), F32), pltpu.VMEM((2, T, 512), BF), pltpu.VMEM((2, T, 512), BF),
               pltpu.VMEM((4, 8, T), F32),
               pltpu.VMEM((4, NU, T, 128), BF), pltpu.VMEM((2, NU, T, 128), BF),
               pltpu.VMEM((2, NU, T, 128), BF), pltpu.VMEM((2, NU, T, 128), BF),
               pltpu.VMEM((4, NU, T, 128), BF), pltpu.VMEM((4, NU, T, 256), BF), pltpu.VMEM((4, NU, T, 128), BF),
               pltpu.VMEM((4, NU, T, 256), BF),
               pltpu.VMEM((T, H), BF), pltpu.VMEM((T, H), F32), pltpu.VMEM((T, H), F32), pltpu.VMEM((H, T), F32),
               pltpu.SemaphoreType.DMA((NC, 4)), pltpu.SemaphoreType.DMA((NC,)), pltpu.SemaphoreType.DMA((NC + 4,))]
    for n in SEM_NAMES:
        scratch += [pltpu.SemaphoreType.DMA((N_SEM[n],)), pltpu.SemaphoreType.DMA((N_SEM[n],))]
    outs = [sds((4, NU, T, 128), BF), sds((4, NU, T, 256), BF), sds((T, H), BF), sds((T, H), F32), sds((T, H), F32),
            sds((4 * NU, 1, 256), F32), sds((T, H), BF)]
    return pl.pallas_call(
        comm_kernel, out_shape=outs, name="comm",
        in_specs=[VMEM, ANY, VMEM, ANY, VMEM, VMEM, VMEM], out_specs=[ANY] * 5 + [VMEM] * 2, scratch_shapes=scratch,
        compiler_params=pltpu.CompilerParams(collective_id=0, has_side_effects=True, vmem_limit_bytes=VLIM),
        cost_estimate=pl.CostEstimate(flops=8 * 10 ** 9, bytes_accessed=32 << 20, transcendentals=0),
    )(x, w1, b1, w2, b2, gam, dy)


NB2 = 6
NB1 = 6


def grads_kernel(m_hbm, du_hbm, d_hbm, nrm_hbm, dr_hbm, db1_in, x_ref, gam_ref, beta_ref, dy_ref,
                 dw1_ref, dw2_ref, y_ref, db1_ref, db2_ref, dgam_ref, dbeta_ref,
                 m_ref, du_ref, d_ref, nrm_ref, dr_ref, ob2, ob1, xt, ls, so2, so1):
    loads = [pltpu.make_async_copy(a, b, ls.at[i]) for i, (a, b) in enumerate(
        ((d_hbm, d_ref), (m_hbm, m_ref), (du_hbm, du_ref), (nrm_hbm, nrm_ref), (dr_hbm, dr_ref)))]
    for cp in loads:
        cp.start()
    tiles = [(j, q) for j in range(NC) for q in range(4)]

    def put2(t):
        j, q = tiles[t]
        n = CH[j][1] - CH[j][0]
        r0 = unit(j, q) * 128
        return pltpu.make_async_copy(ob2.at[t % NB2, :n * 128], dw2_ref.at[r0:r0 + n * 128, :], so2.at[t % NB2])

    def put1(t):
        j, q = tiles[t]
        n = CH[j][1] - CH[j][0]
        c0 = unit(j, q) * 256
        return pltpu.make_async_copy(ob1.at[t % NB1, :, :n * 256], dw1_ref.at[:, c0:c0 + n * 256], so1.at[t % NB1])

    loads[0].wait()
    loads[1].wait()
    for t, (j, q) in enumerate(tiles):
        if t >= NB2:
            put2(t - NB2).wait()
        for i, a in enumerate(range(*CH[j])):
            ob2[t % NB2, i * 128:(i + 1) * 128] = dot(m_ref[q, a].T, d_ref[...])
        put2(t).start()
        if t == 0:
            xt[...] = x_ref[...].T
    loads[2].wait()
    for t, (j, q) in enumerate(tiles):
        if t >= NB1:
            put1(t - NB1).wait()
        for i, a in enumerate(range(*CH[j])):
            ob1[t % NB1, :, i * 256:(i + 1) * 256] = dot(xt[...], du_ref[q, a])
        put1(t).start()
    loads[3].wait()
    loads[4].wait()
    dy = dy_ref[...].astype(F32)
    y_ref[...] = (gam_ref[...] * nrm_ref[...] + beta_ref[...]).astype(BF)
    db2_ref[...] = jnp.sum(dr_ref[...], axis=0, keepdims=True)
    dgam_ref[...] = jnp.sum(dy * nrm_ref[...], axis=0, keepdims=True)
    dbeta_ref[...] = jnp.sum(dy, axis=0, keepdims=True)
    for i in range(4 * NU):
        db1_ref[:, i * 256:(i + 1) * 256] = db1_in[i]
    last = len(tiles)
    for t in range(last - NB2, last):
        put2(t).wait()
    for t in range(last - NB1, last):
        put1(t).wait()


def grads_call(m, du, d, nrm, dr, db1, x, gam, beta, dy):
    outs = [sds((H, 4 * NU * 256), F32), sds((4 * NU * 128, H), F32), sds((T, H), BF), sds((1, 4 * NU * 256), F32),
            sds((1, H), F32), sds((1, H), F32), sds((1, H), F32)]
    return pl.pallas_call(
        grads_kernel, out_shape=outs, name="grads",
        in_specs=[ANY] * 5 + [VMEM] * 5, out_specs=[ANY, ANY] + [VMEM] * 5,
        scratch_shapes=[pltpu.VMEM((4, NU, T, 128), BF), pltpu.VMEM((4, NU, T, 256), BF), pltpu.VMEM((T, H), BF),
                        pltpu.VMEM((T, H), F32), pltpu.VMEM((T, H), F32),
                        pltpu.VMEM((NB2, 256, H), F32), pltpu.VMEM((NB1, H, 512), F32), pltpu.VMEM((H, T), BF),
                        pltpu.SemaphoreType.DMA((5,)), pltpu.SemaphoreType.DMA((NB2,)), pltpu.SemaphoreType.DMA((NB1,))],
        compiler_params=pltpu.CompilerParams(vmem_limit_bytes=40 * 1024 * 1024),
        cost_estimate=pl.CostEstimate(flops=4 * 10 ** 9, bytes_accessed=66 << 20, transcendentals=0),
    )(m, du, d, nrm, dr, db1, x, gam, beta, dy)


def solution(mesh):
    data_spec = P('dp', 'hd')
    hid_spec = P('hd')
    in_specs = (data_spec, P('hd', 'ff'), P('ff'), P('ff', 'hd'), hid_spec, hid_spec, hid_spec, data_spec)
    out_specs = (data_spec, data_spec, P(('dp', 'hd'), 'ff'), P(('dp', 'ff'), 'hd'), P(('dp', 'ff')), P(('dp', 'hd')), P(('dp', 'hd')), P(('dp', 'hd')))

    def device_step(x, w1, b1, w2, b2, gam, beta, dy):
        b2, gam, beta = (a.reshape(1, H) for a in (b2, gam, beta))
        m, du, d, dr, nrm, db1, dxp = comm_call(x, w1, b1.reshape(4 * NU, 1, 256), w2, b2, gam, dy)
        dxr = lax.ppermute(dxp, 'ff', [(0, 1), (1, 0)])
        dw1, dw2, y, db1, db2, dgam, dbeta = grads_call(m, du, d, nrm, dr, db1, x, gam, beta, dy)
        dx = (ALPHA * dr + (dxp.astype(F32) + dxr.astype(F32))).astype(BF)
        return y, dx, dw1, dw2, db1.reshape(-1), db2.reshape(-1), dgam.reshape(-1), dbeta.reshape(-1)

    return jax.shard_map(device_step, mesh=mesh, in_specs=in_specs, out_specs=out_specs, check_vma=False)
```

time: 110 us -> 101 us (0.918)
  Pallas kernels: 100 us -> 90 us
  local copies, waits for them, and re-layouts: 5.41 us -> 6.88 us
    pallas_call x4 -> x2, Pallas kernels: 100 us -> 90 us  [the longest x1 68.6 us: comm_call(): pl.pallas_call(comm_kernel, out_shape=outs, name='comm', in_specs=[VMEM,...]
    unnamed x22 -> x20, local copies, waits for them, and re-layouts: 5.41 us -> 6.88 us
  transfers between devices with their start and end apart: 2 -> 1, of which waited for: 0 -> 0; matrix products, arithmetic and copies ran while one was open for 0% -> 0% of each run, Pallas kernels for 27% -> 21%
where the time goes in v2:
time: 101 us
  Pallas kernels  90 us (89%)
  local copies, waits for them, and re-layouts  6.88 us (7%)
  other arithmetic  1.77 us (2%)
  starting transfers between devices  1.51 us (1%)
    pallas_call x1, Pallas kernels, comm_call(): pl.pallas_call(comm_kernel, out_shape=outs, name='comm', in_specs=[VMEM,...  68.6 us
    pallas_call x1, Pallas kernels, grads_call(): pl.pallas_call(grads_kernel, out_shape=outs, name='grads', in_specs=[ANY]...  21.5 us
    unnamed x20, local copies, waits for them, and re-layouts  6.88 us
  transfers between devices with their start and end apart: 1, of which 0 were waited for; matrix products, arithmetic and copies ran while one was open for 0% of the time, Pallas kernels for 21%

profile of v2, /device:TPU:0, one launch (start us, length us, event | category | flops | bytes accessed | tf_op | source)
XLA Modules:
  0.0 100.9 jit_solution(9135559749012579282)
XLA Ops:
  0.6 0.0 copy-start.2
  0.6 0.0 copy-start.1
  0.7 0.0 copy-start.3
  0.7 0.0 copy-start.9
  0.7 68.6 %comm.1 = (bf16[4,10,128,128]{3,2,1,0:T(8,128)(2,1)}, bf16[4,10,128,256]{3,2,1,0:T(8,128)(2,1)}, bf16[128,1024]{1,0:T(8,128)(2,1)}, f32[128,1024]{1,0:T(8,128)},...) custom-call(bf16[128,1024]{1,0:T(8,128)(2,1)} %x_ref.3, bf16[1024,10240]{1,0:T(8,128)(2,1)} %w1_ref.1, ...), custom_call_target="tpu_custom_call" | custom-call | flops 8000000000 | bytes 33554432 | tf_op jit(solution)/shard_map/comm/pallas_call | solution.py:377
  69.2 1.5 %collective-permute-start = (bf16[128,1024]{1,0:T(8,128)(2,1)}, bf16[128,1024]{1,0:T(8,128)(2,1)S(1)}, u32[]{:S(2)}, u32[]{:S(2)}) collective-permute-start(bf16[128,1024]{1,0:T(8,128)(2,1)} %get-tuple-element.29), channel_id=1, source_target_pairs={{0,4},{4,0},{1,5},{5,1},{2,6},{6,2},{3,7},{7,3}} | collective-permute-start | bytes 786440 | tf_op jit(solution)/shard_map/ppermute | solution.py:467
  70.8 0.0 copy-done.2
  70.8 0.0 copy-done.1
  70.8 0.0 copy-done.3
  70.8 0.0 copy-done.9
  70.8 0.0 copy-start
  70.8 1.0 %copy-done = f32[128,1024]{1,0:T(8,128)S(1)} copy-done((f32[128,1024]{1,0:T(8,128)S(1)}, f32[128,1024]{1,0:T(8,128)}, u32[]{:S(2)}) %copy-start) | copy-done | bytes 524312
  71.8 0.0 copy-start.4
  71.8 1.7 %copy-done.4 = bf16[4,10,128,256]{3,2,1,0:T(8,128)(2,1)S(1)} copy-done((bf16[4,10,128,256]{3,2,1,0:T(8,128)(2,1)S(1)}, bf16[4,10,128,256]{3,2,1,0:T(8,128)(2,1)}, u32[]{:S(2)}) %copy-start.4) | copy-done | bytes 2621464
  73.5 0.0 copy-start.5
  73.6 1.3 %copy-done.5 = bf16[4,10,128,128]{3,2,1,0:T(8,128)(2,1)S(1)} copy-done((bf16[4,10,128,128]{3,2,1,0:T(8,128)(2,1)S(1)}, bf16[4,10,128,128]{3,2,1,0:T(8,128)(2,1)}, u32[]{:S(2)}) %copy-start.5) | copy-done | bytes 1310744
  74.9 0.0 copy-start.6
  74.9 1.0 %copy-done.6 = f32[128,1024]{1,0:T(8,128)S(1)} copy-done((f32[128,1024]{1,0:T(8,128)S(1)}, f32[128,1024]{1,0:T(8,128)}, u32[]{:S(2)}) %copy-start.6) | copy-done | bytes 524312
  75.9 0.0 copy-start.7
  75.9 0.9 copy-done.7
  76.9 0.0 copy-start.8
  76.9 0.8 copy-done.8
  77.6 21.5 %grads.1 = (f32[1024,10240]{1,0:T(8,128)}, f32[5120,1024]{1,0:T(8,128)}, bf16[128,1024]{1,0:T(8,128)(2,1)}, f32[1,10240]{1,0:T(1,128)}, f32[1,1024]{1,0:T(1,128)}, /*index=5*/f32[1,1024]{1,0:T(1,128)}, f32[1,1024]{1,0:T(1,128)}) custom-call(bf16[4,10,128,128]{3,2,1,0:T(8,128)(2,1)S(1)} %copy-done.5, bf16[4,10,128,256]{3,2,1,0:T(8,128)(2,1)S(1)} %copy-done.4, ...), custom_call_target="tpu_custom_call" | custom-call | flops 4000000000 | bytes 69206016 | tf_op jit(solution)/shard_map/grads/pallas_call | solution.py:446
  99.1 0.0 collective-permute-done
  99.1 1.8 %add_convert_fusion = bf16[128,1024]{1,0:T(8,128)(2,1)} fusion(bf16[128,1024]{1,0:T(8,128)(2,1)S(1)} %collective-permute-done, bf16[128,1024]{1,0:T(8,128)(2,1)} %get-tuple-element.29, f32[128,1024]{1,0:T(8,128)S(1)} %copy-done), kind=kLoop, calls=%fused_computation | loop fusion | flops 786432 | bytes 1310720 | tf_op jit(solution)/shard_map/convert_element_type | solution.py:469
Async XLA Ops:
  0.6 70.1 %copy-start.2 = (bf16[128,1024]{1,0:T(8,128)(2,1)S(1)}, bf16[128,1024]{1,0:T(8,128)(2,1)}, u32[]{:S(2)}) copy-start(bf16[128,1024]{1,0:T(8,128)(2,1)} %dy_ref.3) | copy-start | bytes 786436
  0.6 70.1 %copy-start.1 = (bf16[128,1024]{1,0:T(8,128)(2,1)S(1)}, bf16[128,1024]{1,0:T(8,128)(2,1)}, u32[]{:S(2)}) copy-start(bf16[128,1024]{1,0:T(8,128)(2,1)} %x_ref.3) | copy-start | bytes 786436
  0.7 70.1 %copy-start.3 = (f32[1024]{0:T(1024)S(1)}, f32[1024]{0:T(1024)}, u32[]{:S(2)}) copy-start(f32[1024]{0:T(1024)} %param.13) | copy-start | bytes 12292
  0.7 70.1 %copy-start.9 = (f32[1024]{0:T(1024)S(1)}, f32[1024]{0:T(1024)}, u32[]{:S(2)}) copy-start(f32[1024]{0:T(1024)} %param.14) | copy-start | bytes 12292
  69.2 29.9 %collective-permute-start = (bf16[128,1024]{1,0:T(8,128)(2,1)}, bf16[128,1024]{1,0:T(8,128)(2,1)S(1)}, u32[]{:S(2)}, u32[]{:S(2)}) collective-permute-start(bf16[128,1024]{1,0:T(8,128)(2,1)} %get-tuple-element.29), channel_id=1, source_target_pairs={{0,4},{4,0},{1,5},{5,1},{2,6},{6,2},{3,7},{7,3}} | collective-permute-start | bytes 786440 | tf_op jit(solution)/shard_map/ppermute | solution.py:467
  70.8 1.0 %copy-start = (f32[128,1024]{1,0:T(8,128)S(1)}, f32[128,1024]{1,0:T(8,128)}, u32[]{:S(2)}) copy-start(f32[128,1024]{1,0:T(8,128)} %get-tuple-element.26.dr_hbm) | copy-start | bytes 1572868
  71.8 1.7 %copy-start.4 = (bf16[4,10,128,256]{3,2,1,0:T(8,128)(2,1)S(1)}, bf16[4,10,128,256]{3,2,1,0:T(8,128)(2,1)}, u32[]{:S(2)}) copy-start(bf16[4,10,128,256]{3,2,1,0:T(8,128)(2,1)} %get-tuple-element.23.du_hbm) | copy-start | bytes 7864324
  73.5 1.3 %copy-start.5 = (bf16[4,10,128,128]{3,2,1,0:T(8,128)(2,1)S(1)}, bf16[4,10,128,128]{3,2,1,0:T(8,128)(2,1)}, u32[]{:S(2)}) copy-start(bf16[4,10,128,128]{3,2,1,0:T(8,128)(2,1)} %get-tuple-element.22.m_hbm) | copy-start | bytes 3932164
  74.9 1.0 %copy-start.6 = (f32[128,1024]{1,0:T(8,128)S(1)}, f32[128,1024]{1,0:T(8,128)}, u32[]{:S(2)}) copy-start(f32[128,1024]{1,0:T(8,128)} %get-tuple-element.25.nrm_hbm) | copy-start | bytes 1572868
  75.9 0.9 copy-start.7
  76.9 0.8 copy-start.8

commit v3 on v2

--- a/solution.py
+++ b/solution.py
@@ -450,7 +450,7 @@
                         pltpu.VMEM((T, H), F32), pltpu.VMEM((T, H), F32),
                         pltpu.VMEM((NB2, 256, H), F32), pltpu.VMEM((NB1, H, 512), F32), pltpu.VMEM((H, T), BF),
                         pltpu.SemaphoreType.DMA((5,)), pltpu.SemaphoreType.DMA((NB2,)), pltpu.SemaphoreType.DMA((NB1,))],
-        compiler_params=pltpu.CompilerParams(vmem_limit_bytes=40 * 1024 * 1024),
+        compiler_params=pltpu.CompilerParams(vmem_limit_bytes=VLIM),
         cost_estimate=pl.CostEstimate(flops=4 * 10 ** 9, bytes_accessed=66 << 20, transcendentals=0),
     )(m, du, d, nrm, dr, db1, x, gam, beta, dy)
 

time: 101 us -> 96.3 us (0.953)
  local copies, waits for them, and re-layouts: 6.88 us -> 0 us
  Pallas kernels: 90 us -> 92.1 us
    unnamed x20 -> x0, local copies, waits for them, and re-layouts: 6.88 us -> none
    pallas_call x1, Pallas kernels: 21.5 us -> 23.6 us  [grads_call(): pl.pallas_call(grads_kernel, out_shape=outs, name='grads', in_specs=[ANY]...]
  transfers between devices with their start and end apart: 1 -> 1, of which waited for: 0 -> 0; matrix products, arithmetic and copies ran while one was open for 0% -> 0% of each run, Pallas kernels for 21% -> 25%
where the time goes in v3:
time: 96.3 us; the launch traced here: 96.2 us
  Pallas kernels  92.1 us (96%)
  other arithmetic  1.93 us (2%)
  starting transfers between devices  1.49 us (2%)
    pallas_call x1, Pallas kernels, comm_call(): pl.pallas_call(comm_kernel, out_shape=outs, name='comm', in_specs=[VMEM,...  68.5 us
    pallas_call x1, Pallas kernels, grads_call(): pl.pallas_call(grads_kernel, out_shape=outs, name='grads', in_specs=[ANY]...  23.6 us
    convert_element_type x1, other arithmetic, device_step(): dx = (ALPHA * dr + (dxp.astype(F32) + dxr.astype(F32))).astype(BF)  1.93 us
  transfers between devices with their start and end apart: 1, of which 0 were waited for; matrix products, arithmetic and copies ran while one was open for 0% of the time, Pallas kernels for 25%

profile of v3, /device:TPU:0, one launch (start us, length us, event | category | flops | bytes accessed | tf_op | source)
XLA Modules:
  0.0 96.2 jit_solution(13942258874728716134)
XLA Ops:
  0.6 68.5 %comm.1 = (bf16[4,10,128,128]{3,2,1,0:T(8,128)(2,1)}, bf16[4,10,128,256]{3,2,1,0:T(8,128)(2,1)}, bf16[128,1024]{1,0:T(8,128)(2,1)}, f32[128,1024]{1,0:T(8,128)},...) custom-call(bf16[128,1024]{1,0:T(8,128)(2,1)} %x_ref.3, bf16[1024,10240]{1,0:T(8,128)(2,1)} %w1_ref.1, ...), custom_call_target="tpu_custom_call" | custom-call | flops 8000000000 | bytes 33554432 | tf_op jit(solution)/shard_map/comm/pallas_call | solution.py:377
  69.1 1.5 %collective-permute-start = (bf16[128,1024]{1,0:T(8,128)(2,1)}, bf16[128,1024]{1,0:T(8,128)(2,1)S(1)}, u32[]{:S(2)}, u32[]{:S(2)}) collective-permute-start(bf16[128,1024]{1,0:T(8,128)(2,1)} %get-tuple-element.29), channel_id=1, source_target_pairs={{0,4},{4,0},{1,5},{5,1},{2,6},{6,2},{3,7},{7,3}} | collective-permute-start | bytes 786440 | tf_op jit(solution)/shard_map/ppermute | solution.py:467
  70.6 23.6 %grads.1 = (f32[1024,10240]{1,0:T(8,128)}, f32[5120,1024]{1,0:T(8,128)}, bf16[128,1024]{1,0:T(8,128)(2,1)}, f32[1,10240]{1,0:T(1,128)}, f32[1,1024]{1,0:T(1,128)}, /*index=5*/f32[1,1024]{1,0:T(1,128)}, f32[1,1024]{1,0:T(1,128)}) custom-call(bf16[4,10,128,128]{3,2,1,0:T(8,128)(2,1)} %get-tuple-element.22.m_hbm, ...), custom_call_target="tpu_custom_call" | custom-call | flops 4000000000 | bytes 69206016 | tf_op jit(solution)/shard_map/grads/pallas_call | solution.py:446
  94.2 0.0 collective-permute-done
  94.2 1.9 %add_convert_fusion = bf16[128,1024]{1,0:T(8,128)(2,1)} fusion(bf16[128,1024]{1,0:T(8,128)(2,1)S(1)} %collective-permute-done, bf16[128,1024]{1,0:T(8,128)(2,1)} %get-tuple-element.29, f32[128,1024]{1,0:T(8,128)} %get-tuple-element.26.dr_hbm), kind=kLoop, calls=%fused_computation | loop fusion | flops 786432 | bytes 1310720 | tf_op jit(solution)/shard_map/convert_element_type | solution.py:469
Async XLA Ops:
  69.1 25.1 %collective-permute-start = (bf16[128,1024]{1,0:T(8,128)(2,1)}, bf16[128,1024]{1,0:T(8,128)(2,1)S(1)}, u32[]{:S(2)}, u32[]{:S(2)}) collective-permute-start(bf16[128,1024]{1,0:T(8,128)(2,1)} %get-tuple-element.29), channel_id=1, source_target_pairs={{0,4},{4,0},{1,5},{5,1},{2,6},{6,2},{3,7},{7,3}} | collective-permute-start | bytes 786440 | tf_op jit(solution)/shard_map/ppermute | solution.py:467

commit v4 on v3

--- a/solution.py
+++ b/solution.py
@@ -20,10 +20,12 @@
 NU = 10
 CH = ((0, 1), (1, 3), (3, 5), (5, 7), (7, 9), (9, 10))
 NC = len(CH)
-VLIM = 62 * 1024 * 1024
+COMM_LIM = 48 * 1024 * 1024
+GRADS_LIM = 28 * 1024 * 1024
 
 VMEM = pl.BlockSpec(memory_space=pltpu.VMEM)
 ANY = pl.BlockSpec(memory_space=pl.ANY)
+HBM = pl.BlockSpec(memory_space=pltpu.HBM)
 
 
 def sds(shape, dtype):
@@ -83,16 +85,14 @@
 SEM_NAMES = list(N_SEM)
 
 
-def comm_kernel(x_ref, w1_ref, b1_ref, w2_ref, b2_ref, gam_ref, dy_ref,
-                m_out, du_out, d_out, dr_out, nrm_out, db1_ref, dxp_ref,
-                w1b, w2b, ub, rb, xsb, xrb, facc, fs, fr, stb, dmb, dmr, dsum, dxr, m_ref, u_ref, dmf, du_ref,
-                d_ref, dr_ref, nrm_ref, acc,
-                ls1, ls2, os, *sem_list):
+def comm_kernel(x_hbm, w1_ref, b1_hbm, w2_ref, b2_hbm, gam_hbm, dy_hbm,
+                m_ref, du_ref, d_ref, dr_ref, nrm_ref, db1_ref, dxp_ref,
+                x_ref, b1_ref, b2_ref, gam_ref, dy_ref, w1b, w2b, ub, rb, xsb, xrb, facc, fs, fr, stb, dmb, dmr, dsum, dxr, u_ref, dmf, acc,
+                ls0, ls1, ls2, *sem_list):
     sems = {n: (sem_list[2 * i], sem_list[2 * i + 1]) for i, n in enumerate(SEM_NAMES)}
     h, y, c, sib, xn, xs = places()
     dev_sib, dev_x, dev_xs, dev_y = (0, y, sib), (0, y, xn), (0, y, xs), (0, 1 - y, h)
     order = [xs, xn, sib, h]
-    outs = []
 
     def w1_load(j, k):
         u0, u1 = CH[j]
@@ -104,11 +104,12 @@
         rows = slice(4 * 128 * CH[j][0], 4 * 128 * CH[j][1])
         return pltpu.make_async_copy(w2_ref.at[rows, :], w2b.at[rows, :], ls2.at[j])
 
-    def put(src, dst):
-        cp = pltpu.make_async_copy(src, dst, os.at[len(outs)])
-        cp.start()
-        outs.append(cp)
-
+    ins = [pltpu.make_async_copy(a, b, ls0.at[i]) for i, (a, b) in enumerate(
+        ((x_hbm, x_ref), (b1_hbm, b1_ref), (b2_hbm, b2_ref), (gam_hbm, gam_ref), (dy_hbm, dy_ref)))]
+    bar = pltpu.get_barrier_semaphore()
+    for dev in (dev_sib, dev_x, dev_xs, dev_y):
+        pl.semaphore_signal(bar, inc=1, device_id=dev, device_id_type=MESH)
+    ins[0].start()
     for j in range(NC + 1):
         for k in (0, 1):
             if j < NC:
@@ -116,10 +117,9 @@
         for k in (2, 3):
             if j > 0:
                 w1_load(j - 1, k).start()
-    bar = pltpu.get_barrier_semaphore()
-    for dev in (dev_sib, dev_x, dev_xs, dev_y):
-        pl.semaphore_signal(bar, inc=1, device_id=dev, device_id_type=MESH)
-    pl.semaphore_wait(bar, 4)
+    for cp in ins[1:]:
+        cp.start()
+    ins[0].wait()
 
     live = []
 
@@ -137,7 +137,10 @@
             r = dot(x_ref[...], w1b[k, :, u0 * 256:u1 * 256]).astype(BF)
             for i in range(u1 - u0):
                 ub[k, u0 + i] = r[:, i * 256:(i + 1) * 256]
-            if k == 0:
+            if j == 0 and k == 1:
+                pl.semaphore_wait(bar, 4)
+                c_ud[j, 1] = send(ub.at[0, us], rb.at[1, us], "ud", 2 * j + 1, dev_sib)
+            if j > 0 and k == 0:
                 c_ud[j, 1] = send(ub.at[0, us], rb.at[1, us], "ud", 2 * j + 1, dev_sib)
             if k == 2:
                 c_ud[j, 0] = send(ub.at[2, us], rb.at[0, us], "ud", 2 * j, dev_sib)
@@ -216,6 +219,7 @@
     uo(2)
     ux(4)
     s1(3)
+    ins[1].wait()
     s2(0)
     ux(5)
     s1(4)
@@ -237,7 +241,8 @@
         if j > 1:
             s4(j - 1)
     s4(NC - 1)
-    put(m_ref, m_out)
+    for cp in ins[2:]:
+        cp.wait()
 
     for n in range(2):
         cols = slice(n * 512, (n + 1) * 512)
@@ -277,9 +282,6 @@
     dr_ref[...] = dr
     d_ref[...] = dr.astype(BF)
     d_t = dr.T.astype(BF)
-    put(nrm_ref, nrm_out)
-    put(dr_ref, dr_out)
-    put(d_ref, d_out)
 
     c_dd, c_dx, c_df = {}, {}, {}
     mine, mine_k, theirs, theirs_k = (h, xn), (3, 1), (sib, xs), (2, 0)
@@ -328,11 +330,9 @@
         grads(j, mine, mine_k, j == 0)
 
     def grads_theirs(j):
-        us = slice(*CH[j])
         for i in range(2):
             c_df[j, i].wait_recv()
         grads(j, theirs, theirs_k, False)
-        put(du_ref.at[:, us], du_out.at[:, us])
 
     dm_part(0)
     dm_part(1)
@@ -348,36 +348,32 @@
         cp.wait_recv()
     for j in range(NC):
         grads_mine(j)
-        if j > 0:
-            grads_theirs(j - 1)
-    grads_theirs(NC - 1)
+        grads_theirs(j)
     dxp_ref[...] = acc[...].T.astype(BF)
     for cp in live:
         cp.wait_send()
-    for cp in outs:
-        cp.wait()
 
 
 def comm_call(x, w1, b1, w2, b2, gam, dy):
-    scratch = [pltpu.VMEM((4, H, NU * 256), BF), pltpu.VMEM((4 * NU * 128, H), BF),
+    scratch = [pltpu.VMEM((T, H), BF), pltpu.VMEM((4 * NU, 1, 256), F32), pltpu.VMEM((1, H), F32), pltpu.VMEM((1, H), F32),
+               pltpu.VMEM((T, H), BF),
+               pltpu.VMEM((4, H, NU * 256), BF), pltpu.VMEM((4 * NU * 128, H), BF),
                pltpu.VMEM((4, NU, T, 256), BF), pltpu.VMEM((2, NU, T, 256), BF),
                pltpu.VMEM((NU, T, 256), BF), pltpu.VMEM((NU, T, 256), BF),
                pltpu.VMEM((T, H), F32), pltpu.VMEM((2, T, 512), BF), pltpu.VMEM((2, T, 512), BF),
                pltpu.VMEM((4, 8, T), F32),
                pltpu.VMEM((4, NU, T, 128), BF), pltpu.VMEM((2, NU, T, 128), BF),
                pltpu.VMEM((2, NU, T, 128), BF), pltpu.VMEM((2, NU, T, 128), BF),
-               pltpu.VMEM((4, NU, T, 128), BF), pltpu.VMEM((4, NU, T, 256), BF), pltpu.VMEM((4, NU, T, 128), BF),
-               pltpu.VMEM((4, NU, T, 256), BF),
-               pltpu.VMEM((T, H), BF), pltpu.VMEM((T, H), F32), pltpu.VMEM((T, H), F32), pltpu.VMEM((H, T), F32),
-               pltpu.SemaphoreType.DMA((NC, 4)), pltpu.SemaphoreType.DMA((NC,)), pltpu.SemaphoreType.DMA((NC + 4,))]
+               pltpu.VMEM((4, NU, T, 256), BF), pltpu.VMEM((4, NU, T, 128), BF), pltpu.VMEM((H, T), F32),
+               pltpu.SemaphoreType.DMA((5,)), pltpu.SemaphoreType.DMA((NC, 4)), pltpu.SemaphoreType.DMA((NC,))]
     for n in SEM_NAMES:
         scratch += [pltpu.SemaphoreType.DMA((N_SEM[n],)), pltpu.SemaphoreType.DMA((N_SEM[n],))]
     outs = [sds((4, NU, T, 128), BF), sds((4, NU, T, 256), BF), sds((T, H), BF), sds((T, H), F32), sds((T, H), F32),
             sds((4 * NU, 1, 256), F32), sds((T, H), BF)]
     return pl.pallas_call(
         comm_kernel, out_shape=outs, name="comm",
-        in_specs=[VMEM, ANY, VMEM, ANY, VMEM, VMEM, VMEM], out_specs=[ANY] * 5 + [VMEM] * 2, scratch_shapes=scratch,
-        compiler_params=pltpu.CompilerParams(collective_id=0, has_side_effects=True, vmem_limit_bytes=VLIM),
+        in_specs=[HBM] * 7, out_specs=[VMEM] * 7, scratch_shapes=scratch,
+        compiler_params=pltpu.CompilerParams(collective_id=0, has_side_effects=True, vmem_limit_bytes=COMM_LIM),
         cost_estimate=pl.CostEstimate(flops=8 * 10 ** 9, bytes_accessed=32 << 20, transcendentals=0),
     )(x, w1, b1, w2, b2, gam, dy)
 
@@ -386,13 +382,9 @@
 NB1 = 6
 
 
-def grads_kernel(m_hbm, du_hbm, d_hbm, nrm_hbm, dr_hbm, db1_in, x_ref, gam_ref, beta_ref, dy_ref,
+def grads_kernel(m_ref, du_ref, d_ref, nrm_ref, dr_ref, db1_in, x_ref, gam_ref, beta_ref, dy_ref,
                  dw1_ref, dw2_ref, y_ref, db1_ref, db2_ref, dgam_ref, dbeta_ref,
-                 m_ref, du_ref, d_ref, nrm_ref, dr_ref, ob2, ob1, xt, ls, so2, so1):
-    loads = [pltpu.make_async_copy(a, b, ls.at[i]) for i, (a, b) in enumerate(
-        ((d_hbm, d_ref), (m_hbm, m_ref), (du_hbm, du_ref), (nrm_hbm, nrm_ref), (dr_hbm, dr_ref)))]
-    for cp in loads:
-        cp.start()
+                 ob2, ob1, xt, yb, db1b, so2, so1, so0):
     tiles = [(j, q) for j in range(NC) for q in range(4)]
 
     def put2(t):
@@ -407,35 +399,37 @@
         c0 = unit(j, q) * 256
         return pltpu.make_async_copy(ob1.at[t % NB1, :, :n * 256], dw1_ref.at[:, c0:c0 + n * 256], so1.at[t % NB1])
 
-    loads[0].wait()
-    loads[1].wait()
+    small = [pltpu.make_async_copy(yb, y_ref, so0.at[0]), pltpu.make_async_copy(db1b, db1_ref, so0.at[1])]
     for t, (j, q) in enumerate(tiles):
         if t >= NB2:
             put2(t - NB2).wait()
         for i, a in enumerate(range(*CH[j])):
             ob2[t % NB2, i * 128:(i + 1) * 128] = dot(m_ref[q, a].T, d_ref[...])
         put2(t).start()
-        if t == 0:
+        if t == 6:
             xt[...] = x_ref[...].T
-    loads[2].wait()
+        if t == 8:
+            yb[...] = (gam_ref[...] * nrm_ref[...] + beta_ref[...]).astype(BF)
+            for i in range(4 * NU):
+                db1b[:, i * 256:(i + 1) * 256] = db1_in[i]
+            for cp in small:
+                cp.start()
+        if t == 10:
+            dy = dy_ref[...].astype(F32)
+            db2_ref[...] = jnp.sum(dr_ref[...], axis=0, keepdims=True)
+            dgam_ref[...] = jnp.sum(dy * nrm_ref[...], axis=0, keepdims=True)
+            dbeta_ref[...] = jnp.sum(dy, axis=0, keepdims=True)
     for t, (j, q) in enumerate(tiles):
         if t >= NB1:
             put1(t - NB1).wait()
         for i, a in enumerate(range(*CH[j])):
             ob1[t % NB1, :, i * 256:(i + 1) * 256] = dot(xt[...], du_ref[q, a])
         put1(t).start()
-    loads[3].wait()
-    loads[4].wait()
-    dy = dy_ref[...].astype(F32)
-    y_ref[...] = (gam_ref[...] * nrm_ref[...] + beta_ref[...]).astype(BF)
-    db2_ref[...] = jnp.sum(dr_ref[...], axis=0, keepdims=True)
-    dgam_ref[...] = jnp.sum(dy * nrm_ref[...], axis=0, keepdims=True)
-    dbeta_ref[...] = jnp.sum(dy, axis=0, keepdims=True)
-    for i in range(4 * NU):
-        db1_ref[:, i * 256:(i + 1) * 256] = db1_in[i]
     last = len(tiles)
     for t in range(last - NB2, last):
         put2(t).wait()
+    for cp in small:
+        cp.wait()
     for t in range(last - NB1, last):
         put1(t).wait()
 
@@ -445,12 +439,11 @@
             sds((1, H), F32), sds((1, H), F32), sds((1, H), F32)]
     return pl.pallas_call(
         grads_kernel, out_shape=outs, name="grads",
-        in_specs=[ANY] * 5 + [VMEM] * 5, out_specs=[ANY, ANY] + [VMEM] * 5,
-        scratch_shapes=[pltpu.VMEM((4, NU, T, 128), BF), pltpu.VMEM((4, NU, T, 256), BF), pltpu.VMEM((T, H), BF),
-                        pltpu.VMEM((T, H), F32), pltpu.VMEM((T, H), F32),
-                        pltpu.VMEM((NB2, 256, H), F32), pltpu.VMEM((NB1, H, 512), F32), pltpu.VMEM((H, T), BF),
-                        pltpu.SemaphoreType.DMA((5,)), pltpu.SemaphoreType.DMA((NB2,)), pltpu.SemaphoreType.DMA((NB1,))],
-        compiler_params=pltpu.CompilerParams(vmem_limit_bytes=VLIM),
+        in_specs=[VMEM] * 10, out_specs=[HBM] * 4 + [VMEM] * 3,
+        scratch_shapes=[pltpu.VMEM((NB2, 256, H), F32), pltpu.VMEM((NB1, H, 512), F32), pltpu.VMEM((H, T), BF),
+                        pltpu.VMEM((T, H), BF), pltpu.VMEM((1, 4 * NU * 256), F32),
+                        pltpu.SemaphoreType.DMA((NB2,)), pltpu.SemaphoreType.DMA((NB1,)), pltpu.SemaphoreType.DMA((2,))],
+        compiler_params=pltpu.CompilerParams(vmem_limit_bytes=GRADS_LIM),
         cost_estimate=pl.CostEstimate(flops=4 * 10 ** 9, bytes_accessed=66 << 20, transcendentals=0),
     )(m, du, d, nrm, dr, db1, x, gam, beta, dy)
 
@@ -463,7 +456,8 @@
 
     def device_step(x, w1, b1, w2, b2, gam, beta, dy):
         b2, gam, beta = (a.reshape(1, H) for a in (b2, gam, beta))
-        m, du, d, dr, nrm, db1, dxp = comm_call(x, w1, b1.reshape(4 * NU, 1, 256), w2, b2, gam, dy)
+        hbm = [pltpu.with_memory_space_constraint(a, pltpu.HBM) for a in (x, w1, b1.reshape(4 * NU, 1, 256), w2, b2, gam, dy)]
+        m, du, d, dr, nrm, db1, dxp = comm_call(*hbm)
         dxr = lax.ppermute(dxp, 'ff', [(0, 1), (1, 0)])
         dw1, dw2, y, db1, db2, dgam, dbeta = grads_call(m, du, d, nrm, dr, db1, x, gam, beta, dy)
         dx = (ALPHA * dr + (dxp.astype(F32) + dxr.astype(F32))).astype(BF)

time: 96.3 us -> 96 us (level)
  other arithmetic: 1.93 us -> 0.82 us
    convert_element_type x1, other arithmetic: 1.93 us -> 0.82 us  [device_step(): dx = (ALPHA * dr + (dxp.astype(F32) + dxr.astype(F32))).astype(BF)]
  transfers between devices with their start and end apart: 1 -> 1, of which waited for: 0 -> 0; matrix products, arithmetic and copies ran while one was open for 0% -> 0% of each run, Pallas kernels for 25% -> 22%
where the time goes in v4:
time: 96 us; the launch traced here: 95.9 us
  Pallas kernels  92.9 us (97%)
  starting transfers between devices  1.54 us (2%)
    pallas_call x1, Pallas kernels, comm_call(): pl.pallas_call(comm_kernel, out_shape=outs, name='comm', in_specs=[HBM] *...  71.9 us
    pallas_call x1, Pallas kernels, grads_call(): pl.pallas_call(grads_kernel, out_shape=outs, name='grads', in_specs=[VMEM...  21 us
  transfers between devices with their start and end apart: 1, of which 0 were waited for; matrix products, arithmetic and copies ran while one was open for 0% of the time, Pallas kernels for 22%

profile of v4, /device:TPU:0, one launch (start us, length us, event | category | flops | bytes accessed | tf_op | source)
XLA Modules:
  0.0 95.9 jit_solution(9172171135667905397)
XLA Ops:
  0.6 0.0 copy-start.1
  0.6 0.0 copy-start
  0.7 0.0 copy-start.2
  0.7 0.0 copy-start.3
  0.7 71.9 %comm.1 = (bf16[4,10,128,128]{3,2,1,0:T(8,128)(2,1)S(1)}, bf16[4,10,128,256]{3,2,1,0:T(8,128)(2,1)S(1)}, bf16[128,1024]{1,0:T(8,128)(2,1)S(1)}, f32[128,1024]{1,...) custom-call(bf16[128,1024]{1,0:T(8,128)(2,1)} %x_ref.1, ...), custom_call_target="tpu_custom_call" | custom-call | flops 8000000000 | bytes 33554432 | tf_op jit(solution)/shard_map/comm/pallas_call | solution.py:373
  72.6 1.5 %collective-permute-start = (bf16[128,1024]{1,0:T(8,128)(2,1)S(1)}, bf16[128,1024]{1,0:T(8,128)(2,1)S(1)}, u32[]{:S(2)}, u32[]{:S(2)}) collective-permute-start(bf16[128,1024]{1,0:T(8,128)(2,1)S(1)} %get-tuple-element.29), channel_id=1, source_target_pairs={{0,4},{4,0},{1,5},{5,1},{2,6},{6,2},{3,7},{7,3}} | collective-permute-start | bytes 786440 | tf_op jit(solution)/shard_map/ppermute | solution.py:461
  74.1 0.0 copy-done.1
  74.1 0.0 copy-done
  74.1 0.0 copy-done.2
  74.1 0.0 copy-done.3
  74.1 21.0 %grads.1 = (f32[1024,10240]{1,0:T(8,128)}, f32[5120,1024]{1,0:T(8,128)}, bf16[128,1024]{1,0:T(8,128)(2,1)}, f32[1,10240]{1,0:T(1,128)}, f32[1,1024]{1,0:T(1,128)}, /*index=5*/f32[1,1024]{1,0:T(1,128)}, f32[1,1024]{1,0:T(1,128)}) custom-call(bf16[4,10,128,128]{3,2,1,0:T(8,128)(2,1)S(1)} %get-tuple-element.22.m_ref, ...), custom_call_target="tpu_custom_call" | custom-call | flops 4000000000 | bytes 69206016 | tf_op jit(solution)/shard_map/grads/pallas_call | solution.py:440
  95.1 0.0 collective-permute-done
  95.1 0.8 add_convert_fusion
Async XLA Ops:
  0.6 73.5 %copy-start.1 = (bf16[128,1024]{1,0:T(8,128)(2,1)S(1)}, bf16[128,1024]{1,0:T(8,128)(2,1)}, u32[]{:S(2)}) copy-start(bf16[128,1024]{1,0:T(8,128)(2,1)} %dy_ref.1) | copy-start | bytes 786436
  0.6 73.5 %copy-start = (bf16[128,1024]{1,0:T(8,128)(2,1)S(1)}, bf16[128,1024]{1,0:T(8,128)(2,1)}, u32[]{:S(2)}) copy-start(bf16[128,1024]{1,0:T(8,128)(2,1)} %x_ref.1) | copy-start | bytes 786436
  0.7 73.5 %copy-start.2 = (f32[1024]{0:T(1024)S(1)}, f32[1024]{0:T(1024)}, u32[]{:S(2)}) copy-start(f32[1024]{0:T(1024)} %param.13) | copy-start | bytes 12292
  0.7 73.4 %copy-start.3 = (f32[1024]{0:T(1024)S(1)}, f32[1024]{0:T(1024)}, u32[]{:S(2)}) copy-start(f32[1024]{0:T(1024)} %param.14) | copy-start | bytes 12292
  72.6 22.6 %collective-permute-start = (bf16[128,1024]{1,0:T(8,128)(2,1)S(1)}, bf16[128,1024]{1,0:T(8,128)(2,1)S(1)}, u32[]{:S(2)}, u32[]{:S(2)}) collective-permute-start(bf16[128,1024]{1,0:T(8,128)(2,1)S(1)} %get-tuple-element.29), channel_id=1, source_target_pairs={{0,4},{4,0},{1,5},{5,1},{2,6},{6,2},{3,7},{7,3}} | collective-permute-start | bytes 786440 | tf_op jit(solution)/shard_map/ppermute | solution.py:461

commit v5 on v4

--- a/solution.py
+++ b/solution.py
@@ -36,24 +36,12 @@
     return jnp.dot(a, b, preferred_element_type=F32)
 
 
-def gelu(g):
-    t = jnp.tanh(C0 * (g + C1 * (g * g * g)))
-    return g * (0.5 * (1.0 + t))
-
-
 def gelu_both(g):
     g2 = g * g
     t = jnp.tanh(C0 * (g + C1 * (g2 * g)))
     cdf = 0.5 * (1.0 + t)
     slope = cdf + (0.5 * g) * (1.0 - t * t) * (C0 * (1.0 + (3.0 * C1) * g2))
     return g * cdf, slope
-
-
-def grad_u(u, dm):
-    u = u.astype(F32)
-    v, g = u[:, :PAIR], u[:, PAIR:]
-    val, slope = gelu_both(g)
-    return jnp.concatenate([dm * val, dm * v * slope], axis=1)
 
 
 def places():
@@ -87,7 +75,7 @@
 
 def comm_kernel(x_hbm, w1_ref, b1_hbm, w2_ref, b2_hbm, gam_hbm, dy_hbm,
                 m_ref, du_ref, d_ref, dr_ref, nrm_ref, db1_ref, dxp_ref,
-                x_ref, b1_ref, b2_ref, gam_ref, dy_ref, w1b, w2b, ub, rb, xsb, xrb, facc, fs, fr, stb, dmb, dmr, dsum, dxr, u_ref, dmf, acc,
+                x_ref, b1_ref, b2_ref, gam_ref, dy_ref, w1b, w2b, ub, rb, xsb, xrb, fs, fr, stb, dmb, dmr, u_ref, dmf, pr_ref, acc,
                 ls0, ls1, ls2, *sem_list):
     sems = {n: (sem_list[2 * i], sem_list[2 * i + 1]) for i, n in enumerate(SEM_NAMES)}
     h, y, c, sib, xn, xs = places()
@@ -129,27 +117,22 @@
         live.append(cp)
         return cp
 
-    def u_part(j, ks):
-        u0, u1 = CH[j]
-        us = slice(u0, u1)
-        for k in ks:
+    def u_parts(*slabs):
+        for j, k in slabs:
             w1_load(j, k).wait()
+        for j, k in slabs:
+            u0, u1 = CH[j]
             r = dot(x_ref[...], w1b[k, :, u0 * 256:u1 * 256]).astype(BF)
             for i in range(u1 - u0):
                 ub[k, u0 + i] = r[:, i * 256:(i + 1) * 256]
-            if j == 0 and k == 1:
-                pl.semaphore_wait(bar, 4)
-                c_ud[j, 1] = send(ub.at[0, us], rb.at[1, us], "ud", 2 * j + 1, dev_sib)
-            if j > 0 and k == 0:
+        if slabs[0] == (0, 0):
+            pl.semaphore_wait(bar, 4)
+        for j, k in slabs:
+            us = slice(*CH[j])
+            if k == 0:
                 c_ud[j, 1] = send(ub.at[0, us], rb.at[1, us], "ud", 2 * j + 1, dev_sib)
             if k == 2:
                 c_ud[j, 0] = send(ub.at[2, us], rb.at[0, us], "ud", 2 * j, dev_sib)
-
-    def ux(j):
-        u_part(j, (0, 1))
-
-    def uo(j):
-        u_part(j, (2, 3))
 
     def s1(j):
         us = slice(*CH[j])
@@ -168,7 +151,10 @@
             u = u.astype(BF)
             u_ref[h, a] = u
             u = u.astype(F32)
-            m_ref[h, a] = (u[:, :PAIR] * gelu(u[:, PAIR:])).astype(BF)
+            val, slope = gelu_both(u[:, PAIR:])
+            m_ref[h, a] = (u[:, :PAIR] * val).astype(BF)
+            pr_ref[h, a, :, :PAIR] = val
+            pr_ref[h, a, :, PAIR:] = u[:, :PAIR] * slope
         c_mx[j] = send(m_ref.at[h, us], m_ref.at[h, us], "mx", j, dev_x)
         c_md[j] = send(m_ref.at[h, us], m_ref.at[h, us], "md", j, dev_sib)
 
@@ -187,9 +173,9 @@
             cols = slice(n * 512, (n + 1) * 512)
             part = dot(m, w2b[4 * 128 * u0:4 * 128 * u1, cols])
             if j > 0:
-                part = facc[:, cols] + part
+                part = nrm_ref[:, cols] + part
             if j < NC - 1:
-                facc[:, cols] = part
+                nrm_ref[:, cols] = part
             else:
                 fs[n] = part.astype(BF)
                 c_fy.append(send(fs.at[n], fr.at[n], "fy", n, dev_y))
@@ -203,31 +189,40 @@
         us = slice(*CH[j])
         c_gx[j].wait_recv()
         c_gf[j] = send(u_ref.at[xn, us], u_ref.at[xn, us], "gf", j, dev_sib)
+        products(j, xn)
+
+    def products(j, q):
+        for a in range(*CH[j]):
+            u = u_ref[q, a].astype(F32)
+            val, slope = gelu_both(u[:, PAIR:])
+            pr_ref[q, a, :, :PAIR] = val
+            pr_ref[q, a, :, PAIR:] = u[:, :PAIR] * slope
+
+    def products_sib(j):
+        c_gd[j].wait_recv()
+        c_gf[j].wait_recv()
+        products(j, sib)
+        products(j, xs)
 
     c_ud, c_ux, c_mx, c_md, c_mf, c_fy, c_gx, c_gd, c_gf = {}, {}, {}, {}, {}, [], {}, {}, {}
-    ux(0)
-    ux(1)
+    u_parts((0, 0), (0, 1))
+    u_parts((1, 0), (1, 1), (0, 2), (0, 3))
     s1(0)
-    uo(0)
-    ux(2)
+    u_parts((2, 0), (2, 1), (1, 2), (1, 3))
     s1(1)
-    uo(1)
-    ux(3)
+    u_parts((3, 0), (3, 1), (2, 2), (2, 3))
     s1(2)
     for j in range(NC):
         w2_load(j).start()
-    uo(2)
-    ux(4)
+    u_parts((4, 0), (4, 1), (3, 2), (3, 3))
     s1(3)
     ins[1].wait()
     s2(0)
-    ux(5)
+    u_parts((5, 0), (5, 1), (4, 2), (4, 3))
     s1(4)
-    uo(3)
+    u_parts((5, 2), (5, 3))
     s1(5)
-    uo(4)
     s2(1)
-    uo(5)
     s2(2)
     s2(3)
     s2(4)
@@ -244,6 +239,8 @@
     for cp in ins[2:]:
         cp.wait()
 
+    for j in range(3):
+        forward_u(j)
     for n in range(2):
         cols = slice(n * 512, (n + 1) * 512)
         c_fy[n].wait_recv()
@@ -260,6 +257,9 @@
     pack = jnp.where(lane == 0, m_loc, jnp.where(lane == 1, m2, jnp.where(lane == 2, sg, cg)))
     stb[h] = pack.T[0:8]
     c_st = [send(stb.at[h], stb.at[h], "st", i, dev) for i, dev in enumerate((dev_sib, dev_x, dev_xs))]
+    forward_u(3)
+    for j in range(3):
+        products_sib(j)
     for cp in c_st:
         cp.wait_recv()
     st = [stb[i] for i in range(4)]
@@ -293,22 +293,28 @@
             r = dot(w2b[aligned(unit(j, q), n, 128), :], d_t).T.astype(BF)
             for a in range(n):
                 dmb[i, u0 + a] = r[:, a * 128:(a + 1) * 128]
-            if i < 2:
-                c_dd[j, i] = send(dmb.at[i, u0:u1], dmr.at[i, u0:u1], "dd", 2 * j + i, dev_sib)
+            if i == 1:
+                for k in range(2):
+                    c_dd[j, k] = send(dmb.at[k, u0:u1], dmr.at[k, u0:u1], "dd", 2 * j + k, dev_sib)
 
     def dm_sum(j):
         us = slice(*CH[j])
+        c_ux[j].wait_send()
+        live[:] = [cp for cp in live if cp is not c_ux[j]]
         for i in range(2):
             c_dd[j, i].wait_recv()
-            dsum[i, us] = (dmb[2 + i, us].astype(F32) + dmr[i, us].astype(F32)).astype(BF)
-        c_dx[j] = send(dsum.at[:, us], dxr.at[:, us], "dx", j, dev_x)
+            xsb[us, :, i * 128:(i + 1) * 128] = (dmb[2 + i, us].astype(F32) + dmr[i, us].astype(F32)).astype(BF)
+        c_dx[j] = send(xsb.at[us], xrb.at[us], "dx", j, dev_x)
 
     def dm_full(j):
         us = slice(*CH[j])
         c_dx[j].wait_recv()
         for i in range(2):
             q = mine[i]
-            dmf[q, us] = (dsum[i, us].astype(F32) + dxr[1 - i, us].astype(F32)).astype(BF)
+            dmf[q, us] = (xsb[us, :, i * 128:(i + 1) * 128].astype(F32)
+                          + xrb[us, :, (1 - i) * 128:(2 - i) * 128].astype(F32)).astype(BF)
+        for i in range(2):
+            q = mine[i]
             c_df[j, i] = send(dmf.at[q, us], dmf.at[q, us], "df", 2 * j + i, dev_sib)
 
     def grads(j, qs, ks, first):
@@ -316,7 +322,8 @@
         for q, k in zip(qs, ks):
             parts = []
             for a in range(u0, u1):
-                du_f = grad_u(u_ref[q, a], dmf[q, a].astype(F32))
+                dm = dmf[q, a].astype(F32)
+                du_f = pr_ref[q, a] * jnp.concatenate([dm, dm], axis=1)
                 db1_ref[unit(j, q) + a - u0] = jnp.sum(du_f, axis=0, keepdims=True)
                 du_ref[q, a] = du_f.astype(BF)
                 parts.append(du_f)
@@ -337,18 +344,24 @@
     dm_part(0)
     dm_part(1)
     dm_sum(0)
-    for j in range(2, NC):
-        dm_part(j)
-        dm_sum(j - 1)
-        forward_u(j - 2)
-    dm_sum(NC - 1)
-    forward_u(NC - 2)
-    forward_u(NC - 1)
-    for cp in list(c_gd.values()) + list(c_gf.values()):
-        cp.wait_recv()
-    for j in range(NC):
+    dm_part(2)
+    dm_sum(1)
+    dm_part(3)
+    dm_sum(2)
+    forward_u(4)
+    dm_part(4)
+    dm_sum(3)
+    forward_u(5)
+    dm_part(5)
+    dm_sum(4)
+    dm_sum(5)
+    for j in range(3, NC):
+        products_sib(j)
+    grads_mine(0)
+    for j in range(1, NC):
+        grads_theirs(j - 1)
         grads_mine(j)
-        grads_theirs(j)
+    grads_theirs(NC - 1)
     dxp_ref[...] = acc[...].T.astype(BF)
     for cp in live:
         cp.wait_send()
@@ -360,11 +373,11 @@
                pltpu.VMEM((4, H, NU * 256), BF), pltpu.VMEM((4 * NU * 128, H), BF),
                pltpu.VMEM((4, NU, T, 256), BF), pltpu.VMEM((2, NU, T, 256), BF),
                pltpu.VMEM((NU, T, 256), BF), pltpu.VMEM((NU, T, 256), BF),
-               pltpu.VMEM((T, H), F32), pltpu.VMEM((2, T, 512), BF), pltpu.VMEM((2, T, 512), BF),
+               pltpu.VMEM((2, T, 512), BF), pltpu.VMEM((2, T, 512), BF),
                pltpu.VMEM((4, 8, T), F32),
                pltpu.VMEM((4, NU, T, 128), BF), pltpu.VMEM((2, NU, T, 128), BF),
-               pltpu.VMEM((2, NU, T, 128), BF), pltpu.VMEM((2, NU, T, 128), BF),
-               pltpu.VMEM((4, NU, T, 256), BF), pltpu.VMEM((4, NU, T, 128), BF), pltpu.VMEM((H, T), F32),
+               pltpu.VMEM((4, NU, T, 256), BF), pltpu.VMEM((4, NU, T, 128), BF), pltpu.VMEM((4, NU, T, 256), F32),
+               pltpu.VMEM((H, T), F32),
                pltpu.SemaphoreType.DMA((5,)), pltpu.SemaphoreType.DMA((NC, 4)), pltpu.SemaphoreType.DMA((NC,))]
     for n in SEM_NAMES:
         scratch += [pltpu.SemaphoreType.DMA((N_SEM[n],)), pltpu.SemaphoreType.DMA((N_SEM[n],))]

time: 96 us -> 94 us (0.979)
  Pallas kernels: 92.9 us -> 90.6 us
    pallas_call x1, Pallas kernels: 71.9 us -> 69.6 us  [comm_call(): pl.pallas_call(comm_kernel, out_shape=outs, name='comm', in_specs=[HBM] *...]
where the time goes in v5:
time: 94 us; the launch traced here: 93.9 us
  Pallas kernels  90.6 us (96%)
  starting transfers between devices  1.82 us (2%)
    pallas_call x1, Pallas kernels, comm_call(): pl.pallas_call(comm_kernel, out_shape=outs, name='comm', in_specs=[HBM] *...  69.6 us
    pallas_call x1, Pallas kernels, grads_call(): pl.pallas_call(grads_kernel, out_shape=outs, name='grads', in_specs=[VMEM...  21 us
  transfers between devices with their start and end apart: 1, of which 0 were waited for; matrix products, arithmetic and copies ran while one was open for 0% of the time, Pallas kernels for 22%

profile of v5, /device:TPU:0, one launch (start us, length us, event | category | flops | bytes accessed | tf_op | source)
XLA Modules:
  0.0 93.9 jit_solution(2256974016089152901)
XLA Ops:
  0.6 0.0 copy-start.1
  0.6 0.0 copy-start
  0.7 0.0 copy-start.2
  0.7 0.0 copy-start.3
  0.7 69.6 %comm.1 = (bf16[4,10,128,128]{3,2,1,0:T(8,128)(2,1)S(1)}, bf16[4,10,128,256]{3,2,1,0:T(8,128)(2,1)S(1)}, bf16[128,1024]{1,0:T(8,128)(2,1)S(1)}, f32[128,1024]{1,...) custom-call(bf16[128,1024]{1,0:T(8,128)(2,1)} %x_ref.1, ...), custom_call_target="tpu_custom_call" | custom-call | flops 8000000000 | bytes 33554432 | tf_op jit(solution)/shard_map/comm/pallas_call | solution.py:386
  70.3 1.8 %collective-permute-start = (bf16[128,1024]{1,0:T(8,128)(2,1)S(1)}, bf16[128,1024]{1,0:T(8,128)(2,1)S(1)}, u32[]{:S(2)}, u32[]{:S(2)}) collective-permute-start(bf16[128,1024]{1,0:T(8,128)(2,1)S(1)} %get-tuple-element.29), channel_id=1, source_target_pairs={{0,4},{4,0},{1,5},{5,1},{2,6},{6,2},{3,7},{7,3}} | collective-permute-start | bytes 786440 | tf_op jit(solution)/shard_map/ppermute | solution.py:474
  72.1 0.0 copy-done.1
  72.1 0.0 copy-done
  72.1 0.0 copy-done.2
  72.1 0.0 copy-done.3
  72.1 21.0 %grads.1 = (f32[1024,10240]{1,0:T(8,128)}, f32[5120,1024]{1,0:T(8,128)}, bf16[128,1024]{1,0:T(8,128)(2,1)}, f32[1,10240]{1,0:T(1,128)}, f32[1,1024]{1,0:T(1,128)}, /*index=5*/f32[1,1024]{1,0:T(1,128)}, f32[1,1024]{1,0:T(1,128)}) custom-call(bf16[4,10,128,128]{3,2,1,0:T(8,128)(2,1)S(1)} %get-tuple-element.22.m_ref, ...), custom_call_target="tpu_custom_call" | custom-call | flops 4000000000 | bytes 69206016 | tf_op jit(solution)/shard_map/grads/pallas_call | solution.py:453
  93.1 0.0 collective-permute-done
  93.1 0.8 add_convert_fusion
Async XLA Ops:
  0.6 71.5 %copy-start.1 = (bf16[128,1024]{1,0:T(8,128)(2,1)S(1)}, bf16[128,1024]{1,0:T(8,128)(2,1)}, u32[]{:S(2)}) copy-start(bf16[128,1024]{1,0:T(8,128)(2,1)} %dy_ref.1) | copy-start | bytes 786436
  0.6 71.4 %copy-start = (bf16[128,1024]{1,0:T(8,128)(2,1)S(1)}, bf16[128,1024]{1,0:T(8,128)(2,1)}, u32[]{:S(2)}) copy-start(bf16[128,1024]{1,0:T(8,128)(2,1)} %x_ref.1) | copy-start | bytes 786436
  0.7 71.4 %copy-start.2 = (f32[1024]{0:T(1024)S(1)}, f32[1024]{0:T(1024)}, u32[]{:S(2)}) copy-start(f32[1024]{0:T(1024)} %param.13) | copy-start | bytes 12292
  0.7 71.4 %copy-start.3 = (f32[1024]{0:T(1024)S(1)}, f32[1024]{0:T(1024)}, u32[]{:S(2)}) copy-start(f32[1024]{0:T(1024)} %param.14) | copy-start | bytes 12292
  70.3 22.8 %collective-permute-start = (bf16[128,1024]{1,0:T(8,128)(2,1)S(1)}, bf16[128,1024]{1,0:T(8,128)(2,1)S(1)}, u32[]{:S(2)}, u32[]{:S(2)}) collective-permute-start(bf16[128,1024]{1,0:T(8,128)(2,1)S(1)} %get-tuple-element.29), channel_id=1, source_target_pairs={{0,4},{4,0},{1,5},{5,1},{2,6},{6,2},{3,7},{7,3}} | collective-permute-start | bytes 786440 | tf_op jit(solution)/shard_map/ppermute | solution.py:474

commit v6 on v5

--- a/solution.py
+++ b/solution.py
@@ -98,15 +98,18 @@
     for dev in (dev_sib, dev_x, dev_xs, dev_y):
         pl.semaphore_signal(bar, inc=1, device_id=dev, device_id_type=MESH)
     ins[0].start()
+    load_order = []
     for j in range(NC + 1):
-        for k in (0, 1):
-            if j < NC:
-                w1_load(j, k).start()
-        for k in (2, 3):
-            if j > 0:
-                w1_load(j - 1, k).start()
-    for cp in ins[1:]:
-        cp.start()
+        load_order += [(j, k) for k in (0, 1) if j < NC] + [(j - 1, k) for k in (2, 3) if j > 0]
+    for j, k in load_order[:6]:
+        w1_load(j, k).start()
+    loaded = [6]
+
+    def load_more(n):
+        for j, k in load_order[loaded[0]:loaded[0] + n]:
+            w1_load(j, k).start()
+        loaded[0] += n
+
     ins[0].wait()
 
     live = []
@@ -120,6 +123,7 @@
     def u_parts(*slabs):
         for j, k in slabs:
             w1_load(j, k).wait()
+        load_more(4)
         for j, k in slabs:
             u0, u1 = CH[j]
             r = dot(x_ref[...], w1b[k, :, u0 * 256:u1 * 256]).astype(BF)
@@ -127,6 +131,8 @@
                 ub[k, u0 + i] = r[:, i * 256:(i + 1) * 256]
         if slabs[0] == (0, 0):
             pl.semaphore_wait(bar, 4)
+            for cp in ins[1:]:
+                cp.start()
         for j, k in slabs:
             us = slice(*CH[j])
             if k == 0:

time: 94 us -> 90 us (0.957)
  Pallas kernels: 90.6 us -> 86.6 us
    pallas_call x1, Pallas kernels: 69.6 us -> 65.6 us  [comm_call(): pl.pallas_call(comm_kernel, out_shape=outs, name='comm', in_specs=[HBM] *...]
  transfers between devices with their start and end apart: 1 -> 1, of which waited for: 0 -> 0; matrix products, arithmetic and copies ran while one was open for 0% -> 0% of each run, Pallas kernels for 22% -> 23%
where the time goes in v6:
time: 90 us; the launch traced here: 89.9 us
  Pallas kernels  86.6 us (96%)
  starting transfers between devices  1.77 us (2%)
    pallas_call x1, Pallas kernels, comm_call(): pl.pallas_call(comm_kernel, out_shape=outs, name='comm', in_specs=[HBM] *...  65.6 us
    pallas_call x1, Pallas kernels, grads_call(): pl.pallas_call(grads_kernel, out_shape=outs, name='grads', in_specs=[VMEM...  21 us
  transfers between devices with their start and end apart: 1, of which 0 were waited for; matrix products, arithmetic and copies ran while one was open for 0% of the time, Pallas kernels for 23%

profile of v6, /device:TPU:0, one launch (start us, length us, event | category | flops | bytes accessed | tf_op | source)
XLA Modules:
  0.0 89.9 jit_solution(5834782142663685095)
XLA Ops:
  0.6 0.0 copy-start.1
  0.6 0.0 copy-start
  0.7 0.0 copy-start.2
  0.7 0.0 copy-start.3
  0.7 65.6 %comm.1 = (bf16[4,10,128,128]{3,2,1,0:T(8,128)(2,1)S(1)}, bf16[4,10,128,256]{3,2,1,0:T(8,128)(2,1)S(1)}, bf16[128,1024]{1,0:T(8,128)(2,1)S(1)}, f32[128,1024]{1,...) custom-call(bf16[128,1024]{1,0:T(8,128)(2,1)} %x_ref.1, ...), custom_call_target="tpu_custom_call" | custom-call | flops 8000000000 | bytes 33554432 | tf_op jit(solution)/shard_map/comm/pallas_call | solution.py:392
  66.3 1.8 %collective-permute-start = (bf16[128,1024]{1,0:T(8,128)(2,1)S(1)}, bf16[128,1024]{1,0:T(8,128)(2,1)S(1)}, u32[]{:S(2)}, u32[]{:S(2)}) collective-permute-start(bf16[128,1024]{1,0:T(8,128)(2,1)S(1)} %get-tuple-element.29), channel_id=1, source_target_pairs={{0,4},{4,0},{1,5},{5,1},{2,6},{6,2},{3,7},{7,3}} | collective-permute-start | bytes 786440 | tf_op jit(solution)/shard_map/ppermute | solution.py:480
  68.1 0.0 copy-done.1
  68.1 0.0 copy-done
  68.1 0.0 copy-done.2
  68.1 0.0 copy-done.3
  68.1 21.0 %grads.1 = (f32[1024,10240]{1,0:T(8,128)}, f32[5120,1024]{1,0:T(8,128)}, bf16[128,1024]{1,0:T(8,128)(2,1)}, f32[1,10240]{1,0:T(1,128)}, f32[1,1024]{1,0:T(1,128)}, /*index=5*/f32[1,1024]{1,0:T(1,128)}, f32[1,1024]{1,0:T(1,128)}) custom-call(bf16[4,10,128,128]{3,2,1,0:T(8,128)(2,1)S(1)} %get-tuple-element.22.m_ref, ...), custom_call_target="tpu_custom_call" | custom-call | flops 4000000000 | bytes 69206016 | tf_op jit(solution)/shard_map/grads/pallas_call | solution.py:459
  89.1 0.0 collective-permute-done
  89.1 0.8 add_convert_fusion
Async XLA Ops:
  0.6 67.4 %copy-start.1 = (bf16[128,1024]{1,0:T(8,128)(2,1)S(1)}, bf16[128,1024]{1,0:T(8,128)(2,1)}, u32[]{:S(2)}) copy-start(bf16[128,1024]{1,0:T(8,128)(2,1)} %dy_ref.1) | copy-start | bytes 786436
  0.6 67.4 %copy-start = (bf16[128,1024]{1,0:T(8,128)(2,1)S(1)}, bf16[128,1024]{1,0:T(8,128)(2,1)}, u32[]{:S(2)}) copy-start(bf16[128,1024]{1,0:T(8,128)(2,1)} %x_ref.1) | copy-start | bytes 786436
  0.7 67.4 %copy-start.2 = (f32[1024]{0:T(1024)S(1)}, f32[1024]{0:T(1024)}, u32[]{:S(2)}) copy-start(f32[1024]{0:T(1024)} %param.13) | copy-start | bytes 12292
  0.7 67.4 %copy-start.3 = (f32[1024]{0:T(1024)S(1)}, f32[1024]{0:T(1024)}, u32[]{:S(2)}) copy-start(f32[1024]{0:T(1024)} %param.14) | copy-start | bytes 12292
  66.3 22.8 %collective-permute-start = (bf16[128,1024]{1,0:T(8,128)(2,1)S(1)}, bf16[128,1024]{1,0:T(8,128)(2,1)S(1)}, u32[]{:S(2)}, u32[]{:S(2)}) collective-permute-start(bf16[128,1024]{1,0:T(8,128)(2,1)S(1)} %get-tuple-element.29), channel_id=1, source_target_pairs={{0,4},{4,0},{1,5},{5,1},{2,6},{6,2},{3,7},{7,3}} | collective-permute-start | bytes 786440 | tf_op jit(solution)/shard_map/ppermute | solution.py:480

commit v7 on v6

--- a/solution.py
+++ b/solution.py
@@ -68,29 +68,35 @@
     return pl.ds(pl.multiple_of(start * tile, tile), size * tile)
 
 
-N_SEM = {"ud": 2 * NC, "ux": NC, "mx": NC, "md": NC, "mf": NC, "gx": NC, "gd": NC, "gf": NC, "fy": 2, "st": 3,
-         "dd": 2 * NC, "dx": NC, "df": 2 * NC}
+GCH = ((0, 3), (3, 7), (7, 10))
+NG = len(GCH)
+NLS = 16
+N_SEM = {"ud": 2 * NC, "ux": NC, "mx": NC, "md": 2 * NC, "gx": NG, "gd": NG, "gf": NG, "fy": 2, "st": 3}
 SEM_NAMES = list(N_SEM)
 
 
 def comm_kernel(x_hbm, w1_ref, b1_hbm, w2_ref, b2_hbm, gam_hbm, dy_hbm,
                 m_ref, du_ref, d_ref, dr_ref, nrm_ref, db1_ref, dxp_ref,
                 x_ref, b1_ref, b2_ref, gam_ref, dy_ref, w1b, w2b, ub, rb, xsb, xrb, fs, fr, stb, dmb, dmr, u_ref, dmf, pr_ref, acc,
-                ls0, ls1, ls2, *sem_list):
+                ls0, ls1, *sem_list):
     sems = {n: (sem_list[2 * i], sem_list[2 * i + 1]) for i, n in enumerate(SEM_NAMES)}
     h, y, c, sib, xn, xs = places()
     dev_sib, dev_x, dev_xs, dev_y = (0, y, sib), (0, y, xn), (0, y, xs), (0, 1 - y, h)
     order = [xs, xn, sib, h]
 
+    load_order = []
+    for j in range(NC + 1):
+        load_order += [(j, k) for k in (0, 1) if j < NC] + [(j - 1, k) for k in (2, 3) if j > 0]
+
     def w1_load(j, k):
         u0, u1 = CH[j]
         n = u1 - u0
         return pltpu.make_async_copy(w1_ref.at[:, aligned(unit(j, order[k]), n, 256)], w1b.at[k, :, u0 * 256:u1 * 256],
-                                     ls1.at[j, k])
+                                     ls1.at[load_order.index((j, k)) % NLS])
 
     def w2_load(j):
         rows = slice(4 * 128 * CH[j][0], 4 * 128 * CH[j][1])
-        return pltpu.make_async_copy(w2_ref.at[rows, :], w2b.at[rows, :], ls2.at[j])
+        return pltpu.make_async_copy(w2_ref.at[rows, :], w2b.at[rows, :], ls1.at[(4 * NC + j) % NLS])
 
     ins = [pltpu.make_async_copy(a, b, ls0.at[i]) for i, (a, b) in enumerate(
         ((x_hbm, x_ref), (b1_hbm, b1_ref), (b2_hbm, b2_ref), (gam_hbm, gam_ref), (dy_hbm, dy_ref)))]
@@ -98,9 +104,6 @@
     for dev in (dev_sib, dev_x, dev_xs, dev_y):
         pl.semaphore_signal(bar, inc=1, device_id=dev, device_id_type=MESH)
     ins[0].start()
-    load_order = []
-    for j in range(NC + 1):
-        load_order += [(j, k) for k in (0, 1) if j < NC] + [(j - 1, k) for k in (2, 3) if j > 0]
     for j, k in load_order[:6]:
         w1_load(j, k).start()
     loaded = [6]
@@ -119,6 +122,11 @@
         cp.start()
         live.append(cp)
         return cp
+
+    def sent(*cps):
+        for cp in cps:
+            cp.wait_send()
+        live[:] = [cp for cp in live if not any(cp is old for old in cps)]
 
     def u_parts(*slabs):
         for j, k in slabs:
@@ -162,12 +170,12 @@
             pr_ref[h, a, :, :PAIR] = val
             pr_ref[h, a, :, PAIR:] = u[:, :PAIR] * slope
         c_mx[j] = send(m_ref.at[h, us], m_ref.at[h, us], "mx", j, dev_x)
-        c_md[j] = send(m_ref.at[h, us], m_ref.at[h, us], "md", j, dev_sib)
+        c_md[j] = send(m_ref.at[h, us], m_ref.at[h, us], "md", 2 * j, dev_sib)
 
     def s3(j):
         us = slice(*CH[j])
         c_mx[j].wait_recv()
-        c_mf[j] = send(m_ref.at[xn, us], m_ref.at[xn, us], "mf", j, dev_sib)
+        c_mf[j] = send(m_ref.at[xn, us], m_ref.at[xn, us], "md", 2 * j + 1, dev_sib)
 
     def s4(j):
         u0, u1 = CH[j]
@@ -187,18 +195,18 @@
                 c_fy.append(send(fs.at[n], fr.at[n], "fy", n, dev_y))
 
     def gather_u(j):
-        us = slice(*CH[j])
+        us = slice(*GCH[j])
         c_gx[j] = send(u_ref.at[h, us], u_ref.at[h, us], "gx", j, dev_x)
         c_gd[j] = send(u_ref.at[h, us], u_ref.at[h, us], "gd", j, dev_sib)
 
     def forward_u(j):
-        us = slice(*CH[j])
+        us = slice(*GCH[j])
         c_gx[j].wait_recv()
         c_gf[j] = send(u_ref.at[xn, us], u_ref.at[xn, us], "gf", j, dev_sib)
         products(j, xn)
 
     def products(j, q):
-        for a in range(*CH[j]):
+        for a in range(*GCH[j]):
             u = u_ref[q, a].astype(F32)
             val, slope = gelu_both(u[:, PAIR:])
             pr_ref[q, a, :, :PAIR] = val
@@ -235,7 +243,7 @@
     s3(0)
     s4(0)
     s2(5)
-    for j in range(NC):
+    for j in range(NG):
         gather_u(j)
     for j in range(1, NC):
         s3(j)
@@ -245,8 +253,7 @@
     for cp in ins[2:]:
         cp.wait()
 
-    for j in range(3):
-        forward_u(j)
+    forward_u(0)
     for n in range(2):
         cols = slice(n * 512, (n + 1) * 512)
         c_fy[n].wait_recv()
@@ -263,9 +270,8 @@
     pack = jnp.where(lane == 0, m_loc, jnp.where(lane == 1, m2, jnp.where(lane == 2, sg, cg)))
     stb[h] = pack.T[0:8]
     c_st = [send(stb.at[h], stb.at[h], "st", i, dev) for i, dev in enumerate((dev_sib, dev_x, dev_xs))]
-    forward_u(3)
-    for j in range(3):
-        products_sib(j)
+    forward_u(1)
+    products_sib(0)
     for cp in c_st:
         cp.wait_recv()
     st = [stb[i] for i in range(4)]
@@ -296,32 +302,33 @@
         u0, u1 = CH[j]
         n = u1 - u0
         for i, q in enumerate(theirs + mine):
-            r = dot(w2b[aligned(unit(j, q), n, 128), :], d_t).T.astype(BF)
+            r = dot(w2b[aligned(unit(j, q), n, 128), :], d_t).astype(BF).T
             for a in range(n):
                 dmb[i, u0 + a] = r[:, a * 128:(a + 1) * 128]
             if i == 1:
+                sent(c_ud[j, 0], c_ud[j, 1])
                 for k in range(2):
-                    c_dd[j, k] = send(dmb.at[k, u0:u1], dmr.at[k, u0:u1], "dd", 2 * j + k, dev_sib)
+                    c_dd[j, k] = send(dmb.at[k, u0:u1], dmr.at[k, u0:u1], "ud", 2 * j + k, dev_sib)
 
     def dm_sum(j):
         us = slice(*CH[j])
-        c_ux[j].wait_send()
-        live[:] = [cp for cp in live if cp is not c_ux[j]]
+        sent(c_ux[j])
         for i in range(2):
             c_dd[j, i].wait_recv()
             xsb[us, :, i * 128:(i + 1) * 128] = (dmb[2 + i, us].astype(F32) + dmr[i, us].astype(F32)).astype(BF)
-        c_dx[j] = send(xsb.at[us], xrb.at[us], "dx", j, dev_x)
+        c_dx[j] = send(xsb.at[us], xrb.at[us], "ux", j, dev_x)
 
     def dm_full(j):
         us = slice(*CH[j])
         c_dx[j].wait_recv()
+        sent(c_md[j], c_mf[j])
         for i in range(2):
             q = mine[i]
             dmf[q, us] = (xsb[us, :, i * 128:(i + 1) * 128].astype(F32)
                           + xrb[us, :, (1 - i) * 128:(2 - i) * 128].astype(F32)).astype(BF)
         for i in range(2):
             q = mine[i]
-            c_df[j, i] = send(dmf.at[q, us], dmf.at[q, us], "df", 2 * j + i, dev_sib)
+            c_df[j, i] = send(dmf.at[q, us], dmf.at[q, us], "md", 2 * j + i, dev_sib)
 
     def grads(j, qs, ks, first):
         u0, u1 = CH[j]
@@ -331,9 +338,10 @@
                 dm = dmf[q, a].astype(F32)
                 du_f = pr_ref[q, a] * jnp.concatenate([dm, dm], axis=1)
                 db1_ref[unit(j, q) + a - u0] = jnp.sum(du_f, axis=0, keepdims=True)
-                du_ref[q, a] = du_f.astype(BF)
-                parts.append(du_f)
-            du_t = jnp.concatenate(parts, axis=1).T.astype(BF)
+                du = du_f.astype(BF)
+                du_ref[q, a] = du
+                parts.append(du)
+            du_t = jnp.concatenate(parts, axis=1).T
             part = dot(w1b[k, :, u0 * 256:u1 * 256], du_t)
             acc[...] = part if first else acc[...] + part
             first = False
@@ -354,15 +362,14 @@
     dm_sum(1)
     dm_part(3)
     dm_sum(2)
-    forward_u(4)
+    products_sib(1)
     dm_part(4)
     dm_sum(3)
-    forward_u(5)
+    forward_u(2)
     dm_part(5)
     dm_sum(4)
     dm_sum(5)
-    for j in range(3, NC):
-        products_sib(j)
+    products_sib(2)
     grads_mine(0)
     for j in range(1, NC):
         grads_theirs(j - 1)
@@ -384,7 +391,7 @@
                pltpu.VMEM((4, NU, T, 128), BF), pltpu.VMEM((2, NU, T, 128), BF),
                pltpu.VMEM((4, NU, T, 256), BF), pltpu.VMEM((4, NU, T, 128), BF), pltpu.VMEM((4, NU, T, 256), F32),
                pltpu.VMEM((H, T), F32),
-               pltpu.SemaphoreType.DMA((5,)), pltpu.SemaphoreType.DMA((NC, 4)), pltpu.SemaphoreType.DMA((NC,))]
+               pltpu.SemaphoreType.DMA((5,)), pltpu.SemaphoreType.DMA((NLS,))]
     for n in SEM_NAMES:
         scratch += [pltpu.SemaphoreType.DMA((N_SEM[n],)), pltpu.SemaphoreType.DMA((N_SEM[n],))]
     outs = [sds((4, NU, T, 128), BF), sds((4, NU, T, 256), BF), sds((T, H), BF), sds((T, H), F32), sds((T, H), F32),
@@ -403,7 +410,7 @@
 
 def grads_kernel(m_ref, du_ref, d_ref, nrm_ref, dr_ref, db1_in, x_ref, gam_ref, beta_ref, dy_ref,
                  dw1_ref, dw2_ref, y_ref, db1_ref, db2_ref, dgam_ref, dbeta_ref,
-                 ob2, ob1, xt, yb, db1b, so2, so1, so0):
+                 ob2, ob1, xt, yb, db1b, sb, so2, so1, so0):
     tiles = [(j, q) for j in range(NC) for q in range(4)]
 
     def put2(t):
@@ -418,7 +425,8 @@
         c0 = unit(j, q) * 256
         return pltpu.make_async_copy(ob1.at[t % NB1, :, :n * 256], dw1_ref.at[:, c0:c0 + n * 256], so1.at[t % NB1])
 
-    small = [pltpu.make_async_copy(yb, y_ref, so0.at[0]), pltpu.make_async_copy(db1b, db1_ref, so0.at[1])]
+    small = [pltpu.make_async_copy(a, b, so0.at[i]) for i, (a, b) in enumerate(
+        ((yb, y_ref), (db1b, db1_ref), (sb.at[0], db2_ref), (sb.at[1], dgam_ref), (sb.at[2], dbeta_ref)))]
     for t, (j, q) in enumerate(tiles):
         if t >= NB2:
             put2(t - NB2).wait()
@@ -431,13 +439,15 @@
             yb[...] = (gam_ref[...] * nrm_ref[...] + beta_ref[...]).astype(BF)
             for i in range(4 * NU):
                 db1b[:, i * 256:(i + 1) * 256] = db1_in[i]
-            for cp in small:
+            for cp in small[:2]:
                 cp.start()
         if t == 10:
             dy = dy_ref[...].astype(F32)
-            db2_ref[...] = jnp.sum(dr_ref[...], axis=0, keepdims=True)
-            dgam_ref[...] = jnp.sum(dy * nrm_ref[...], axis=0, keepdims=True)
-            dbeta_ref[...] = jnp.sum(dy, axis=0, keepdims=True)
+            sb[0] = jnp.sum(dr_ref[...], axis=0, keepdims=True)
+            sb[1] = jnp.sum(dy * nrm_ref[...], axis=0, keepdims=True)
+            sb[2] = jnp.sum(dy, axis=0, keepdims=True)
+            for cp in small[2:]:
+                cp.start()
     for t, (j, q) in enumerate(tiles):
         if t >= NB1:
             put1(t - NB1).wait()
@@ -458,10 +468,10 @@
             sds((1, H), F32), sds((1, H), F32), sds((1, H), F32)]
     return pl.pallas_call(
         grads_kernel, out_shape=outs, name="grads",
-        in_specs=[VMEM] * 10, out_specs=[HBM] * 4 + [VMEM] * 3,
+        in_specs=[VMEM] * 10, out_specs=[HBM] * 7,
         scratch_shapes=[pltpu.VMEM((NB2, 256, H), F32), pltpu.VMEM((NB1, H, 512), F32), pltpu.VMEM((H, T), BF),
-                        pltpu.VMEM((T, H), BF), pltpu.VMEM((1, 4 * NU * 256), F32),
-                        pltpu.SemaphoreType.DMA((NB2,)), pltpu.SemaphoreType.DMA((NB1,)), pltpu.SemaphoreType.DMA((2,))],
+                        pltpu.VMEM((T, H), BF), pltpu.VMEM((1, 4 * NU * 256), F32), pltpu.VMEM((3, 1, H), F32),
+                        pltpu.SemaphoreType.DMA((NB2,)), pltpu.SemaphoreType.DMA((NB1,)), pltpu.SemaphoreType.DMA((5,))],
         compiler_params=pltpu.CompilerParams(vmem_limit_bytes=GRADS_LIM),
         cost_estimate=pl.CostEstimate(flops=4 * 10 ** 9, bytes_accessed=66 << 20, transcendentals=0),
     )(m, du, d, nrm, dr, db1, x, gam, beta, dy)

time: 90 us -> 88.4 us (0.982)
  Pallas kernels: 86.6 us -> 84.3 us
    pallas_call x1, Pallas kernels: 65.6 us -> 63.9 us  [comm_call(): pl.pallas_call(comm_kernel, out_shape=outs, name='comm', in_specs=[HBM] *...]
where the time goes in v7:
time: 88.4 us; the launch traced here: 88.3 us
  Pallas kernels  84.3 us (95%)
  starting transfers between devices  2.42 us (3%)
    pallas_call x1, Pallas kernels, comm_call(): pl.pallas_call(comm_kernel, out_shape=outs, name='comm', in_specs=[HBM] *...  63.9 us
    pallas_call x1, Pallas kernels, grads_call(): pl.pallas_call(grads_kernel, out_shape=outs, name='grads', in_specs=[VMEM...  20.4 us
    ppermute x1, starting transfers between devices, device_step(): dxr = lax.ppermute(dxp, 'ff', [(0, 1), (1, 0)])  2.42 us
  transfers between devices with their start and end apart: 1, of which 0 were waited for; matrix products, arithmetic and copies ran while one was open for 0% of the time, Pallas kernels for 23%

profile of v7, /device:TPU:0, one launch (start us, length us, event | category | flops | bytes accessed | tf_op | source)
XLA Modules:
  0.0 88.3 jit_solution(4929332263456975393)
XLA Ops:
  0.6 0.0 copy-start.1
  0.6 0.0 copy-start
  0.7 0.0 copy-start.2
  0.7 0.0 copy-start.3
  0.7 63.9 %comm.1 = (bf16[4,10,128,128]{3,2,1,0:T(8,128)(2,1)S(1)}, bf16[4,10,128,256]{3,2,1,0:T(8,128)(2,1)S(1)}, bf16[128,1024]{1,0:T(8,128)(2,1)S(1)}, f32[128,1024]{1,...) custom-call(bf16[128,1024]{1,0:T(8,128)(2,1)} %x_ref.1, ...), custom_call_target="tpu_custom_call" | custom-call | flops 8000000000 | bytes 33554432 | tf_op jit(solution)/shard_map/comm/pallas_call | solution.py:399
  64.6 2.4 %collective-permute-start = (bf16[128,1024]{1,0:T(8,128)(2,1)S(1)}, bf16[128,1024]{1,0:T(8,128)(2,1)S(1)}, u32[]{:S(2)}, u32[]{:S(2)}) collective-permute-start(bf16[128,1024]{1,0:T(8,128)(2,1)S(1)} %get-tuple-element.29), channel_id=1, source_target_pairs={{0,4},{4,0},{1,5},{5,1},{2,6},{6,2},{3,7},{7,3}} | collective-permute-start | bytes 786440 | tf_op jit(solution)/shard_map/ppermute | solution.py:490
  67.0 0.0 copy-done.1
  67.0 0.0 copy-done
  67.0 0.0 copy-done.2
  67.1 0.0 copy-done.3
  67.1 20.4 %grads.1 = (f32[1024,10240]{1,0:T(8,128)}, f32[5120,1024]{1,0:T(8,128)}, bf16[128,1024]{1,0:T(8,128)(2,1)}, f32[1,10240]{1,0:T(1,128)}, f32[1,1024]{1,0:T(1,128)}, /*index=5*/f32[1,1024]{1,0:T(1,128)}, f32[1,1024]{1,0:T(1,128)}) custom-call(bf16[4,10,128,128]{3,2,1,0:T(8,128)(2,1)S(1)} %get-tuple-element.22.m_ref, ...), custom_call_target="tpu_custom_call" | custom-call | flops 4000000000 | bytes 69206016 | tf_op jit(solution)/shard_map/grads/pallas_call | solution.py:469
  87.4 0.0 collective-permute-done
  87.4 0.8 add_convert_fusion
Async XLA Ops:
  0.6 66.4 %copy-start.1 = (bf16[128,1024]{1,0:T(8,128)(2,1)S(1)}, bf16[128,1024]{1,0:T(8,128)(2,1)}, u32[]{:S(2)}) copy-start(bf16[128,1024]{1,0:T(8,128)(2,1)} %dy_ref.1) | copy-start | bytes 786436
  0.6 66.4 %copy-start = (bf16[128,1024]{1,0:T(8,128)(2,1)S(1)}, bf16[128,1024]{1,0:T(8,128)(2,1)}, u32[]{:S(2)}) copy-start(bf16[128,1024]{1,0:T(8,128)(2,1)} %x_ref.1) | copy-start | bytes 786436
  0.7 66.4 %copy-start.2 = (f32[1024]{0:T(1024)S(1)}, f32[1024]{0:T(1024)}, u32[]{:S(2)}) copy-start(f32[1024]{0:T(1024)} %param.13) | copy-start | bytes 12292
  0.7 66.4 %copy-start.3 = (f32[1024]{0:T(1024)S(1)}, f32[1024]{0:T(1024)}, u32[]{:S(2)}) copy-start(f32[1024]{0:T(1024)} %param.14) | copy-start | bytes 12292
  64.6 22.8 %collective-permute-start = (bf16[128,1024]{1,0:T(8,128)(2,1)S(1)}, bf16[128,1024]{1,0:T(8,128)(2,1)S(1)}, u32[]{:S(2)}, u32[]{:S(2)}) collective-permute-start(bf16[128,1024]{1,0:T(8,128)(2,1)S(1)} %get-tuple-element.29), channel_id=1, source_target_pairs={{0,4},{4,0},{1,5},{5,1},{2,6},{6,2},{3,7},{7,3}} | collective-permute-start | bytes 786440 | tf_op jit(solution)/shard_map/ppermute | solution.py:490

commit v8 on v7

--- a/solution.py
+++ b/solution.py
@@ -332,7 +332,9 @@
 
     def grads(j, qs, ks, first):
         u0, u1 = CH[j]
-        for q, k in zip(qs, ks):
+        total = None
+        dus = []
+        for q in qs:
             parts = []
             for a in range(u0, u1):
                 dm = dmf[q, a].astype(F32)
@@ -341,10 +343,11 @@
                 du = du_f.astype(BF)
                 du_ref[q, a] = du
                 parts.append(du)
-            du_t = jnp.concatenate(parts, axis=1).T
+            dus.append(jnp.concatenate(parts, axis=1).T)
+        for du_t, k in zip(dus, ks):
             part = dot(w1b[k, :, u0 * 256:u1 * 256], du_t)
-            acc[...] = part if first else acc[...] + part
-            first = False
+            total = part if total is None else total + part
+        acc[...] = total if first else acc[...] + total
 
     def grads_mine(j):
         dm_full(j)

time: 88.4 us -> 88.3 us (level)
  no operation moved by 1% of the time
where the time goes in v8:
time: 88.3 us; the launch traced here: 88.2 us
  Pallas kernels  84.3 us (95%)
  starting transfers between devices  2.39 us (3%)
    pallas_call x1, Pallas kernels, comm_call(): pl.pallas_call(comm_kernel, out_shape=outs, name='comm', in_specs=[HBM] *...  64 us
    pallas_call x1, Pallas kernels, grads_call(): pl.pallas_call(grads_kernel, out_shape=outs, name='grads', in_specs=[VMEM...  20.3 us
    ppermute x1, starting transfers between devices, device_step(): dxr = lax.ppermute(dxp, 'ff', [(0, 1), (1, 0)])  2.39 us
  transfers between devices with their start and end apart: 1, of which 0 were waited for; matrix products, arithmetic and copies ran while one was open for 0% of the time, Pallas kernels for 23%

profile of v8, /device:TPU:0, one launch (start us, length us, event | category | flops | bytes accessed | tf_op | source)
XLA Modules:
  0.0 88.2 jit_solution(3947858230356793557)
XLA Ops:
  0.6 0.0 copy-start.1
  0.6 0.0 copy-start
  0.7 0.0 copy-start.2
  0.7 0.0 copy-start.3
  0.7 64.0 %comm.1 = (bf16[4,10,128,128]{3,2,1,0:T(8,128)(2,1)S(1)}, bf16[4,10,128,256]{3,2,1,0:T(8,128)(2,1)S(1)}, bf16[128,1024]{1,0:T(8,128)(2,1)S(1)}, f32[128,1024]{1,...) custom-call(bf16[128,1024]{1,0:T(8,128)(2,1)} %x_ref.1, ...), custom_call_target="tpu_custom_call" | custom-call | flops 8000000000 | bytes 33554432 | tf_op jit(solution)/shard_map/comm/pallas_call | solution.py:402
  64.6 2.4 %collective-permute-start = (bf16[128,1024]{1,0:T(8,128)(2,1)S(1)}, bf16[128,1024]{1,0:T(8,128)(2,1)S(1)}, u32[]{:S(2)}, u32[]{:S(2)}) collective-permute-start(bf16[128,1024]{1,0:T(8,128)(2,1)S(1)} %get-tuple-element.29), channel_id=1, source_target_pairs={{0,4},{4,0},{1,5},{5,1},{2,6},{6,2},{3,7},{7,3}} | collective-permute-start | bytes 786440 | tf_op jit(solution)/shard_map/ppermute | solution.py:493
  67.0 0.0 copy-done.1
  67.0 0.0 copy-done
  67.0 0.0 copy-done.2
  67.1 0.0 copy-done.3
  67.1 20.3 %grads.1 = (f32[1024,10240]{1,0:T(8,128)}, f32[5120,1024]{1,0:T(8,128)}, bf16[128,1024]{1,0:T(8,128)(2,1)}, f32[1,10240]{1,0:T(1,128)}, f32[1,1024]{1,0:T(1,128)}, /*index=5*/f32[1,1024]{1,0:T(1,128)}, f32[1,1024]{1,0:T(1,128)}) custom-call(bf16[4,10,128,128]{3,2,1,0:T(8,128)(2,1)S(1)} %get-tuple-element.22.m_ref, ...), custom_call_target="tpu_custom_call" | custom-call | flops 4000000000 | bytes 69206016 | tf_op jit(solution)/shard_map/grads/pallas_call | solution.py:472
  87.4 0.0 collective-permute-done
  87.4 0.8 add_convert_fusion
Async XLA Ops:
  0.6 66.4 %copy-start.1 = (bf16[128,1024]{1,0:T(8,128)(2,1)S(1)}, bf16[128,1024]{1,0:T(8,128)(2,1)}, u32[]{:S(2)}) copy-start(bf16[128,1024]{1,0:T(8,128)(2,1)} %dy_ref.1) | copy-start | bytes 786436
  0.6 66.4 %copy-start = (bf16[128,1024]{1,0:T(8,128)(2,1)S(1)}, bf16[128,1024]{1,0:T(8,128)(2,1)}, u32[]{:S(2)}) copy-start(bf16[128,1024]{1,0:T(8,128)(2,1)} %x_ref.1) | copy-start | bytes 786436
  0.7 66.4 %copy-start.2 = (f32[1024]{0:T(1024)S(1)}, f32[1024]{0:T(1024)}, u32[]{:S(2)}) copy-start(f32[1024]{0:T(1024)} %param.13) | copy-start | bytes 12292
  0.7 66.4 %copy-start.3 = (f32[1024]{0:T(1024)S(1)}, f32[1024]{0:T(1024)}, u32[]{:S(2)}) copy-start(f32[1024]{0:T(1024)} %param.14) | copy-start | bytes 12292
  64.6 22.8 %collective-permute-start = (bf16[128,1024]{1,0:T(8,128)(2,1)S(1)}, bf16[128,1024]{1,0:T(8,128)(2,1)S(1)}, u32[]{:S(2)}, u32[]{:S(2)}) collective-permute-start(bf16[128,1024]{1,0:T(8,128)(2,1)S(1)} %get-tuple-element.29), channel_id=1, source_target_pairs={{0,4},{4,0},{1,5},{5,1},{2,6},{6,2},{3,7},{7,3}} | collective-permute-start | bytes 786440 | tf_op jit(solution)/shard_map/ppermute | solution.py:493

commit v9 on v8

--- a/solution.py
+++ b/solution.py
@@ -69,9 +69,10 @@
 
 
 GCH = ((0, 3), (3, 7), (7, 10))
+HT = T // 2
 NG = len(GCH)
 NLS = 16
-N_SEM = {"ud": 2 * NC, "ux": NC, "mx": NC, "md": 2 * NC, "gx": NG, "gd": NG, "gf": NG, "fy": 2, "st": 3}
+N_SEM = {"ud": 2 * NC, "ux": 2 * NC, "mx": 2 * NG, "md": 4 * NG, "gx": NG, "gd": NG, "gf": NG, "fy": 4, "st": 3}
 SEM_NAMES = list(N_SEM)
 
 
@@ -152,47 +153,62 @@
         us = slice(*CH[j])
         c_ud[j, 1].wait_recv()
         xsb[us] = (ub[1, us].astype(F32) + rb[1, us].astype(F32)).astype(BF)
-        c_ux[j] = send(xsb.at[us], xrb.at[us], "ux", j, dev_x)
-
-    def s2(j):
+        send_x(0, j)
+
+    def half(a):
+        return slice(a * HT, (a + 1) * HT)
+
+    def send_x(a, j):
+        us = slice(*CH[j])
+        c_ux[a, j] = send(xsb.at[us, half(a)], xrb.at[us, half(a)], "ux", a * NC + j, dev_x)
+
+    def s2(a, j):
+        rows = half(a)
         u0, u1 = CH[j]
-        us = slice(u0, u1)
-        c_ud[j, 0].wait_recv()
-        c_ux[j].wait_recv()
+        if a == 0:
+            c_ud[j, 0].wait_recv()
+        c_ux[a, j].wait_recv()
         for i in range(u1 - u0):
-            a = u0 + i
-            u = ub[3, a].astype(F32) + rb[0, a].astype(F32) + xrb[a].astype(F32) + b1_ref[unit(j, h) + i]
+            n = u0 + i
+            u = (ub[3, n, rows].astype(F32) + rb[0, n, rows].astype(F32) + xrb[n, rows].astype(F32)
+                 + b1_ref[unit(j, h) + i])
             u = u.astype(BF)
-            u_ref[h, a] = u
+            u_ref[h, n, rows] = u
             u = u.astype(F32)
             val, slope = gelu_both(u[:, PAIR:])
-            m_ref[h, a] = (u[:, :PAIR] * val).astype(BF)
-            pr_ref[h, a, :, :PAIR] = val
-            pr_ref[h, a, :, PAIR:] = u[:, :PAIR] * slope
-        c_mx[j] = send(m_ref.at[h, us], m_ref.at[h, us], "mx", j, dev_x)
-        c_md[j] = send(m_ref.at[h, us], m_ref.at[h, us], "md", 2 * j, dev_sib)
-
-    def s3(j):
-        us = slice(*CH[j])
-        c_mx[j].wait_recv()
-        c_mf[j] = send(m_ref.at[xn, us], m_ref.at[xn, us], "md", 2 * j + 1, dev_sib)
-
-    def s4(j):
-        u0, u1 = CH[j]
-        c_md[j].wait_recv()
-        c_mf[j].wait_recv()
-        w2_load(j).wait()
-        m = jnp.concatenate([m_ref[q, a] for q in range(4) for a in range(u0, u1)], axis=1)
+            m_ref[h, n, rows] = (u[:, :PAIR] * val).astype(BF)
+            pr_ref[h, n, rows, :PAIR] = val
+            pr_ref[h, n, rows, PAIR:] = u[:, :PAIR] * slope
+        if j % 2 == 1:
+            g = j // 2
+            part = m_ref.at[h, slice(*GCH[g]), rows]
+            c_mx[a, g] = send(part, part, "mx", a * NG + g, dev_x)
+            c_md[a, g] = send(part, part, "md", a * NG + g, dev_sib)
+
+    def s3(a, g):
+        c_mx[a, g].wait_recv()
+        part = m_ref.at[xn, slice(*GCH[g]), half(a)]
+        c_mf[a, g] = send(part, part, "md", (2 + a) * NG + g, dev_sib)
+
+    def s4(a, g):
+        rows = half(a)
+        c_md[a, g].wait_recv()
+        c_mf[a, g].wait_recv()
+        if a == 0:
+            for j in (2 * g, 2 * g + 1):
+                w2_load(j).wait()
+        m = jnp.concatenate([m_ref[q, n, rows] for j in (2 * g, 2 * g + 1) for q in range(4) for n in range(*CH[j])], axis=1)
+        u0, u1 = GCH[g]
         for n in range(2):
             cols = slice(n * 512, (n + 1) * 512)
             part = dot(m, w2b[4 * 128 * u0:4 * 128 * u1, cols])
-            if j > 0:
-                part = nrm_ref[:, cols] + part
-            if j < NC - 1:
-                nrm_ref[:, cols] = part
+            if g > 0:
+                part = nrm_ref[rows, cols] + part
+            if g < NG - 1:
+                nrm_ref[rows, cols] = part
             else:
-                fs[n] = part.astype(BF)
-                c_fy.append(send(fs.at[n], fr.at[n], "fy", n, dev_y))
+                fs[a, n] = part.astype(BF)
+                c_fy[a, n] = send(fs.at[a, n], fr.at[a, n], "fy", 2 * a + n, dev_y)
 
     def gather_u(j):
         us = slice(*GCH[j])
@@ -218,7 +234,7 @@
         products(j, sib)
         products(j, xs)
 
-    c_ud, c_ux, c_mx, c_md, c_mf, c_fy, c_gx, c_gd, c_gf = {}, {}, {}, {}, {}, [], {}, {}, {}
+    c_ud, c_ux, c_mx, c_md, c_mf, c_fy, c_gx, c_gd, c_gf = {}, {}, {}, {}, {}, {}, {}, {}, {}
     u_parts((0, 0), (0, 1))
     u_parts((1, 0), (1, 1), (0, 2), (0, 3))
     s1(0)
@@ -230,35 +246,36 @@
         w2_load(j).start()
     u_parts((4, 0), (4, 1), (3, 2), (3, 3))
     s1(3)
-    ins[1].wait()
-    s2(0)
     u_parts((5, 0), (5, 1), (4, 2), (4, 3))
     s1(4)
+    send_x(1, 0)
     u_parts((5, 2), (5, 3))
     s1(5)
-    s2(1)
-    s2(2)
-    s2(3)
-    s2(4)
-    s3(0)
-    s4(0)
-    s2(5)
-    for j in range(NG):
-        gather_u(j)
     for j in range(1, NC):
-        s3(j)
-        if j > 1:
-            s4(j - 1)
-    s4(NC - 1)
+        send_x(1, j)
+    ins[1].wait()
+    for a in range(2):
+        for j in range(NC):
+            s2(a, j)
+    for g in range(NG):
+        gather_u(g)
+    for a in range(2):
+        s3(a, 0)
+        s3(a, 1)
+        s4(a, 0)
+        s3(a, 2)
+        s4(a, 1)
+        s4(a, 2)
     for cp in ins[2:]:
         cp.wait()
 
     forward_u(0)
-    for n in range(2):
-        cols = slice(n * 512, (n + 1) * 512)
-        c_fy[n].wait_recv()
-        f = fs[n].astype(F32) + fr[n].astype(F32)
-        nrm_ref[:, cols] = ALPHA * x_ref[:, cols].astype(F32) + f + b2_ref[:, cols]
+    for a in range(2):
+        for n in range(2):
+            rows, cols = half(a), slice(n * 512, (n + 1) * 512)
+            c_fy[a, n].wait_recv()
+            f = fs[a, n].astype(F32) + fr[a, n].astype(F32)
+            nrm_ref[rows, cols] = ALPHA * x_ref[rows, cols].astype(F32) + f + b2_ref[:, cols]
     r = nrm_ref[...]
     gdy = dy_ref[...].astype(F32) * gam_ref[...]
     m_loc = jnp.sum(r, axis=1, keepdims=True) * (1.0 / H)
@@ -312,7 +329,7 @@
 
     def dm_sum(j):
         us = slice(*CH[j])
-        sent(c_ux[j])
+        sent(c_ux[0, j], c_ux[1, j])
         for i in range(2):
             c_dd[j, i].wait_recv()
             xsb[us, :, i * 128:(i + 1) * 128] = (dmb[2 + i, us].astype(F32) + dmr[i, us].astype(F32)).astype(BF)
@@ -321,7 +338,8 @@
     def dm_full(j):
         us = slice(*CH[j])
         c_dx[j].wait_recv()
-        sent(c_md[j], c_mf[j])
+        if j == 0:
+            sent(*c_md.values(), *c_mf.values())
         for i in range(2):
             q = mine[i]
             dmf[q, us] = (xsb[us, :, i * 128:(i + 1) * 128].astype(F32)
@@ -350,7 +368,6 @@
         acc[...] = total if first else acc[...] + total
 
     def grads_mine(j):
-        dm_full(j)
         grads(j, mine, mine_k, j == 0)
 
     def grads_theirs(j):
@@ -373,9 +390,14 @@
     dm_sum(4)
     dm_sum(5)
     products_sib(2)
+    dm_full(0)
     grads_mine(0)
     for j in range(1, NC):
+        if j == NC - 1:
+            dm_full(j)
         grads_theirs(j - 1)
+        if j < NC - 1:
+            dm_full(j)
         grads_mine(j)
     grads_theirs(NC - 1)
     dxp_ref[...] = acc[...].T.astype(BF)
@@ -389,7 +411,7 @@
                pltpu.VMEM((4, H, NU * 256), BF), pltpu.VMEM((4 * NU * 128, H), BF),
                pltpu.VMEM((4, NU, T, 256), BF), pltpu.VMEM((2, NU, T, 256), BF),
                pltpu.VMEM((NU, T, 256), BF), pltpu.VMEM((NU, T, 256), BF),
-               pltpu.VMEM((2, T, 512), BF), pltpu.VMEM((2, T, 512), BF),
+               pltpu.VMEM((2, 2, HT, 512), BF), pltpu.VMEM((2, 2, HT, 512), BF),
                pltpu.VMEM((4, 8, T), F32),
                pltpu.VMEM((4, NU, T, 128), BF), pltpu.VMEM((2, NU, T, 128), BF),
                pltpu.VMEM((4, NU, T, 256), BF), pltpu.VMEM((4, NU, T, 128), BF), pltpu.VMEM((4, NU, T, 256), F32),

time: 88.3 us -> 88.8 us (level)
  no operation moved by 1% of the time
where the time goes in v9:
time: 88.8 us; the launch traced here: 88.7 us
  Pallas kernels  84.8 us (95%)
  starting transfers between devices  2.4 us (3%)
    pallas_call x1, Pallas kernels, comm_call(): pl.pallas_call(comm_kernel, out_shape=outs, name='comm', in_specs=[HBM] *...  64.5 us
    pallas_call x1, Pallas kernels, grads_call(): pl.pallas_call(grads_kernel, out_shape=outs, name='grads', in_specs=[VMEM...  20.4 us
    ppermute x1, starting transfers between devices, device_step(): dxr = lax.ppermute(dxp, 'ff', [(0, 1), (1, 0)])  2.4 us
  transfers between devices with their start and end apart: 1, of which 0 were waited for; matrix products, arithmetic and copies ran while one was open for 0% of the time, Pallas kernels for 23%

profile of v9, /device:TPU:0, one launch (start us, length us, event | category | flops | bytes accessed | tf_op | source)
XLA Modules:
  0.0 88.7 jit_solution(184362207192896559)
XLA Ops:
  0.6 0.0 copy-start.1
  0.6 0.0 copy-start
  0.7 0.0 copy-start.2
  0.7 0.0 copy-start.3
  0.7 64.5 %comm.1 = (bf16[4,10,128,128]{3,2,1,0:T(8,128)(2,1)S(1)}, bf16[4,10,128,256]{3,2,1,0:T(8,128)(2,1)S(1)}, bf16[128,1024]{1,0:T(8,128)(2,1)S(1)}, f32[128,1024]{1,...) custom-call(bf16[128,1024]{1,0:T(8,128)(2,1)} %x_ref.1, ...), custom_call_target="tpu_custom_call" | custom-call | flops 8000000000 | bytes 33554432 | tf_op jit(solution)/shard_map/comm/pallas_call | solution.py:424
  65.1 2.4 %collective-permute-start = (bf16[128,1024]{1,0:T(8,128)(2,1)S(1)}, bf16[128,1024]{1,0:T(8,128)(2,1)S(1)}, u32[]{:S(2)}, u32[]{:S(2)}) collective-permute-start(bf16[128,1024]{1,0:T(8,128)(2,1)S(1)} %get-tuple-element.29), channel_id=1, source_target_pairs={{0,4},{4,0},{1,5},{5,1},{2,6},{6,2},{3,7},{7,3}} | collective-permute-start | bytes 786440 | tf_op jit(solution)/shard_map/ppermute | solution.py:515
  67.5 0.0 copy-done.1
  67.5 0.0 copy-done
  67.5 0.0 copy-done.2
  67.5 0.0 copy-done.3
  67.5 20.4 %grads.1 = (f32[1024,10240]{1,0:T(8,128)}, f32[5120,1024]{1,0:T(8,128)}, bf16[128,1024]{1,0:T(8,128)(2,1)}, f32[1,10240]{1,0:T(1,128)}, f32[1,1024]{1,0:T(1,128)}, /*index=5*/f32[1,1024]{1,0:T(1,128)}, f32[1,1024]{1,0:T(1,128)}) custom-call(bf16[4,10,128,128]{3,2,1,0:T(8,128)(2,1)S(1)} %get-tuple-element.22.m_ref, ...), custom_call_target="tpu_custom_call" | custom-call | flops 4000000000 | bytes 69206016 | tf_op jit(solution)/shard_map/grads/pallas_call | solution.py:494
  87.9 0.0 collective-permute-done
  87.9 0.8 add_convert_fusion
Async XLA Ops:
  0.6 66.9 %copy-start.1 = (bf16[128,1024]{1,0:T(8,128)(2,1)S(1)}, bf16[128,1024]{1,0:T(8,128)(2,1)}, u32[]{:S(2)}) copy-start(bf16[128,1024]{1,0:T(8,128)(2,1)} %dy_ref.1) | copy-start | bytes 786436
  0.6 66.9 %copy-start = (bf16[128,1024]{1,0:T(8,128)(2,1)S(1)}, bf16[128,1024]{1,0:T(8,128)(2,1)}, u32[]{:S(2)}) copy-start(bf16[128,1024]{1,0:T(8,128)(2,1)} %x_ref.1) | copy-start | bytes 786436
  0.7 66.9 %copy-start.2 = (f32[1024]{0:T(1024)S(1)}, f32[1024]{0:T(1024)}, u32[]{:S(2)}) copy-start(f32[1024]{0:T(1024)} %param.13) | copy-start | bytes 12292
  0.7 66.9 %copy-start.3 = (f32[1024]{0:T(1024)S(1)}, f32[1024]{0:T(1024)}, u32[]{:S(2)}) copy-start(f32[1024]{0:T(1024)} %param.14) | copy-start | bytes 12292
  65.1 22.8 %collective-permute-start = (bf16[128,1024]{1,0:T(8,128)(2,1)S(1)}, bf16[128,1024]{1,0:T(8,128)(2,1)S(1)}, u32[]{:S(2)}, u32[]{:S(2)}) collective-permute-start(bf16[128,1024]{1,0:T(8,128)(2,1)S(1)} %get-tuple-element.29), channel_id=1, source_target_pairs={{0,4},{4,0},{1,5},{5,1},{2,6},{6,2},{3,7},{7,3}} | collective-permute-start | bytes 786440 | tf_op jit(solution)/shard_map/ppermute | solution.py:515

commit v10 on v9

--- a/solution.py
+++ b/solution.py
@@ -240,18 +240,19 @@
     s1(0)
     u_parts((2, 0), (2, 1), (1, 2), (1, 3))
     s1(1)
+    send_x(1, 0)
     u_parts((3, 0), (3, 1), (2, 2), (2, 3))
     s1(2)
     for j in range(NC):
         w2_load(j).start()
     u_parts((4, 0), (4, 1), (3, 2), (3, 3))
     s1(3)
+    send_x(1, 1)
     u_parts((5, 0), (5, 1), (4, 2), (4, 3))
     s1(4)
-    send_x(1, 0)
     u_parts((5, 2), (5, 3))
     s1(5)
-    for j in range(1, NC):
+    for j in range(2, NC):
         send_x(1, j)
     ins[1].wait()
     for a in range(2):
@@ -287,7 +288,6 @@
     pack = jnp.where(lane == 0, m_loc, jnp.where(lane == 1, m2, jnp.where(lane == 2, sg, cg)))
     stb[h] = pack.T[0:8]
     c_st = [send(stb.at[h], stb.at[h], "st", i, dev) for i, dev in enumerate((dev_sib, dev_x, dev_xs))]
-    forward_u(1)
     products_sib(0)
     for cp in c_st:
         cp.wait_recv()
@@ -378,18 +378,18 @@
     dm_part(0)
     dm_part(1)
     dm_sum(0)
+    forward_u(1)
     dm_part(2)
     dm_sum(1)
+    products_sib(1)
     dm_part(3)
     dm_sum(2)
-    products_sib(1)
     dm_part(4)
     dm_sum(3)
     forward_u(2)
     dm_part(5)
     dm_sum(4)
     dm_sum(5)
-    products_sib(2)
     dm_full(0)
     grads_mine(0)
     for j in range(1, NC):
@@ -399,6 +399,8 @@
         if j < NC - 1:
             dm_full(j)
         grads_mine(j)
+        if j == 3:
+            products_sib(2)
     grads_theirs(NC - 1)
     dxp_ref[...] = acc[...].T.astype(BF)
     for cp in live:

time: 88.8 us -> 88.5 us (level)
  no operation moved by 1% of the time
where the time goes in v10:
time: 88.5 us; the launch traced here: 88.4 us
  Pallas kernels  84.9 us (96%)
  starting transfers between devices  1.95 us (2%)
    pallas_call x1, Pallas kernels, comm_call(): pl.pallas_call(comm_kernel, out_shape=outs, name='comm', in_specs=[HBM] *...  64.5 us
    pallas_call x1, Pallas kernels, grads_call(): pl.pallas_call(grads_kernel, out_shape=outs, name='grads', in_specs=[VMEM...  20.4 us
    ppermute x1, starting transfers between devices, device_step(): dxr = lax.ppermute(dxp, 'ff', [(0, 1), (1, 0)])  1.95 us
  transfers between devices with their start and end apart: 1, of which 0 were waited for; matrix products, arithmetic and copies ran while one was open for 0% of the time, Pallas kernels for 23%

profile of v10, /device:TPU:0, one launch (start us, length us, event | category | flops | bytes accessed | tf_op | source)
XLA Modules:
  0.0 88.4 jit_solution(18060162040586327313)
XLA Ops:
  0.6 0.0 copy-start.1
  0.6 0.0 copy-start
  0.7 0.0 copy-start.2
  0.7 0.0 copy-start.3
  0.7 64.5 %comm.1 = (bf16[4,10,128,128]{3,2,1,0:T(8,128)(2,1)S(1)}, bf16[4,10,128,256]{3,2,1,0:T(8,128)(2,1)S(1)}, bf16[128,1024]{1,0:T(8,128)(2,1)S(1)}, f32[128,1024]{1,...) custom-call(bf16[128,1024]{1,0:T(8,128)(2,1)} %x_ref.1, ...), custom_call_target="tpu_custom_call" | custom-call | flops 8000000000 | bytes 33554432 | tf_op jit(solution)/shard_map/comm/pallas_call | solution.py:426
  65.2 2.0 %collective-permute-start = (bf16[128,1024]{1,0:T(8,128)(2,1)S(1)}, bf16[128,1024]{1,0:T(8,128)(2,1)S(1)}, u32[]{:S(2)}, u32[]{:S(2)}) collective-permute-start(bf16[128,1024]{1,0:T(8,128)(2,1)S(1)} %get-tuple-element.29), channel_id=1, source_target_pairs={{0,4},{4,0},{1,5},{5,1},{2,6},{6,2},{3,7},{7,3}} | collective-permute-start | bytes 786440 | tf_op jit(solution)/shard_map/ppermute | solution.py:517
  67.2 0.0 copy-done.1
  67.2 0.0 copy-done
  67.2 0.0 copy-done.2
  67.2 0.0 copy-done.3
  67.2 20.4 %grads.1 = (f32[1024,10240]{1,0:T(8,128)}, f32[5120,1024]{1,0:T(8,128)}, bf16[128,1024]{1,0:T(8,128)(2,1)}, f32[1,10240]{1,0:T(1,128)}, f32[1,1024]{1,0:T(1,128)}, /*index=5*/f32[1,1024]{1,0:T(1,128)}, f32[1,1024]{1,0:T(1,128)}) custom-call(bf16[4,10,128,128]{3,2,1,0:T(8,128)(2,1)S(1)} %get-tuple-element.22.m_ref, ...), custom_call_target="tpu_custom_call" | custom-call | flops 4000000000 | bytes 69206016 | tf_op jit(solution)/shard_map/grads/pallas_call | solution.py:496
  87.5 0.0 collective-permute-done
  87.6 0.8 add_convert_fusion
Async XLA Ops:
  0.6 66.5 %copy-start.1 = (bf16[128,1024]{1,0:T(8,128)(2,1)S(1)}, bf16[128,1024]{1,0:T(8,128)(2,1)}, u32[]{:S(2)}) copy-start(bf16[128,1024]{1,0:T(8,128)(2,1)} %dy_ref.1) | copy-start | bytes 786436
  0.6 66.5 %copy-start = (bf16[128,1024]{1,0:T(8,128)(2,1)S(1)}, bf16[128,1024]{1,0:T(8,128)(2,1)}, u32[]{:S(2)}) copy-start(bf16[128,1024]{1,0:T(8,128)(2,1)} %x_ref.1) | copy-start | bytes 786436
  0.7 66.5 %copy-start.2 = (f32[1024]{0:T(1024)S(1)}, f32[1024]{0:T(1024)}, u32[]{:S(2)}) copy-start(f32[1024]{0:T(1024)} %param.13) | copy-start | bytes 12292
  0.7 66.5 %copy-start.3 = (f32[1024]{0:T(1024)S(1)}, f32[1024]{0:T(1024)}, u32[]{:S(2)}) copy-start(f32[1024]{0:T(1024)} %param.14) | copy-start | bytes 12292
  65.2 22.3 %collective-permute-start = (bf16[128,1024]{1,0:T(8,128)(2,1)S(1)}, bf16[128,1024]{1,0:T(8,128)(2,1)S(1)}, u32[]{:S(2)}, u32[]{:S(2)}) collective-permute-start(bf16[128,1024]{1,0:T(8,128)(2,1)S(1)} %get-tuple-element.29), channel_id=1, source_target_pairs={{0,4},{4,0},{1,5},{5,1},{2,6},{6,2},{3,7},{7,3}} | collective-permute-start | bytes 786440 | tf_op jit(solution)/shard_map/ppermute | solution.py:517

commit v11 on v10

--- a/solution.py
+++ b/solution.py
@@ -258,7 +258,7 @@
     for a in range(2):
         for j in range(NC):
             s2(a, j)
-    for g in range(NG):
+    for g in range(NG - 1):
         gather_u(g)
     for a in range(2):
         s3(a, 0)
@@ -288,6 +288,7 @@
     pack = jnp.where(lane == 0, m_loc, jnp.where(lane == 1, m2, jnp.where(lane == 2, sg, cg)))
     stb[h] = pack.T[0:8]
     c_st = [send(stb.at[h], stb.at[h], "st", i, dev) for i, dev in enumerate((dev_sib, dev_x, dev_xs))]
+    gather_u(NG - 1)
     products_sib(0)
     for cp in c_st:
         cp.wait_recv()

time: 88.5 us -> 85.3 us (0.964)
  Pallas kernels: 84.9 us -> 82 us
    pallas_call x1, Pallas kernels: 64.5 us -> 61.7 us  [comm_call(): pl.pallas_call(comm_kernel, out_shape=outs, name='comm', in_specs=[HBM] *...]
  transfers between devices with their start and end apart: 1 -> 1, of which waited for: 0 -> 0; matrix products, arithmetic and copies ran while one was open for 0% -> 0% of each run, Pallas kernels for 23% -> 24%
where the time goes in v11:
time: 85.3 us; the launch traced here: 85.2 us
  Pallas kernels  82 us (96%)
  starting transfers between devices  1.63 us (2%)
    pallas_call x1, Pallas kernels, comm_call(): pl.pallas_call(comm_kernel, out_shape=outs, name='comm', in_specs=[HBM] *...  61.7 us
    pallas_call x1, Pallas kernels, grads_call(): pl.pallas_call(grads_kernel, out_shape=outs, name='grads', in_specs=[VMEM...  20.4 us
  transfers between devices with their start and end apart: 1, of which 0 were waited for; matrix products, arithmetic and copies ran while one was open for 0% of the time, Pallas kernels for 24%

profile of v11, /device:TPU:0, one launch (start us, length us, event | category | flops | bytes accessed | tf_op | source)
XLA Modules:
  0.0 85.2 jit_solution(3929935757775828382)
XLA Ops:
  0.6 0.0 copy-start.1
  0.6 0.0 copy-start
  0.7 0.0 copy-start.2
  0.7 0.0 copy-start.3
  0.7 61.7 %comm.1 = (bf16[4,10,128,128]{3,2,1,0:T(8,128)(2,1)S(1)}, bf16[4,10,128,256]{3,2,1,0:T(8,128)(2,1)S(1)}, bf16[128,1024]{1,0:T(8,128)(2,1)S(1)}, f32[128,1024]{1,...) custom-call(bf16[128,1024]{1,0:T(8,128)(2,1)} %x_ref.1, ...), custom_call_target="tpu_custom_call" | custom-call | flops 8000000000 | bytes 33554432 | tf_op jit(solution)/shard_map/comm/pallas_call | solution.py:427
  62.3 1.6 %collective-permute-start = (bf16[128,1024]{1,0:T(8,128)(2,1)S(1)}, bf16[128,1024]{1,0:T(8,128)(2,1)S(1)}, u32[]{:S(2)}, u32[]{:S(2)}) collective-permute-start(bf16[128,1024]{1,0:T(8,128)(2,1)S(1)} %get-tuple-element.29), channel_id=1, source_target_pairs={{0,4},{4,0},{1,5},{5,1},{2,6},{6,2},{3,7},{7,3}} | collective-permute-start | bytes 786440 | tf_op jit(solution)/shard_map/ppermute | solution.py:518
  64.0 0.0 copy-done.1
  64.0 0.0 copy-done
  64.0 0.0 copy-done.2
  64.0 0.0 copy-done.3
  64.0 20.4 %grads.1 = (f32[1024,10240]{1,0:T(8,128)}, f32[5120,1024]{1,0:T(8,128)}, bf16[128,1024]{1,0:T(8,128)(2,1)}, f32[1,10240]{1,0:T(1,128)}, f32[1,1024]{1,0:T(1,128)}, /*index=5*/f32[1,1024]{1,0:T(1,128)}, f32[1,1024]{1,0:T(1,128)}) custom-call(bf16[4,10,128,128]{3,2,1,0:T(8,128)(2,1)S(1)} %get-tuple-element.22.m_ref, ...), custom_call_target="tpu_custom_call" | custom-call | flops 4000000000 | bytes 69206016 | tf_op jit(solution)/shard_map/grads/pallas_call | solution.py:497
  84.4 0.0 collective-permute-done
  84.4 0.8 add_convert_fusion
Async XLA Ops:
  0.6 63.3 %copy-start.1 = (bf16[128,1024]{1,0:T(8,128)(2,1)S(1)}, bf16[128,1024]{1,0:T(8,128)(2,1)}, u32[]{:S(2)}) copy-start(bf16[128,1024]{1,0:T(8,128)(2,1)} %dy_ref.1) | copy-start | bytes 786436
  0.6 63.3 %copy-start = (bf16[128,1024]{1,0:T(8,128)(2,1)S(1)}, bf16[128,1024]{1,0:T(8,128)(2,1)}, u32[]{:S(2)}) copy-start(bf16[128,1024]{1,0:T(8,128)(2,1)} %x_ref.1) | copy-start | bytes 786436
  0.7 63.3 %copy-start.2 = (f32[1024]{0:T(1024)S(1)}, f32[1024]{0:T(1024)}, u32[]{:S(2)}) copy-start(f32[1024]{0:T(1024)} %param.13) | copy-start | bytes 12292
  0.7 63.3 %copy-start.3 = (f32[1024]{0:T(1024)S(1)}, f32[1024]{0:T(1024)}, u32[]{:S(2)}) copy-start(f32[1024]{0:T(1024)} %param.14) | copy-start | bytes 12292
  62.3 22.0 %collective-permute-start = (bf16[128,1024]{1,0:T(8,128)(2,1)S(1)}, bf16[128,1024]{1,0:T(8,128)(2,1)S(1)}, u32[]{:S(2)}, u32[]{:S(2)}) collective-permute-start(bf16[128,1024]{1,0:T(8,128)(2,1)S(1)} %get-tuple-element.29), channel_id=1, source_target_pairs={{0,4},{4,0},{1,5},{5,1},{2,6},{6,2},{3,7},{7,3}} | collective-permute-start | bytes 786440 | tf_op jit(solution)/shard_map/ppermute | solution.py:518

commit v12 on v11

--- a/solution.py
+++ b/solution.py
@@ -270,22 +270,28 @@
     for cp in ins[2:]:
         cp.wait()
 
+    gdy = dy_ref[...].astype(F32) * gam_ref[...]
+    sg = jnp.sum(gdy, axis=1, keepdims=True)
+    dr_ref[...] = gdy
+    for n in range(2):
+        cols = slice(n * 512, (n + 1) * 512)
+        nrm_ref[:, cols] = ALPHA * x_ref[:, cols].astype(F32) + b2_ref[:, cols]
     forward_u(0)
+    lane = lax.broadcasted_iota(jnp.int32, (HT, 128), 1)
+    packs = []
     for a in range(2):
+        rows = half(a)
         for n in range(2):
-            rows, cols = half(a), slice(n * 512, (n + 1) * 512)
+            cols = slice(n * 512, (n + 1) * 512)
             c_fy[a, n].wait_recv()
-            f = fs[a, n].astype(F32) + fr[a, n].astype(F32)
-            nrm_ref[rows, cols] = ALPHA * x_ref[rows, cols].astype(F32) + f + b2_ref[:, cols]
-    r = nrm_ref[...]
-    gdy = dy_ref[...].astype(F32) * gam_ref[...]
-    m_loc = jnp.sum(r, axis=1, keepdims=True) * (1.0 / H)
-    cen = r - m_loc
-    m2 = jnp.sum(cen * cen, axis=1, keepdims=True)
-    sg = jnp.sum(gdy, axis=1, keepdims=True)
-    cg = jnp.sum(gdy * cen, axis=1, keepdims=True)
-    lane = lax.broadcasted_iota(jnp.int32, (T, 128), 1)
-    pack = jnp.where(lane == 0, m_loc, jnp.where(lane == 1, m2, jnp.where(lane == 2, sg, cg)))
+            nrm_ref[rows, cols] = nrm_ref[rows, cols] + (fs[a, n].astype(F32) + fr[a, n].astype(F32))
+        r = nrm_ref[rows, :]
+        m_loc = jnp.sum(r, axis=1, keepdims=True) * (1.0 / H)
+        cen = r - m_loc
+        m2 = jnp.sum(cen * cen, axis=1, keepdims=True)
+        cg = jnp.sum(dr_ref[rows, :] * cen, axis=1, keepdims=True)
+        packs.append(jnp.where(lane == 0, m_loc, jnp.where(lane == 1, m2, jnp.where(lane == 2, sg[rows], cg))))
+    pack = jnp.concatenate(packs, axis=0)
     stb[h] = pack.T[0:8]
     c_st = [send(stb.at[h], stb.at[h], "st", i, dev) for i, dev in enumerate((dev_sib, dev_x, dev_xs))]
     gather_u(NG - 1)
@@ -306,6 +312,8 @@
     rows = jnp.concatenate([mu, rho, sgt * (1.0 / (4 * H)), cgt * rho * (1.0 / (4 * H)), jnp.zeros((124, T), F32)], axis=0)
     colst = rows.T
     mu_c, rho_c, mg_c, mgr_c = (colst[:, i:i + 1] for i in range(4))
+    r = nrm_ref[...]
+    gdy = dr_ref[...]
     nrm = (r - mu_c) * rho_c
     dr = rho_c * (gdy - mg_c - nrm * mgr_c)
     nrm_ref[...] = nrm
@@ -432,8 +440,8 @@
     )(x, w1, b1, w2, b2, gam, dy)
 
 
-NB2 = 6
-NB1 = 6
+NB2 = 8
+NB1 = 8
 
 
 def grads_kernel(m_ref, du_ref, d_ref, nrm_ref, dr_ref, db1_in, x_ref, gam_ref, beta_ref, dy_ref,

time: 85.3 us -> 85.2 us (level)
  no operation moved by 1% of the time
where the time goes in v12:
time: 85.2 us; the launch traced here: 85.1 us
  Pallas kernels  81.9 us (96%)
  starting transfers between devices  1.58 us (2%)
    pallas_call x1, Pallas kernels, comm_call(): pl.pallas_call(comm_kernel, out_shape=outs, name='comm', in_specs=[HBM] *...  61.7 us
    pallas_call x1, Pallas kernels, grads_call(): pl.pallas_call(grads_kernel, out_shape=outs, name='grads', in_specs=[VMEM...  20.2 us
  transfers between devices with their start and end apart: 1, of which 0 were waited for; matrix products, arithmetic and copies ran while one was open for 0% of the time, Pallas kernels for 24%

profile of v12, /device:TPU:0, one launch (start us, length us, event | category | flops | bytes accessed | tf_op | source)
XLA Modules:
  0.0 85.1 jit_solution(13363923645508072153)
XLA Ops:
  0.6 0.0 copy-start.1
  0.6 0.0 copy-start
  0.7 0.0 copy-start.2
  0.7 0.0 copy-start.3
  0.7 61.7 %comm.1 = (bf16[4,10,128,128]{3,2,1,0:T(8,128)(2,1)S(1)}, bf16[4,10,128,256]{3,2,1,0:T(8,128)(2,1)S(1)}, bf16[128,1024]{1,0:T(8,128)(2,1)S(1)}, f32[128,1024]{1,...) custom-call(bf16[128,1024]{1,0:T(8,128)(2,1)} %x_ref.1, ...), custom_call_target="tpu_custom_call" | custom-call | flops 8000000000 | bytes 33554432 | tf_op jit(solution)/shard_map/comm/pallas_call | solution.py:435
  62.4 1.6 %collective-permute-start = (bf16[128,1024]{1,0:T(8,128)(2,1)S(1)}, bf16[128,1024]{1,0:T(8,128)(2,1)S(1)}, u32[]{:S(2)}, u32[]{:S(2)}) collective-permute-start(bf16[128,1024]{1,0:T(8,128)(2,1)S(1)} %get-tuple-element.29), channel_id=1, source_target_pairs={{0,4},{4,0},{1,5},{5,1},{2,6},{6,2},{3,7},{7,3}} | collective-permute-start | bytes 786440 | tf_op jit(solution)/shard_map/ppermute | solution.py:526
  64.0 0.0 copy-done.1
  64.0 0.0 copy-done
  64.0 0.0 copy-done.2
  64.0 0.0 copy-done.3
  64.0 20.2 %grads.1 = (f32[1024,10240]{1,0:T(8,128)}, f32[5120,1024]{1,0:T(8,128)}, bf16[128,1024]{1,0:T(8,128)(2,1)}, f32[1,10240]{1,0:T(1,128)}, f32[1,1024]{1,0:T(1,128)}, /*index=5*/f32[1,1024]{1,0:T(1,128)}, f32[1,1024]{1,0:T(1,128)}) custom-call(bf16[4,10,128,128]{3,2,1,0:T(8,128)(2,1)S(1)} %get-tuple-element.22.m_ref, ...), custom_call_target="tpu_custom_call" | custom-call | flops 4000000000 | bytes 69206016 | tf_op jit(solution)/shard_map/grads/pallas_call | solution.py:505
  84.2 0.0 collective-permute-done
  84.2 0.8 add_convert_fusion
Async XLA Ops:
  0.6 63.3 %copy-start.1 = (bf16[128,1024]{1,0:T(8,128)(2,1)S(1)}, bf16[128,1024]{1,0:T(8,128)(2,1)}, u32[]{:S(2)}) copy-start(bf16[128,1024]{1,0:T(8,128)(2,1)} %dy_ref.1) | copy-start | bytes 786436
  0.6 63.3 %copy-start = (bf16[128,1024]{1,0:T(8,128)(2,1)S(1)}, bf16[128,1024]{1,0:T(8,128)(2,1)}, u32[]{:S(2)}) copy-start(bf16[128,1024]{1,0:T(8,128)(2,1)} %x_ref.1) | copy-start | bytes 786436
  0.7 63.3 %copy-start.2 = (f32[1024]{0:T(1024)S(1)}, f32[1024]{0:T(1024)}, u32[]{:S(2)}) copy-start(f32[1024]{0:T(1024)} %param.13) | copy-start | bytes 12292
  0.7 63.3 %copy-start.3 = (f32[1024]{0:T(1024)S(1)}, f32[1024]{0:T(1024)}, u32[]{:S(2)}) copy-start(f32[1024]{0:T(1024)} %param.14) | copy-start | bytes 12292
  62.4 21.8 %collective-permute-start = (bf16[128,1024]{1,0:T(8,128)(2,1)S(1)}, bf16[128,1024]{1,0:T(8,128)(2,1)S(1)}, u32[]{:S(2)}, u32[]{:S(2)}) collective-permute-start(bf16[128,1024]{1,0:T(8,128)(2,1)S(1)} %get-tuple-element.29), channel_id=1, source_target_pairs={{0,4},{4,0},{1,5},{5,1},{2,6},{6,2},{3,7},{7,3}} | collective-permute-start | bytes 786440 | tf_op jit(solution)/shard_map/ppermute | solution.py:526

commit v13 on v12

--- a/solution.py
+++ b/solution.py
@@ -238,9 +238,9 @@
     u_parts((0, 0), (0, 1))
     u_parts((1, 0), (1, 1), (0, 2), (0, 3))
     s1(0)
+    send_x(1, 0)
     u_parts((2, 0), (2, 1), (1, 2), (1, 3))
     s1(1)
-    send_x(1, 0)
     u_parts((3, 0), (3, 1), (2, 2), (2, 3))
     s1(2)
     for j in range(NC):

time: 85.2 us -> 84.6 us (level)
  no operation moved by 1% of the time
where the time goes in v13:
time: 84.6 us; the launch traced here: 84.5 us
  Pallas kernels  81.4 us (96%)
  starting transfers between devices  1.58 us (2%)
    pallas_call x1, Pallas kernels, comm_call(): pl.pallas_call(comm_kernel, out_shape=outs, name='comm', in_specs=[HBM] *...  61.2 us
    pallas_call x1, Pallas kernels, grads_call(): pl.pallas_call(grads_kernel, out_shape=outs, name='grads', in_specs=[VMEM...  20.2 us
  transfers between devices with their start and end apart: 1, of which 0 were waited for; matrix products, arithmetic and copies ran while one was open for 0% of the time, Pallas kernels for 24%

profile of v13, /device:TPU:0, one launch (start us, length us, event | category | flops | bytes accessed | tf_op | source)
XLA Modules:
  0.0 84.5 jit_solution(17362191945379242152)
XLA Ops:
  0.6 0.0 copy-start.1
  0.6 0.0 copy-start
  0.7 0.0 copy-start.2
  0.7 0.0 copy-start.3
  0.7 61.2 %comm.1 = (bf16[4,10,128,128]{3,2,1,0:T(8,128)(2,1)S(1)}, bf16[4,10,128,256]{3,2,1,0:T(8,128)(2,1)S(1)}, bf16[128,1024]{1,0:T(8,128)(2,1)S(1)}, f32[128,1024]{1,...) custom-call(bf16[128,1024]{1,0:T(8,128)(2,1)} %x_ref.1, ...), custom_call_target="tpu_custom_call" | custom-call | flops 8000000000 | bytes 33554432 | tf_op jit(solution)/shard_map/comm/pallas_call | solution.py:435
  61.8 1.6 %collective-permute-start = (bf16[128,1024]{1,0:T(8,128)(2,1)S(1)}, bf16[128,1024]{1,0:T(8,128)(2,1)S(1)}, u32[]{:S(2)}, u32[]{:S(2)}) collective-permute-start(bf16[128,1024]{1,0:T(8,128)(2,1)S(1)} %get-tuple-element.29), channel_id=1, source_target_pairs={{0,4},{4,0},{1,5},{5,1},{2,6},{6,2},{3,7},{7,3}} | collective-permute-start | bytes 786440 | tf_op jit(solution)/shard_map/ppermute | solution.py:526
  63.4 0.0 copy-done.1
  63.4 0.0 copy-done
  63.4 0.0 copy-done.2
  63.4 0.0 copy-done.3
  63.4 20.2 %grads.1 = (f32[1024,10240]{1,0:T(8,128)}, f32[5120,1024]{1,0:T(8,128)}, bf16[128,1024]{1,0:T(8,128)(2,1)}, f32[1,10240]{1,0:T(1,128)}, f32[1,1024]{1,0:T(1,128)}, /*index=5*/f32[1,1024]{1,0:T(1,128)}, f32[1,1024]{1,0:T(1,128)}) custom-call(bf16[4,10,128,128]{3,2,1,0:T(8,128)(2,1)S(1)} %get-tuple-element.22.m_ref, ...), custom_call_target="tpu_custom_call" | custom-call | flops 4000000000 | bytes 69206016 | tf_op jit(solution)/shard_map/grads/pallas_call | solution.py:505
  83.7 0.0 collective-permute-done
  83.7 0.8 add_convert_fusion
Async XLA Ops:
  0.6 62.8 %copy-start.1 = (bf16[128,1024]{1,0:T(8,128)(2,1)S(1)}, bf16[128,1024]{1,0:T(8,128)(2,1)}, u32[]{:S(2)}) copy-start(bf16[128,1024]{1,0:T(8,128)(2,1)} %dy_ref.1) | copy-start | bytes 786436
  0.6 62.8 %copy-start = (bf16[128,1024]{1,0:T(8,128)(2,1)S(1)}, bf16[128,1024]{1,0:T(8,128)(2,1)}, u32[]{:S(2)}) copy-start(bf16[128,1024]{1,0:T(8,128)(2,1)} %x_ref.1) | copy-start | bytes 786436
  0.7 62.8 %copy-start.2 = (f32[1024]{0:T(1024)S(1)}, f32[1024]{0:T(1024)}, u32[]{:S(2)}) copy-start(f32[1024]{0:T(1024)} %param.13) | copy-start | bytes 12292
  0.7 62.8 %copy-start.3 = (f32[1024]{0:T(1024)S(1)}, f32[1024]{0:T(1024)}, u32[]{:S(2)}) copy-start(f32[1024]{0:T(1024)} %param.14) | copy-start | bytes 12292
  61.8 21.8 %collective-permute-start = (bf16[128,1024]{1,0:T(8,128)(2,1)S(1)}, bf16[128,1024]{1,0:T(8,128)(2,1)S(1)}, u32[]{:S(2)}, u32[]{:S(2)}) collective-permute-start(bf16[128,1024]{1,0:T(8,128)(2,1)S(1)} %get-tuple-element.29), channel_id=1, source_target_pairs={{0,4},{4,0},{1,5},{5,1},{2,6},{6,2},{3,7},{7,3}} | collective-permute-start | bytes 786440 | tf_op jit(solution)/shard_map/ppermute | solution.py:526
